TPU v7x, 128 devices: a 2x2x16 block of a 8x8x16 slice. The times are simulated.
128 devices in a mesh: groups: 4 (over x, y), seq: 32 (over z, core).
Axes of the slice: x: 2, y: 2, z: 16, core: 2. Of those that a mesh axis runs over, the one named last changes fastest.
The devices are a block of a 8x8x16 slice.
Arguments:
- candidates: bfloat16 [64, 512, 256], P('groups', 'seq'), parts along dimension 0, may hold values from -110 to 110
- codes: int32 [64, 4096, 256], P('groups', 'seq'), parts along dimension 0, may hold values from -2147483648 to 2147483647
- scale_index: int32 [64, 16384], P('groups', 'seq'), parts along dimension 0, may hold values from 0 to 255
- lengths: int32 [64], P('groups'), parts along dimension 0, may hold values from 128 to 16384, as said below
- scale_table: float32 [256], replicated, may hold values from 0.004 to 0.04
- query_weight: bfloat16 [256, 256], replicated, may hold values from -0.375 to 0.375
- key_weight: bfloat16 [256, 256], replicated, may hold values from -0.375 to 0.375
- value_weight: bfloat16 [256, 256], replicated, may hold values from -0.375 to 0.375
- out_weight: bfloat16 [256, 256], replicated, may hold values from -0.375 to 0.375
- norm_gain: float32 [256], replicated, may hold values from 0.1 to 1.9
- hidden_weight: bfloat16 [256, 512], replicated, may hold values from -0.375 to 0.375
- hidden_bias: float32 [512], replicated, may hold values from -4 to 4
- score_weight: bfloat16 [512], replicated, may hold values from -0.25 to 0.25
Outputs:
- interest: bfloat16 [64, 512, 256], P('groups', 'seq'), parts along dimension 0
- logits: float32 [64, 512], P('groups', 'seq'), parts along dimension 0
There are 4 independent parts, one for each index of `groups`. A program takes and returns all parts, laid end to end along the dimension named above; an argument that names none is the same for every part. Nothing has to cross between parts.
Inputs may be any that keep to these rules, and one draw needn't show every extreme that they name: `lengths`: each user's history length is a multiple of 128; in every draw some user's length is 16384.
All inputs are finite; a program needn't handle non-finite values.
Results may differ from a plain program's by a relative error of at most 0.02.
The roundings to bfloat16 on the way count: a program that leaves them out, or rounds other values in their place, can miss the bound.
Values may be sent and summed in bfloat16 or wider, within the bound.
No kernel may reach another device: no remote copies, remote signals or barrier semaphores. Data moves between devices by JAX's collectives and lax.ppermute only.
A program may use at most 128 MiB of HBM per device.

v0:
```python
import math

import jax
import jax.numpy as jnp
from jax import lax
from jax.sharding import Mesh
from jax.sharding import PartitionSpec as P

HEADS = 4
SEQ = ("seq_0", "seq_1")


NEG_FILL = -1e30


def total_of_pieces(array, axis):
    blocks = lax.all_gather(array, axis)
    return blocks.max(axis=0)


def sum_in_order(blocks, axes, order):
    dims = [lax.axis_size(a) for a in axes]
    blocks = blocks.reshape(*dims, *blocks.shape[1:])
    blocks = blocks.transpose(*order, *range(len(axes), blocks.ndim))
    blocks = blocks.reshape(-1, *blocks.shape[len(axes) :])
    for k in order:
        blocks = lax.psum_scatter(blocks, axes[k], scatter_dimension=0, tiled=True)
    return blocks[0]


def in_blocks(array, dim, peers):
    before, after = (array.shape[:dim], array.shape[dim + 1 :])
    return jnp.moveaxis(array.reshape(*before, peers, -1, *after), dim, 0)


def summed_rows(array, axes, order, dim):
    peers = lax.axis_size(axes)
    return sum_in_order(in_blocks(array, dim, peers), axes, order)


def unpack_codes(words):
    byte_rows = [jnp.right_shift(jnp.left_shift(words, 24 - 8 * k), 24) for k in range(4)]
    stacked = jnp.stack(byte_rows, axis=1)
    return stacked.reshape(words.shape[0] * 4, words.shape[1])


def score_block(query_rows, key_rows, live_row):
    cand_rows, model_width = query_rows.shape
    head_size = model_width // HEADS
    split_query = query_rows.reshape(cand_rows, HEADS, head_size)
    split_keys = key_rows.reshape(key_rows.shape[0], HEADS, head_size)
    scores = jnp.einsum("chd,khd->hck", split_query, split_keys, preferred_element_type=jnp.float32)
    scores = scores * (1.0 / math.sqrt(head_size))
    return jnp.where(live_row[None, None, :], scores, NEG_FILL)


def exp_weights(scores, live_row, peak_rows):
    return jnp.where(live_row[None, None, :], jnp.exp(scores - peak_rows[:, :, None]), 0.0)


def weighted_rows(weights, value_rows):
    head_count, cand_rows, key_count = weights.shape
    split_values = value_rows.reshape(key_count, head_count, -1)
    blended = jnp.einsum(
        "hck,khd->chd",
        weights.astype(jnp.bfloat16),
        split_values,
        preferred_element_type=jnp.float32,
    )
    return blended.reshape(cand_rows, -1)


def on_device(
    candidates,
    codes,
    scale_index,
    lengths,
    scale_table,
    query_weight,
    key_weight,
    value_weight,
    out_weight,
    norm_gain,
    hidden_weight,
    hidden_bias,
    score_weight,
):
    user_count, cand_local, model_width = candidates.shape
    hist_local = scale_index.shape[1]
    head_size = model_width // HEADS
    own_queries = jnp.einsum(
        "ucd,de->uce", candidates, query_weight, preferred_element_type=jnp.float32
    ).astype(jnp.bfloat16)
    queries = lax.all_gather(own_queries, SEQ, axis=1, tiled=True)
    offset = lax.axis_index(SEQ) * hist_local
    places = offset + jnp.arange(hist_local, dtype=jnp.int32)
    live_mask = places[None, :] < lengths[:, None]
    levels = jnp.arange(scale_table.shape[0], dtype=jnp.int32)

    def project(user_item):
        word_rows, index_rows = user_item
        code_rows = unpack_codes(word_rows)
        row_scales = jnp.sum(
            jnp.where(index_rows[:, None] == levels[None, :], scale_table[None, :], 0.0), axis=1
        )
        history = (code_rows.astype(jnp.float32) * row_scales[:, None]).astype(jnp.bfloat16)
        key_rows = jnp.dot(history, key_weight, preferred_element_type=jnp.float32).astype(
            jnp.bfloat16
        )
        value_rows = jnp.dot(history, value_weight, preferred_element_type=jnp.float32).astype(
            jnp.bfloat16
        )
        return (key_rows, value_rows)

    all_keys, all_values = lax.map(project, (codes, scale_index))

    def first_pass(user_item):
        query_rows, key_rows, live_row = user_item
        return jnp.max(score_block(query_rows, key_rows, live_row), axis=2)

    peak_rows = lax.map(first_pass, (queries, all_keys, live_mask))
    peak_rows = total_of_pieces(peak_rows.astype(jnp.bfloat16), SEQ).astype(peak_rows.dtype)

    def second_pass(user_item):
        query_rows, key_rows, value_rows, live_row, user_peaks = user_item
        scores = score_block(query_rows, key_rows, live_row)
        weights = exp_weights(scores, live_row, user_peaks)
        return (weighted_rows(weights, value_rows), jnp.sum(weights, axis=2))

    numerators, totals = lax.map(second_pass, (queries, all_keys, all_values, live_mask, peak_rows))
    numerators, totals = (
        summed_rows(numerators.astype(jnp.bfloat16), SEQ, (1, 0), 1).astype(jnp.float32),
        summed_rows(totals.astype(jnp.bfloat16), SEQ, (1, 0), 2).astype(jnp.float32),
    )
    split_numer = numerators.reshape(user_count, cand_local, HEADS, head_size)
    attended = (
        (split_numer / jnp.transpose(totals, (0, 2, 1))[..., None])
        .reshape(user_count, cand_local, model_width)
        .astype(jnp.bfloat16)
    )
    interest = jnp.einsum(
        "ucd,de->uce", attended, out_weight, preferred_element_type=jnp.float32
    ).astype(jnp.bfloat16)
    floats = interest.astype(jnp.float32)
    normed = (
        floats * lax.rsqrt(jnp.mean(floats * floats, axis=2, keepdims=True) + 1e-06) * norm_gain
    ).astype(jnp.bfloat16)
    hidden = jax.nn.silu(
        jnp.einsum("ucd,dh->uch", normed, hidden_weight, preferred_element_type=jnp.float32)
        + hidden_bias
    ).astype(jnp.bfloat16)
    logits = jnp.einsum("uch,h->uc", hidden, score_weight, preferred_element_type=jnp.float32)
    return (interest, logits)


def solution(mesh):
    torus = Mesh(mesh.devices.reshape(mesh.shape["groups"], 16, 2), ("groups", "seq_0", "seq_1"))
    in_specs = (
        P("groups", SEQ, None),
        P("groups", SEQ, None),
        P("groups", SEQ),
        P("groups"),
        P(),
        P(),
        P(),
        P(),
        P(),
        P(),
        P(),
        P(),
        P(),
    )
    out_specs = (P("groups", SEQ, None), P("groups", SEQ))
    return jax.shard_map(
        on_device, mesh=torus, in_specs=in_specs, out_specs=out_specs, check_vma=False
    )
```

profile of v0, /device:TPU:70, one launch (start us, length us, event | category | flops | bytes accessed | tf_op | source)
XLA Modules:
  0.0 576.7 jit_solution(5178833307086976015)
XLA Ops:
  9.2 107.8 %while.37 = (s32[]{:T(128)}, bf16[16,512,256]{1,2,0:T(8,128)(2,1)}, bf16[16,512,256]{2,1,0:T(8,128)(2,1)}, s32[16,128,256]{2,1,0:T(8,128)}, s32[16,512]{1,0:T(8,...) while((s32[]{:T(128)}, bf16[16,512,256]{1,2,0:T(8,128)(2,1)}, ...), condition=%wide.region_2.3_spmd.clone, body=%wide.region_0.2_spmd.clone.sunk | while | flops 136183296 | bytes 6436993 | solution.py:115
  117.2 6.4 %copy.65 = bf16[16,512,256]{1,2,0:T(8,128)(2,1)} copy(bf16[16,512,256]{2,1,0:T(8,128)(2,1)} %all-gather.4.cloned.1.call-done) | data formatting | bytes 8388608 | tf_op jit(solution)/shard_map/while | solution.py:130
  123.6 33.0 %while.35 = (s32[]{:T(128)}, bf16[16,4,512]{2,1,0:T(4,128)(2,1)S(1)}, pred[16,512]{1,0:T(8,128)(4,1)S(1)}, bf16[16,512,256]{1,2,0:T(8,128)(2,1)}, bf16[16,512,256]{1,2,0:T(8,128)(2,1)}, /*index=5*/s32[]{:T(128)}) while((s32[]{:T(128)}, bf16[16,4,512]{2,1,0:T(4,128)(2,1)S(1)}, pred[16,512]{1,0:T(8,128)(4,1)S(1)}, ...), condition=%wide.region_5.6_spmd, body=%wide.region_3.5_spmd.sunk | while | flops 137361408 | bytes 1586769 | solution.py:121
  157.4 74.4 %all-gather.6.cloned.1.call-done = bf16[512,4,512]{2,1,0:T(4,128)(2,1)} async-done(((bf16[16,4,512]{2,1,0:T(4,128)(2,1)}), bf16[512,4,512]{2,1,0:T(4,128)(2,1)}) %all-gather.6.cloned.1.call-update) | async-done | bytes 2097168 | tf_op jit(solution)/shard_map/all_gather | solution.py:17
  234.3 156.3 %while.36 = (s32[]{:T(128)}, bf16[16,512,256]{2,1,0:T(8,128)(2,1)}, bf16[16,4,512]{2,1,0:T(4,128)(2,1)S(1)}, bf16[16,512,256]{2,1,0:T(8,128)(2,1)}, pred[16,512]...) while((s32[]{:T(128)}, bf16[16,512,256]{2,1,0:T(8,128)(2,1)}, ...), condition=%wide.region_9.10_spmd, body=%wide.region_7.9_spmd.sunk | while | flops 278919168 | bytes 12630641 | solution.py:130
  235.4 3.4 fusion.60
  245.2 3.4 fusion.60
  254.9 3.4 fusion.60
  259.4 3.3 fusion.61
  264.7 3.4 fusion.60
  269.2 3.3 fusion.61
  274.4 3.4 fusion.60
  278.9 3.3 fusion.61
  284.2 3.4 fusion.60
  294.0 3.4 fusion.60
  303.8 3.4 fusion.60
  313.5 3.4 fusion.60
  323.3 3.4 fusion.60
  327.8 3.3 fusion.61
  333.1 3.4 fusion.60
  342.9 3.4 fusion.60
  352.6 3.4 fusion.60
  362.4 3.4 fusion.60
  366.9 3.3 fusion.61
  372.2 3.4 fusion.60
  376.7 3.3 fusion.61
  382.0 3.4 fusion.60
  393.0 4.7 copy.68
  397.8 7.2 %reduce-scatter.13.cloned.1.call-done = bf16[16,1024]{1,0:T(8,128)(2,1)} async-done(((bf16[32,1024]{1,0:T(8,128)(2,1)}), bf16[16,1024]{1,0:T(8,128)(2,1)}) %reduce-scatter.13.cloned.1.call-update) | async-done | bytes 32784
  407.2 20.6 %reduce-scatter.7.cloned.1.call-done = bf16[16,16,16,256]{3,2,1,0:T(8,128)(2,1)} async-done(((bf16[32,16,16,256]{3,2,1,0:T(8,128)(2,1)}), bf16[16,16,16,256]{3,2,1,0:T(8,128)(2,1)}) %reduce-scatter.7.cloned.1.call-update) | async-done | bytes 2097168 | tf_op jit(solution)/shard_map/reduce_scatter | solution.py:27
  427.8 69.2 %reduce-scatter.11.cloned.1.call-done = bf16[1,16,4,16]{3,1,2,0:T(8,128)(2,1)} async-done(((bf16[16,16,4,16]{3,1,2,0:T(8,128)(2,1)}), bf16[1,16,4,16]{3,1,2,0:T(8,128)(2,1)}) %reduce-scatter.11.cloned.1.call-update) | async-done | bytes 2064 | tf_op jit(solution)/shard_map/reduce_scatter | solution.py:27
  498.6 68.7 %reduce-scatter.9.cloned.1.call-done = bf16[1,16,16,256]{3,2,1,0:T(8,128)(2,1)} async-done(((bf16[16,16,16,256]{3,2,1,0:T(8,128)(2,1)}), bf16[1,16,16,256]{3,2,1,0:T(8,128)(2,1)}) %reduce-scatter.9.cloned.1.call-update) | async-done | bytes 131088 | tf_op jit(solution)/shard_map/reduce_scatter | solution.py:27
  (447 shorter events, 235.9 us)
Async XLA Ops:
  7.2 561.4 %copy-start = (bf16[256,512]{1,0:T(8,128)(2,1)S(1)}, bf16[256,512]{1,0:T(8,128)(2,1)}, u32[]{:S(2)}) copy-start(bf16[256,512]{1,0:T(8,128)(2,1)} %param.29) | copy-start | bytes 786436
  7.2 110.0 %all-gather.4.cloned.1.call-start = ((), (), s32[]{:S(2)}) async-start(), calls=%async_computation.4 | async-start | bytes 4325376 | tf_op jit(solution)/shard_map/all_gather | solution.py:94
  9.1 222.6 %all-gather.6.cloned.1.call-start = ((), (), s32[]{:S(2)}) async-start(), calls=%async_computation.8 | async-start | bytes 2162688 | tf_op jit(solution)/shard_map/all_gather | solution.py:17
  9.2 107.9 %copy-start.4 = (s32[16]{0:T(128)S(1)}, s32[16]{0:T(128)}, u32[]{:S(2)}) copy-start(s32[16]{0:T(128)} %param.22) | copy-start | bytes 196
  9.2 5.8 %copy-start.1 = (bf16[256,256]{1,0:T(8,128)(2,1)S(1)}, bf16[256,256]{1,0:T(8,128)(2,1)}, u32[]{:S(2)}) copy-start(bf16[256,256]{1,0:T(8,128)(2,1)} %get-tuple-element.468) | copy-start | bytes 393220 | tf_op jit(solution)/shard_map/while
  16.0 5.8 copy-start.1
  22.8 5.8 copy-start.1
  29.5 5.8 %copy-start.1 = (bf16[256,256]{1,0:T(8,128)(2,1)S(1)}, bf16[256,256]{1,0:T(8,128)(2,1)}, u32[]{:S(2)}) copy-start(bf16[256,256]{1,0:T(8,128)(2,1)} %get-tuple-element.468) | copy-start | bytes 393220 | tf_op jit(solution)/shard_map/while
  36.3 5.7 copy-start.1
  43.0 5.7 copy-start.1
  49.7 5.8 copy-start.1
  56.4 5.7 copy-start.1
  63.2 5.8 %copy-start.1 = (bf16[256,256]{1,0:T(8,128)(2,1)S(1)}, bf16[256,256]{1,0:T(8,128)(2,1)}, u32[]{:S(2)}) copy-start(bf16[256,256]{1,0:T(8,128)(2,1)} %get-tuple-element.468) | copy-start | bytes 393220 | tf_op jit(solution)/shard_map/while
  69.9 5.8 copy-start.1
  76.7 5.8 copy-start.1
  83.4 5.7 copy-start.1
  90.2 5.7 copy-start.1
  96.9 5.8 copy-start.1
  103.6 5.7 copy-start.1
  110.3 5.7 copy-start.1
  156.6 0.6 copy-start.2
  157.3 247.6 %reduce-scatter.13.cloned.1.call-start = ((), (), s32[]{:S(2)}) async-start(), calls=%async_computation.9 | async-start | bytes 98304
  392.9 34.9 %reduce-scatter.7.cloned.1.call-start = ((), (), s32[]{:S(2)}) async-start(), calls=%async_computation.5 | async-start | bytes 6291456 | tf_op jit(solution)/shard_map/reduce_scatter | solution.py:27
  397.6 30.2 %copy-start.3 = (bf16[512]{0:T(512)(128)(2,1)S(1)}, bf16[512]{0:T(512)(128)(2,1)}, u32[]{:S(2)}) copy-start(bf16[512]{0:T(512)(128)(2,1)} %param.31) | copy-start | bytes 3076
  397.6 169.7 %copy-start.5 = (bf16[256,256]{1,0:T(8,128)(2,1)S(1)}, bf16[256,256]{1,0:T(8,128)(2,1)}, u32[]{:S(2)}) copy-start(bf16[256,256]{1,0:T(8,128)(2,1)} %param.27) | copy-start | bytes 393220
  397.6 170.9 %copy-start.6 = (f32[512]{0:T(512)S(1)}, f32[512]{0:T(512)}, u32[]{:S(2)}) copy-start(f32[512]{0:T(512)} %param.30) | copy-start | bytes 6148
  397.6 170.9 %copy-start.7 = (f32[256]{0:T(256)S(1)}, f32[256]{0:T(256)}, u32[]{:S(2)}) copy-start(f32[256]{0:T(256)} %param.28) | copy-start | bytes 3076
  397.7 99.3 %reduce-scatter.11.cloned.1.call-start = ((), (), s32[]{:S(2)}) async-start(), calls=%async_computation.7 | async-start | bytes 278528 | tf_op jit(solution)/shard_map/reduce_scatter | solution.py:27
  407.1 160.2 %reduce-scatter.9.cloned.1.call-start = ((), (), s32[]{:S(2)}) async-start(), calls=%async_computation.6 | async-start | bytes 2228224 | tf_op jit(solution)/shard_map/reduce_scatter | solution.py:27
  568.5 1.3 copy-start.8
Sparse Core Ops, SparseCore 0:
  10.3 76.3 all-gather.3
  157.4 74.2 all-gather.5
  393.0 11.8 reduce-scatter.12
  407.2 20.4 reduce-scatter.6
  430.0 67.0 reduce-scatter.10
  499.3 67.9 reduce-scatter.8
where the time goes:
time: 581 us; the launch traced here: 577 us
  waiting for transfers between devices  240 us (41%)
  matrix products  160 us (28%)
  local copies, waits for them, and re-layouts  128 us (22%)
  other arithmetic  32 us (6%)
  between operations  14.3 us (2%)
    reduce_scatter x3, waiting for transfers between devices, sum_in_order(): blocks = lax.psum_scatter(blocks, axes[k], scatter_dimension=0, tiled=True)  158 us
    all_gather x1, waiting for transfers between devices, total_of_pieces(): blocks = lax.all_gather(array, axis)  74.4 us
    dot_general x32, matrix products, score_block(): jnp.einsum('chd,khd->hck', split_query, split_keys, preferred_element_typ...  68.7 us
    dynamic_slice x96, local copies, waits for them, and re-layouts, on_device(): peak_rows = lax.map(first_pass, (queries, all_keys, live_mask))  52.8 us
    dot_general x16, matrix products, weighted_rows(): jnp.einsum('hck,khd->chd', weights.astype(jnp.bfloat16), split_values, pr...  52.5 us
    dynamic_slice x32, local copies, waits for them, and re-layouts, on_device(): all_keys, all_values = lax.map(project, (codes, scale_index))  26.9 us
    dot_general x16, matrix products, project(): jnp.dot(history, key_weight, preferred_element_type=jnp.float32)  18.9 us
    dot_general x16, matrix products, project(): jnp.dot(history, value_weight, preferred_element_type=jnp.float32)  15.8 us
  transfers between devices with their start and end apart: 6, of which 5 were waited for; matrix products, arithmetic and copies ran while one was open for 20% of the time, Pallas kernels for 0%

commit v1 on v0

v1 whole, which is shorter than its diff:
```python
import functools

import jax
import jax.numpy as jnp
from jax import lax
from jax.experimental import pallas as pl
from jax.experimental.pallas import tpu as pltpu
from jax.sharding import PartitionSpec as P

HEADS = 4
GRAIN = 128
BYTES = 4
NEG = -1e30
SPAN = 4
GROUP = 4
STATS = 16
ONES = 16
BATCH = 4

NT = (((1,), (1,)), ((), ()))
TN = (((0,), (0,)), ((), ()))


def dot(a, b, dims=(((1,), (0,)), ((), ()))):
    return lax.dot_general(a, b, dims, preferred_element_type=jnp.float32)


def cost(flops, moved):
    return pl.CostEstimate(flops=int(flops), bytes_accessed=int(moved), transcendentals=0)


def history_body(words, index, table, out):
    levels = table.shape[1]
    words_per = GRAIN // BYTES
    spot = lax.broadcasted_iota(jnp.int32, (GRAIN, GRAIN), 0)
    place = lax.broadcasted_iota(jnp.int32, (GRAIN, GRAIN), 1)
    moves = (spot == BYTES * (place % words_per) + place // words_per).astype(jnp.bfloat16)
    level = lax.broadcasted_iota(jnp.int32, (levels, GRAIN), 0).astype(jnp.float32)
    entry = jnp.broadcast_to(table[...], (GRAIN, levels)).T
    users = words.shape[0]
    first = pl.program_id(0) * users
    for u in range(users):
        indices = index[pl.ds(first + u, 1), :].astype(jnp.float32)
        for g in range(words.shape[1] // words_per):
            row = indices[:, g * GRAIN : (g + 1) * GRAIN]
            row = jnp.broadcast_to(row, (16, GRAIN)).astype(jnp.bfloat16)
            row = dot(row, moves)[0:1]
            scales = jnp.sum(jnp.where(level == row, entry, 0.0), axis=0, keepdims=True)
            scales = jnp.broadcast_to(scales, (GRAIN, GRAIN)).T
            block = words[u, g * words_per : (g + 1) * words_per, :]
            for k in range(BYTES):
                codes = jnp.right_shift(jnp.left_shift(block, 24 - 8 * k), 24).astype(jnp.float32)
                part = scales[k * words_per : (k + 1) * words_per]
                part = jnp.concatenate([part] * (block.shape[1] // GRAIN), axis=1)
                start = g * GRAIN + k * words_per
                out[u, start : start + words_per, :] = (codes * part).astype(jnp.bfloat16)


def history_rows(codes, scale_index, scale_table):
    users, words, width = codes.shape
    places = words * BYTES
    levels = scale_table.shape[0]
    return pl.pallas_call(
        history_body,
        grid=(users // BATCH,),
        in_specs=[
            pl.BlockSpec((BATCH, words, width), lambda u: (u, 0, 0)),
            pl.BlockSpec((users, places), lambda u: (0, 0)),
            pl.BlockSpec((1, levels), lambda u: (0, 0)),
        ],
        out_specs=pl.BlockSpec((BATCH, places, width), lambda u: (u, 0, 0)),
        out_shape=jax.ShapeDtypeStruct((users, places, width), jnp.bfloat16),
        cost_estimate=cost(2e9, 6e6),
        name="history",
    )(codes, scale_index, scale_table.reshape(1, levels))


def project_body(rows, key_w, value_wt, keys, values):
    width = key_w.shape[0]
    half = width // 2
    for u in range(rows.shape[0]):
        h = rows[u]
        keys[u] = dot(h, key_w[...]).astype(jnp.bfloat16)
        v = dot(value_wt[...], h, NT).astype(jnp.bfloat16)
        ones = jnp.ones((ONES, h.shape[0]), jnp.bfloat16)
        for p in range(2):
            at = p * (half + ONES)
            values[u, at : at + half, :] = v[p * half : (p + 1) * half]
            values[u, at + half : at + half + ONES, :] = ones


def project(rows, key_w, value_wt):
    users, places, width = rows.shape
    tall = width + 2 * ONES
    return pl.pallas_call(
        project_body,
        grid=(users // BATCH,),
        in_specs=[
            pl.BlockSpec((BATCH, places, width), lambda u: (u, 0, 0)),
            pl.BlockSpec((width, width), lambda u: (0, 0)),
            pl.BlockSpec((width, width), lambda u: (0, 0)),
        ],
        out_specs=[
            pl.BlockSpec((BATCH, places, width), lambda u: (u, 0, 0)),
            pl.BlockSpec((BATCH, tall, places), lambda u: (u, 0, 0)),
        ],
        out_shape=[
            jax.ShapeDtypeStruct((users, places, width), jnp.bfloat16),
            jax.ShapeDtypeStruct((users, tall, places), jnp.bfloat16),
        ],
        cost_estimate=cost(3e9, 12e6),
        name="project",
    )(rows, key_w, value_wt)


def query_body(rows, weight, out):
    head = weight.shape[1] // HEADS
    q = dot(rows[...], weight[...]).astype(jnp.bfloat16)
    out[...] = q * jnp.bfloat16(head**-0.5)


def query_rows(rows, weight):
    return pl.pallas_call(
        query_body,
        out_shape=jax.ShapeDtypeStruct((rows.shape[0], weight.shape[1]), jnp.bfloat16),
        cost_estimate=cost(3e7, 4e5),
        name="query",
    )(rows, weight)


def parts_of(peak):
    hi = peak.astype(jnp.bfloat16).astype(jnp.float32)
    mid = (peak - hi).astype(jnp.bfloat16).astype(jnp.float32)
    return [hi, mid, peak - hi - mid]


def attend_user(user, k, pieces, live, k_own, k_other, v_own, v_other, scores, weights, held, at):
    width = k_own.shape[2]
    head = width // HEADS
    pair = 2 * head
    counts = (live[0, user], live[1, user])
    per = k_own.shape[1] // GRAIN
    lanes = held.shape[1] // GROUP

    @pl.when(counts[0] + counts[1] == 0)
    def _():
        held[0:width, at] = jnp.zeros((width, lanes), jnp.bfloat16)
        row = lax.broadcasted_iota(jnp.int32, (STATS, lanes), 0)
        held[width : width + STATS, at] = jnp.where(row < HEADS, NEG, 0.0).astype(jnp.bfloat16)

    @pl.when(counts[0] + counts[1] > 0)
    def _():
        q = jnp.concatenate([r[user] for r in pieces], axis=0)
        lane = lax.broadcasted_iota(jnp.int32, (lanes, pair), 1)
        peaks, totals = [], []
        for p in range(HEADS // 2):
            both = q[:, p * pair : (p + 1) * pair].astype(jnp.float32)
            right = jnp.concatenate(
                [jnp.where(lane < head, both, 0.0), jnp.where(lane < head, 0.0, both)], axis=0
            ).astype(jnp.bfloat16)
            tops = []
            for t in range(2 * per):
                source, place = ((k_own, t), (k_other, t - per))[t >= per]
                s = dot(source[k, place * GRAIN : (place + 1) * GRAIN, p * pair : (p + 1) * pair], right, NT)
                scores[p, t * GRAIN : (t + 1) * GRAIN, :] = s
                alive = place < counts[t >= per]
                tops.append(jnp.where(alive, jnp.max(s, axis=0, keepdims=True), NEG))
            peaks.append(functools.reduce(jnp.maximum, tops))
        for p in range(HEADS // 2):
            for t in range(2 * per):
                alive = t % per < counts[t >= per]
                lift = jnp.where(alive, peaks[p], -NEG)
                w = jnp.exp(scores[p, t * GRAIN : (t + 1) * GRAIN, :] - lift)
                weights[p, t * GRAIN : (t + 1) * GRAIN, :] = w.astype(jnp.bfloat16)
            rows = slice(p * (pair + ONES), (p + 1) * (pair + ONES))
            half = per * GRAIN
            o = dot(v_own[k, rows, :], weights[p, 0:half, :]) + dot(v_other[k, rows, :], weights[p, half : 2 * half, :])
            held[p * pair : p * pair + head, at] = o[0:head, 0:lanes].astype(jnp.bfloat16)
            held[p * pair + head : (p + 1) * pair, at] = o[head:pair, lanes:].astype(jnp.bfloat16)
            totals += [o[pair : pair + 1, 0:lanes], o[pair : pair + 1, lanes:]]
        peak = jnp.concatenate([x for p in peaks for x in (p[:, 0:lanes], p[:, lanes:])], axis=0)
        stats = jnp.concatenate(parts_of(peak) + totals, axis=0)
        held[width : width + STATS, at] = stats.astype(jnp.bfloat16)


def attend_body(base, live, *refs):
    pieces, refs = refs[: 2 * SPAN], refs[2 * SPAN :]
    (k_own, k_other, v_own, v_other, order), refs = refs[:5], refs[5:]
    outs, (scores, weights, held) = refs[:SPAN], refs[SPAN:]
    lanes = held.shape[1] // GROUP
    batch = k_own.shape[0]
    i = pl.program_id(1)
    for k in range(batch):
        place = i * batch + k
        user = base + pl.program_id(0) * GROUP + place
        at = pl.ds(pl.multiple_of(place * lanes, lanes), lanes)
        attend_user(user, k, pieces, live, k_own, k_other, v_own, v_other, scores, weights, held, at)

    @pl.when(i == GROUP // batch - 1)
    def _():
        mixed = dot(held[...], order[...]).astype(jnp.bfloat16)
        for s in range(SPAN):
            outs[s][...] = mixed[:, s * lanes : (s + 1) * lanes]


def attend(base, users, live, pieces, k_own, k_other, v_own, v_other, order):
    cand, width = pieces[0].shape[1:]
    places = k_own.shape[1]
    tall = v_own.shape[1]
    lanes = cand * len(pieces)
    deep = width + STATS
    batch = 2
    steps = GROUP // batch
    some = lambda g, i, live: (base // batch + g * steps + i, 0, 0)
    flat = lambda g, i, live: (0, 0)
    return pl.pallas_call(
        functools.partial(attend_body, base),
        grid_spec=pltpu.PrefetchScalarGridSpec(
            num_scalar_prefetch=1,
            grid=(users // GROUP, steps),
            in_specs=[pl.BlockSpec(memory_space=pltpu.VMEM) for _ in pieces]
            + [
                pl.BlockSpec((batch, places, width), some),
                pl.BlockSpec((batch, places, width), some),
                pl.BlockSpec((batch, tall, places), some),
                pl.BlockSpec((batch, tall, places), some),
                pl.BlockSpec(memory_space=pltpu.VMEM),
            ],
            out_specs=[pl.BlockSpec((deep, lanes), lambda g, i, live: (0, g))] * SPAN,
            scratch_shapes=[
                pltpu.VMEM((HEADS // 2, 2 * places, 2 * lanes), jnp.float32),
                pltpu.VMEM((HEADS // 2, 2 * places, 2 * lanes), jnp.bfloat16),
                pltpu.VMEM((deep, GROUP * lanes), jnp.bfloat16),
            ],
        ),
        out_shape=[jax.ShapeDtypeStruct((deep, users * lanes // SPAN), jnp.bfloat16)] * SPAN,
        cost_estimate=cost(6e9, 9e6),
        name="attend",
    )(live, *pieces, k_own, k_other, v_own, v_other, order)


def merged(a, b):
    width = a.shape[0] - STATS
    head = width // HEADS
    sa, sb = a[width:].astype(jnp.float32), b[width:].astype(jnp.float32)
    pa = sa[0:4] + sa[4:8] + sa[8:12]
    pb = sb[0:4] + sb[4:8] + sb[8:12]
    peak = jnp.maximum(pa, pb)
    fa, fb = jnp.exp(pa - peak), jnp.exp(pb - peak)
    total = fa * sa[12:16] + fb * sb[12:16]
    rows = []
    for h in range(HEADS):
        na = a[h * head : (h + 1) * head].astype(jnp.float32)
        nb = b[h * head : (h + 1) * head].astype(jnp.float32)
        rows.append(na * fa[h : h + 1] + nb * fb[h : h + 1])
    return rows, peak, total


def packed(rows, peak, total):
    stats = jnp.concatenate(parts_of(peak) + [total], axis=0)
    return jnp.concatenate([r.astype(jnp.bfloat16) for r in rows] + [stats.astype(jnp.bfloat16)], axis=0)


def merge_body(came, mine, out):
    out[...] = packed(*merged(came[...], mine[...]))


def merge(came, mine):
    return pl.pallas_call(
        merge_body,
        out_shape=jax.ShapeDtypeStruct(came.shape, jnp.bfloat16),
        cost_estimate=cost(1e8, 5e5),
        name="merge",
    )(came, mine)


def split_body(came_a, came_b, mine_a, mine_b, order, near, far):
    lanes = came_a.shape[1] // 2
    for n, (came, mine) in enumerate(((came_a, mine_a), (came_b, mine_b))):
        both = dot(packed(*merged(came[...], mine[...])), order[...]).astype(jnp.bfloat16)
        near[:, n * lanes : (n + 1) * lanes] = both[:, 0:lanes]
        far[:, n * lanes : (n + 1) * lanes] = both[:, lanes:]


def split(came_a, came_b, mine_a, mine_b, order):
    return pl.pallas_call(
        split_body,
        out_shape=[jax.ShapeDtypeStruct(came_a.shape, jnp.bfloat16)] * 2,
        cost_estimate=cost(1e8, 1e6),
        name="split",
    )(came_a, came_b, mine_a, mine_b, order)


def finish_body(a, b, out_w, gain, hidden_w, bias, score_w, interest, logits):
    rows, _, total = merged(a[...], b[...])
    attended = jnp.concatenate(
        [(r / total[h : h + 1]).astype(jnp.bfloat16) for h, r in enumerate(rows)], axis=0
    )
    found = dot(attended, out_w[...], TN).astype(jnp.bfloat16)
    interest[...] = found
    f = found.astype(jnp.float32)
    normed = f * lax.rsqrt(jnp.mean(f * f, axis=1, keepdims=True) + 1e-6) * gain[...]
    v = dot(normed.astype(jnp.bfloat16), hidden_w[...]) + bias[...]
    hidden = (v / (1.0 + jnp.exp(-v))).astype(jnp.bfloat16)
    row = dot(jnp.broadcast_to(score_w[...], (16, v.shape[1])), hidden, NT)[0:1]
    users, cand = logits.shape
    lane = lax.broadcasted_iota(jnp.int32, (users, users * cand), 1)
    mine = lane // cand == lax.broadcasted_iota(jnp.int32, (users, users * cand), 0)
    fold = lax.broadcasted_iota(jnp.int32, (users * cand, cand), 0) % cand
    fold = (fold == lax.broadcasted_iota(jnp.int32, (users * cand, cand), 1)).astype(jnp.bfloat16)
    folded = [dot(jnp.where(mine, r, 0.0).astype(jnp.bfloat16), fold) for r in parts_of(row)]
    logits[...] = folded[0] + folded[1] + folded[2]


def finish(users, a, b, out_w, gain, hidden_w, bias, score_w):
    width, wide = hidden_w.shape
    lanes = a.shape[1]
    return pl.pallas_call(
        finish_body,
        out_shape=[
            jax.ShapeDtypeStruct((lanes, width), jnp.bfloat16),
            jax.ShapeDtypeStruct((users, lanes // users), jnp.float32),
        ],
        cost_estimate=cost(2e8, 1e6),
        name="finish",
    )(a, b, out_w, gain.reshape(1, width), hidden_w, bias.reshape(1, wide), score_w.reshape(1, wide))


def reorder(shape, axes):
    size = 1
    for n in shape:
        size *= n
    spot = lax.broadcasted_iota(jnp.int32, (size, size), 1)
    dims = [shape[a] for a in axes]
    digits = []
    for n in reversed(dims):
        digits.insert(0, spot % n)
        spot = spot // n
    source = 0
    for a, n in enumerate(shape):
        source = source * n + digits[axes.index(a)]
    return (lax.broadcasted_iota(jnp.int32, (size, size), 0) == source).astype(jnp.bfloat16)


def solution(mesh):
    peers = mesh.shape["seq"]
    chips = peers // 2
    slots = chips // 2
    near = lambda d, c: (d % chips) * 2 + c
    ring = [(near(d, 0), near(d + 1, 0)) for d in range(chips)] + [(near(d, 1), near(d - 1, 1)) for d in range(chips)]
    stay = [(near(d, 0), near(d, 0)) for d in range(chips)] + [(near(d, 1), near(d - 1, 1)) for d in range(chips)]
    cross = [(near(d, 1), near(d, 0)) for d in range(chips)] + [(near(d, 0), near(d - 1, 1)) for d in range(chips)]
    swap = [(near(d, c), near(d, 1 - c)) for d in range(chips) for c in range(2)]
    back = lambda pairs: [(b, a) for a, b in pairs]

    def on_device(
        candidates,
        codes,
        scale_index,
        lengths,
        scale_table,
        query_weight,
        key_weight,
        value_weight,
        out_weight,
        norm_gain,
        hidden_weight,
        hidden_bias,
        score_weight,
    ):
        users, cand, width = candidates.shape
        places = scale_index.shape[1]
        send = lambda array, pairs: lax.ppermute(array, "seq", pairs)
        me = lax.axis_index("seq")
        mate = me + 1 - 2 * (me % 2)
        starts = jnp.stack([me, mate])[:, None] * places
        live = jnp.clip((lengths[None, :] - starts) // GRAIN, 0, places // GRAIN).astype(jnp.int32)

        mine = query_rows(candidates.reshape(users * cand, width), query_weight).reshape(users, cand, width)
        chunks = [(send(mine, stay), send(mine, cross))]
        for _ in range(slots - 1):
            chunks.append(tuple(send(c, ring) for c in chunks[-1]))

        value_wt = value_weight.T
        own = history_rows(codes, scale_index, scale_table)
        other = send(own, swap)
        k_own, v_own = project(own, key_weight, value_wt)
        k_other, v_other = project(other, key_weight, value_wt)

        order = reorder((GROUP, SPAN, 2 * cand), (1, 0, 2))
        half = users // 2
        partial = [[], []]
        for block in range(slots // SPAN):
            pieces = [c for pair in chunks[block * SPAN : (block + 1) * SPAN] for c in pair]
            for part in range(2):
                partial[part] += attend(part * half, half, live, pieces, k_own, k_other, v_own, v_other, order)

        come = [p[-1] for p in partial]
        for slot in range(slots - 2, -1, -1):
            come = [send(c, back(ring)) for c in come]
            if slot:
                come = [merge(c, p[slot]) for c, p in zip(come, partial)]
        halves = reorder((half, 2, cand), (1, 0, 2))
        first, second = split(*come, partial[0][0], partial[1][0], halves)
        first, second = send(first, back(stay)), send(second, back(cross))
        interest, logits = finish(
            users, first, second, out_weight, norm_gain, hidden_weight, hidden_bias, score_weight
        )
        return interest.reshape(users, cand, width), logits

    in_specs = (
        P("groups", "seq", None),
        P("groups", "seq", None),
        P("groups", "seq"),
        P("groups"),
    ) + (P(),) * 9
    out_specs = (P("groups", "seq", None), P("groups", "seq"))
    return jax.shard_map(on_device, mesh=mesh, in_specs=in_specs, out_specs=out_specs, check_vma=False)
```

time: 581 us -> 184 us (0.32)
  waiting for transfers between devices: 240 us -> 49.5 us
  matrix products: 160 us -> 0 us
  local copies, waits for them, and re-layouts: 128 us -> 11.1 us
  Pallas kernels: 0 us -> 91.8 us
  other arithmetic: 32 us -> 2.41 us
  starting transfers between devices: 0.39 us -> 26.9 us
  between operations: 14.3 us -> 0.98 us
    dot_general x83 -> x0, matrix products: 160 us -> none  [the longest x32 68.7 us: score_block(): jnp.einsum('chd,khd->hck', split_query, split_keys, preferred_element_typ...]
    reduce_scatter x3 -> x0, waiting for transfers between devices: 158 us -> none  [sum_in_order(): blocks = lax.psum_scatter(blocks, axes[k], scatter_dimension=0, tiled=True)]
    pallas_call x0 -> x22, Pallas kernels: none -> 91.8 us  [the longest x4 44.5 us: attend(): pl.pallas_call(functools.partial(attend_body, base), grid_spec=pltpu.Pref...]
    dynamic_slice x128 -> x0, local copies, waits for them, and re-layouts: 79.7 us -> none  [the longest x96 52.8 us: on_device(): peak_rows = lax.map(first_pass, (queries, all_keys, live_mask))]
    all_gather x2 -> x0, waiting for transfers between devices: 74.4 us -> none  [the longest x1 74.4 us: total_of_pieces(): blocks = lax.all_gather(array, axis)]
    ppermute x0 -> x33, waiting for transfers between devices: none -> 49.5 us  [on_device(): send = lambda array, pairs: lax.ppermute(array, 'seq', pairs)]
    dynamic_update_slice x96 -> x0, local copies, waits for them, and re-layouts: 28.2 us -> none  [the longest x32 13.9 us: on_device(): all_keys, all_values = lax.map(project, (codes, scale_index))]
    ppermute x0 -> x33, starting transfers between devices: none -> 26.9 us  [on_device(): send = lambda array, pairs: lax.ppermute(array, 'seq', pairs)]
  transfers between devices with their start and end apart: 6 -> 33, of which waited for: 5 -> 17; matrix products, arithmetic and copies ran while one was open for 20% -> 2% of each run, Pallas kernels for 0% -> 38%
where the time goes in v1:
time: 184 us; the launch traced here: 183 us
  Pallas kernels  91.8 us (50%)
  waiting for transfers between devices  49.5 us (27%)
  starting transfers between devices  26.9 us (15%)
  local copies, waits for them, and re-layouts  11.1 us (6%)
  other arithmetic  2.41 us (1%)
    ppermute x33, waiting for transfers between devices, on_device(): send = lambda array, pairs: lax.ppermute(array, 'seq', pairs)  49.5 us
    pallas_call x4, Pallas kernels, attend(): pl.pallas_call(functools.partial(attend_body, base), grid_spec=pltpu.Pref...  44.5 us
    ppermute x33, starting transfers between devices, on_device(): send = lambda array, pairs: lax.ppermute(array, 'seq', pairs)  26.9 us
    pallas_call x12, Pallas kernels, merge(): pl.pallas_call(merge_body, out_shape=jax.ShapeDtypeStruct(came.shape, jnp...  20.4 us
    pallas_call x2, Pallas kernels, project(): pl.pallas_call(project_body, grid=(users // BATCH,), in_specs=[pl.BlockSp...  14.6 us
    unnamed x71, local copies, waits for them, and re-layouts  10.5 us
    pallas_call x1, Pallas kernels, history_rows(): pl.pallas_call(history_body, grid=(users // BATCH,), in_specs=[pl.BlockSp...  5.58 us
  transfers between devices with their start and end apart: 33, of which 17 were waited for; matrix products, arithmetic and copies ran while one was open for 2% of the time, Pallas kernels for 38%

profile of v1, /device:TPU:70, one launch (start us, length us, event | category | flops | bytes accessed | tf_op | source)
XLA Modules:
  0.0 182.8 jit_solution(5847193057009231223)
XLA Ops:
  0.6 5.6 %history.1.rows = bf16[16,512,256]{2,1,0:T(8,128)(2,1)} custom-call(s32[16,128,256]{2,1,0:T(8,128)} %words.1, s32[16,512]{1,0:T(8,128)} %index.1, f32[1,256]{1,0:T(1,128)} %bitcast.15), custom_call_target="tpu_custom_call" | custom-call | flops 2000000000 | bytes 6000000 | tf_op jit(solution)/shard_map/history/pallas_call | solution.py:63
  6.2 1.8 query.1
  9.6 13.6 %collective-permute-start.5 = (bf16[16,16,256]{2,1,0:T(8,128)(2,1)}, bf16[16,16,256]{2,1,0:T(8,128)(2,1)S(1)}, u32[]{:S(2)}, u32[]{:S(2)}) collective-permute-start(bf16[16,16,256]{2,1,0:T(8,128)(2,1)} %bitcast.11), channel_id=1, source_target_pairs={{1,0},{3,2},{5,4},{7,6},{9,8},{11,10},{13,12},{15,14},{17,16},{19,... | collective-permute-start | bytes 393224 | tf_op jit(solution)/shard_map/ppermute | solution.py:373
  24.4 1.8 collective-permute-done.5.refs_1_
  27.2 2.1 %collective-permute-done.1.refs_2_ = bf16[16,16,256]{2,1,0:T(8,128)(2,1)S(1)} collective-permute-done((bf16[16,16,256]{2,1,0:T(8,128)(2,1)S(1)}, bf16[16,16,256]{2,1,0:T(8,128)(2,1)S(1)}, u32[]{:S(2)}, u32[]{:S(2)}) %collective-permute-start.1) | collective-permute-done | bytes 131104 | tf_op jit(solution)/shard_map/ppermute | solution.py:373
  29.4 3.0 %collective-permute-done.6.refs_3_ = bf16[16,16,256]{2,1,0:T(8,128)(2,1)S(1)} collective-permute-done((bf16[16,16,256]{2,1,0:T(8,128)(2,1)S(1)}, bf16[16,16,256]{2,1,0:T(8,128)(2,1)S(1)}, u32[]{:S(2)}, u32[]{:S(2)}) %collective-permute-start.6) | collective-permute-done | bytes 131104 | tf_op jit(solution)/shard_map/ppermute | solution.py:373
  32.4 3.1 %collective-permute-done.2.refs_4_ = bf16[16,16,256]{2,1,0:T(8,128)(2,1)S(1)} collective-permute-done((bf16[16,16,256]{2,1,0:T(8,128)(2,1)S(1)}, bf16[16,16,256]{2,1,0:T(8,128)(2,1)S(1)}, u32[]{:S(2)}, u32[]{:S(2)}) %collective-permute-start.2) | collective-permute-done | bytes 131104 | tf_op jit(solution)/shard_map/ppermute | solution.py:373
  35.5 3.0 %collective-permute-done.7.refs_5_ = bf16[16,16,256]{2,1,0:T(8,128)(2,1)S(1)} collective-permute-done((bf16[16,16,256]{2,1,0:T(8,128)(2,1)S(1)}, bf16[16,16,256]{2,1,0:T(8,128)(2,1)S(1)}, u32[]{:S(2)}, u32[]{:S(2)}) %collective-permute-start.7) | collective-permute-done | bytes 131104 | tf_op jit(solution)/shard_map/ppermute | solution.py:373
  38.6 3.1 %collective-permute-done.3.refs_6_ = bf16[16,16,256]{2,1,0:T(8,128)(2,1)S(1)} collective-permute-done((bf16[16,16,256]{2,1,0:T(8,128)(2,1)S(1)}, bf16[16,16,256]{2,1,0:T(8,128)(2,1)S(1)}, u32[]{:S(2)}, u32[]{:S(2)}) %collective-permute-start.3) | collective-permute-done | bytes 131104 | tf_op jit(solution)/shard_map/ppermute | solution.py:373
  41.7 3.0 %collective-permute-done.8.refs_7_ = bf16[16,16,256]{2,1,0:T(8,128)(2,1)S(1)} collective-permute-done((bf16[16,16,256]{2,1,0:T(8,128)(2,1)S(1)}, bf16[16,16,256]{2,1,0:T(8,128)(2,1)S(1)}, u32[]{:S(2)}, u32[]{:S(2)}) %collective-permute-start.8) | collective-permute-done | bytes 131104 | tf_op jit(solution)/shard_map/ppermute | solution.py:373
  47.9 3.0 %collective-permute-done.9.refs_1_ = bf16[16,16,256]{2,1,0:T(8,128)(2,1)S(1)} collective-permute-done((bf16[16,16,256]{2,1,0:T(8,128)(2,1)S(1)}, bf16[16,16,256]{2,1,0:T(8,128)(2,1)S(1)}, u32[]{:S(2)}, u32[]{:S(2)}) %collective-permute-start.9) | collective-permute-done | bytes 131104 | tf_op jit(solution)/shard_map/ppermute | solution.py:373
  51.0 7.3 %project.2 = (bf16[16,512,256]{2,1,0:T(8,128)(2,1)}, bf16[16,288,512]{2,1,0:T(8,128)(2,1)}) custom-call(bf16[16,512,256]{2,1,0:T(8,128)(2,1)} %history.1.rows, bf16[256,256]{1,0:T(8,128)(2,1)} %key_w.3, bf16[256,256]{1,0:T(8,128)(2,1)} %bitcast.12), custom_call_target="tpu_custom_call" | custom-call | flops 3000000000 | bytes 12000000 | tf_op jit(solution)/shard_map/project/pallas_call | solution.py:95
  59.4 5.3 %collective-permute-done.12.refs_4_ = bf16[16,16,256]{2,1,0:T(8,128)(2,1)S(1)} collective-permute-done((bf16[16,16,256]{2,1,0:T(8,128)(2,1)S(1)}, bf16[16,16,256]{2,1,0:T(8,128)(2,1)S(1)}, u32[]{:S(2)}, u32[]{:S(2)}) %collective-permute-start.12) | collective-permute-done | bytes 131104 | tf_op jit(solution)/shard_map/ppermute | solution.py:373
  66.1 7.3 %project.3 = (bf16[16,512,256]{2,1,0:T(8,128)(2,1)}, bf16[16,288,512]{2,1,0:T(8,128)(2,1)}) custom-call(bf16[16,512,256]{2,1,0:T(8,128)(2,1)} %collective-permute-done.16.rows, bf16[256,256]{1,0:T(8,128)(2,1)} %key_w.3, bf16[256,256]{1,0:T(8,128)(2,1)} %bitcast.13), custom_call_target="tpu_custom_call" | custom-call | flops 3000000000 | bytes 12000000 | tf_op jit(solution)/shard_map/project/pallas_call | solution.py:95
  74.1 11.1 %attend.6 = (bf16[272,256]{1,0:T(8,128)(2,1)}, bf16[272,256]{1,0:T(8,128)(2,1)}, bf16[272,256]{1,0:T(8,128)(2,1)}, bf16[272,256]{1,0:T(8,128)(2,1)}) custom-call(s32[2,16]{1,0:T(2,128)} %fusion.28.live, bf16[16,16,256]{2,1,0:T(8,128)(2,1)} %copy-done.27, bf16[16,16,256]{2,1,0:T(8,128)(2,1)} %copy-done.28, bf16[16,16,256]{2,1,0:T(8,128)(2,1)} %copy-done.29, ...), custom_call_target="tpu_custom_call" | custom-call | flops 6000000000 | bytes 9000000 | tf_op jit(solution)/shard_map/attend/pallas_call | solution.py:216
  85.5 11.1 %attend.4 = (bf16[272,256]{1,0:T(8,128)(2,1)}, bf16[272,256]{1,0:T(8,128)(2,1)}, bf16[272,256]{1,0:T(8,128)(2,1)}, bf16[272,256]{1,0:T(8,128)(2,1)}) custom-call(s32[2,16]{1,0:T(2,128)} %fusion.28.live, bf16[16,16,256]{2,1,0:T(8,128)(2,1)} %copy-done.27, bf16[16,16,256]{2,1,0:T(8,128)(2,1)} %copy-done.28, bf16[16,16,256]{2,1,0:T(8,128)(2,1)} %copy-done.29, ...), custom_call_target="tpu_custom_call" | custom-call | flops 6000000000 | bytes 9000000 | tf_op jit(solution)/shard_map/attend/pallas_call | solution.py:216
  99.2 2.9 %collective-permute-done.17.came = bf16[272,256]{1,0:T(8,128)(2,1)S(1)} collective-permute-done((bf16[272,256]{1,0:T(8,128)(2,1)}, bf16[272,256]{1,0:T(8,128)(2,1)S(1)}, u32[]{:S(2)}, u32[]{:S(2)}) %collective-permute-start.17) | collective-permute-done | bytes 139296 | tf_op jit(solution)/shard_map/ppermute | solution.py:373
  102.7 1.7 merge.12
  110.3 1.7 merge.13
  112.0 2.4 %collective-permute-start.19 = (bf16[272,256]{1,0:T(8,128)(2,1)}, bf16[272,256]{1,0:T(8,128)(2,1)S(1)}, u32[]{:S(2)}, u32[]{:S(2)}) collective-permute-start(bf16[272,256]{1,0:T(8,128)(2,1)} %merge.13), channel_id=1, source_target_pairs={{2,0},{4,2},{6,4},{8,6},{10,8},{12,10},{14,12},{16,14},{18,16},{20... | collective-permute-start | bytes 417800 | tf_op jit(solution)/shard_map/ppermute | solution.py:373
  114.5 11.1 %attend.7 = (bf16[272,256]{1,0:T(8,128)(2,1)}, bf16[272,256]{1,0:T(8,128)(2,1)}, bf16[272,256]{1,0:T(8,128)(2,1)}, bf16[272,256]{1,0:T(8,128)(2,1)}) custom-call(s32[2,16]{1,0:T(2,128)} %fusion.28.live, bf16[16,16,256]{2,1,0:T(8,128)(2,1)} %copy-done.19, bf16[16,16,256]{2,1,0:T(8,128)(2,1)} %copy-done.20, bf16[16,16,256]{2,1,0:T(8,128)(2,1)} %copy-done.21, ...), custom_call_target="tpu_custom_call" | custom-call | flops 6000000000 | bytes 9000000 | tf_op jit(solution)/shard_map/attend/pallas_call | solution.py:216
  126.3 1.7 merge.20
  130.3 11.2 %attend.5 = (bf16[272,256]{1,0:T(8,128)(2,1)}, bf16[272,256]{1,0:T(8,128)(2,1)}, bf16[272,256]{1,0:T(8,128)(2,1)}, bf16[272,256]{1,0:T(8,128)(2,1)}) custom-call(s32[2,16]{1,0:T(2,128)} %fusion.28.live, bf16[16,16,256]{2,1,0:T(8,128)(2,1)} %copy-done.19, bf16[16,16,256]{2,1,0:T(8,128)(2,1)} %copy-done.20, bf16[16,16,256]{2,1,0:T(8,128)(2,1)} %copy-done.21, ...), custom_call_target="tpu_custom_call" | custom-call | flops 6000000000 | bytes 9000000 | tf_op jit(solution)/shard_map/attend/pallas_call | solution.py:216
  142.2 1.7 merge.21
  146.3 2.9 %collective-permute-done.28.came = bf16[272,256]{1,0:T(8,128)(2,1)S(1)} collective-permute-done((bf16[272,256]{1,0:T(8,128)(2,1)}, bf16[272,256]{1,0:T(8,128)(2,1)S(1)}, u32[]{:S(2)}, u32[]{:S(2)}) %collective-permute-start.28) | collective-permute-done | bytes 139296 | tf_op jit(solution)/shard_map/ppermute | solution.py:373
  149.8 1.7 merge.22
  157.4 1.7 merge.23
  159.2 2.4 %collective-permute-start.30 = (bf16[272,256]{1,0:T(8,128)(2,1)}, bf16[272,256]{1,0:T(8,128)(2,1)S(1)}, u32[]{:S(2)}, u32[]{:S(2)}) collective-permute-start(bf16[272,256]{1,0:T(8,128)(2,1)} %merge.23), channel_id=1, source_target_pairs={{2,0},{4,2},{6,4},{8,6},{10,8},{12,10},{14,12},{16,14},{18,16},{20... | collective-permute-start | bytes 417800 | tf_op jit(solution)/shard_map/ppermute | solution.py:373
  164.6 4.6 %collective-permute-done.23.came_a = bf16[272,256]{1,0:T(8,128)(2,1)S(1)} collective-permute-done((bf16[272,256]{1,0:T(8,128)(2,1)}, bf16[272,256]{1,0:T(8,128)(2,1)S(1)}, u32[]{:S(2)}, u32[]{:S(2)}) %collective-permute-start.23) | collective-permute-done | bytes 139296 | tf_op jit(solution)/shard_map/ppermute | solution.py:373
  169.9 2.2 %split.1 = (bf16[272,256]{1,0:T(8,128)(2,1)}, bf16[272,256]{1,0:T(8,128)(2,1)}) custom-call(bf16[272,256]{1,0:T(8,128)(2,1)} %copy-done.3, bf16[272,256]{1,0:T(8,128)(2,1)} %copy-done.1, bf16[272,256]{1,0:T(8,128)(2,1)} %get-tuple-element.44.mine_a, bf16[272,256]{1,0:T(8,128)(2,1)} %get-tuple-element.45.mine_b, bf16[256,256]{1,0:T(8,128)(2,1)} %fusion.21.order), custom_call_target="tpu_custom_call" | custom-call | flops 100000000 | bytes 1000000 | tf_op jit(solution)/shard_map/split/pallas_call | solution.py:286
  174.2 5.3 %collective-permute-done.32.b = bf16[272,256]{1,0:T(8,128)(2,1)S(1)} collective-permute-done((bf16[272,256]{1,0:T(8,128)(2,1)}, bf16[272,256]{1,0:T(8,128)(2,1)S(1)}, u32[]{:S(2)}, u32[]{:S(2)}) %collective-permute-start.32) | collective-permute-done | bytes 139296 | tf_op jit(solution)/shard_map/ppermute | solution.py:373
  180.1 2.7 %finish.1 = (bf16[256,256]{1,0:T(8,128)(2,1)}, f32[16,16]{1,0:T(8,128)}) custom-call(bf16[272,256]{1,0:T(8,128)(2,1)} %copy-done.17, bf16[272,256]{1,0:T(8,128)(2,1)} %copy-done.18, bf16[256,256]{1,0:T(8,128)(2,1)} %out_w.1, f32[1,256]{1,0:T(1,128)} %bitcast.16, bf16[256,512]{1,0:T(8,128)(2,1)} %hidden_w.1, f32[1,512]{1,0:T(1,128)} %bitcast.14, ...), custom_call_target="tpu_custom_call" | custom-call | flops 200000000 | bytes 1000000 | tf_op jit(solution)/shard_map/finish/pallas_call | solution.py:318
  (138 shorter events, 38.4 us)
Async XLA Ops:
  6.2 59.9 %collective-permute-start.16 = (bf16[16,512,256]{2,1,0:T(8,128)(2,1)}, bf16[16,512,256]{2,1,0:T(8,128)(2,1)}, u32[]{:S(2)}, u32[]{:S(2)}) collective-permute-start(bf16[16,512,256]{2,1,0:T(8,128)(2,1)} %history.1.rows), channel_id=1, source_target_pairs={{0,1},{1,0},{2,3},{3,2},{4,5},{5,4},{6,7},{7,6},{8,9},{9,8},{10,11... | collective-permute-start | bytes 12582920 | tf_op jit(solution)/shard_map/ppermute | solution.py:373
  8.0 15.1 %collective-permute-start = (bf16[16,16,256]{2,1,0:T(8,128)(2,1)}, bf16[16,16,256]{2,1,0:T(8,128)(2,1)S(1)}, u32[]{:S(2)}, u32[]{:S(2)}) collective-permute-start(bf16[16,16,256]{2,1,0:T(8,128)(2,1)} %bitcast.10), channel_id=1, source_target_pairs={{0,0},{2,2},{4,4},{6,6},{8,8},{10,10},{12,12},{14,14},{16,16},{18,... | collective-permute-start | bytes 393224 | tf_op jit(solution)/shard_map/ppermute | solution.py:373
  9.6 16.6 %collective-permute-start.5 = (bf16[16,16,256]{2,1,0:T(8,128)(2,1)}, bf16[16,16,256]{2,1,0:T(8,128)(2,1)S(1)}, u32[]{:S(2)}, u32[]{:S(2)}) collective-permute-start(bf16[16,16,256]{2,1,0:T(8,128)(2,1)} %bitcast.11), channel_id=1, source_target_pairs={{1,0},{3,2},{5,4},{7,6},{9,8},{11,10},{13,12},{15,14},{17,16},{19,... | collective-permute-start | bytes 393224 | tf_op jit(solution)/shard_map/ppermute | solution.py:373
  23.2 6.2 %collective-permute-start.1 = (bf16[16,16,256]{2,1,0:T(8,128)(2,1)S(1)}, bf16[16,16,256]{2,1,0:T(8,128)(2,1)S(1)}, u32[]{:S(2)}, u32[]{:S(2)}) collective-permute-start(bf16[16,16,256]{2,1,0:T(8,128)(2,1)S(1)} %collective-permute-done.refs_0_), channel_id=1, source_target_pairs={{0,2},{2,4},{4,6},{6,8},{8,10},{10,12},{12,14},{14,16},{16,18},{18... | collective-permute-start | bytes 393224 | tf_op jit(solution)/shard_map/ppermute | solution.py:373
  26.2 6.2 %collective-permute-start.6 = (bf16[16,16,256]{2,1,0:T(8,128)(2,1)S(1)}, bf16[16,16,256]{2,1,0:T(8,128)(2,1)S(1)}, u32[]{:S(2)}, u32[]{:S(2)}) collective-permute-start(bf16[16,16,256]{2,1,0:T(8,128)(2,1)S(1)} %collective-permute-done.5.refs_1_), channel_id=1, source_target_pairs={{0,2},{2,4},{4,6},{6,8},{8,10},{10,12},{12,14},{14,16},{16,18},{18... | collective-permute-start | bytes 393224 | tf_op jit(solution)/shard_map/ppermute | solution.py:373
  29.4 6.2 %collective-permute-start.2 = (bf16[16,16,256]{2,1,0:T(8,128)(2,1)S(1)}, bf16[16,16,256]{2,1,0:T(8,128)(2,1)S(1)}, u32[]{:S(2)}, u32[]{:S(2)}) collective-permute-start(bf16[16,16,256]{2,1,0:T(8,128)(2,1)S(1)} %collective-permute-done.1.refs_2_), channel_id=1, source_target_pairs={{0,2},{2,4},{4,6},{6,8},{8,10},{10,12},{12,14},{14,16},{16,18},{18... | collective-permute-start | bytes 393224 | tf_op jit(solution)/shard_map/ppermute | solution.py:373
  32.4 6.2 %collective-permute-start.7 = (bf16[16,16,256]{2,1,0:T(8,128)(2,1)S(1)}, bf16[16,16,256]{2,1,0:T(8,128)(2,1)S(1)}, u32[]{:S(2)}, u32[]{:S(2)}) collective-permute-start(bf16[16,16,256]{2,1,0:T(8,128)(2,1)S(1)} %collective-permute-done.6.refs_3_), channel_id=1, source_target_pairs={{0,2},{2,4},{4,6},{6,8},{8,10},{10,12},{12,14},{14,16},{16,18},{18... | collective-permute-start | bytes 393224 | tf_op jit(solution)/shard_map/ppermute | solution.py:373
  35.5 6.2 %collective-permute-start.3 = (bf16[16,16,256]{2,1,0:T(8,128)(2,1)S(1)}, bf16[16,16,256]{2,1,0:T(8,128)(2,1)S(1)}, u32[]{:S(2)}, u32[]{:S(2)}) collective-permute-start(bf16[16,16,256]{2,1,0:T(8,128)(2,1)S(1)} %collective-permute-done.2.refs_4_), channel_id=1, source_target_pairs={{0,2},{2,4},{4,6},{6,8},{8,10},{10,12},{12,14},{14,16},{16,18},{18... | collective-permute-start | bytes 393224 | tf_op jit(solution)/shard_map/ppermute | solution.py:373
  38.6 6.2 %collective-permute-start.8 = (bf16[16,16,256]{2,1,0:T(8,128)(2,1)S(1)}, bf16[16,16,256]{2,1,0:T(8,128)(2,1)S(1)}, u32[]{:S(2)}, u32[]{:S(2)}) collective-permute-start(bf16[16,16,256]{2,1,0:T(8,128)(2,1)S(1)} %collective-permute-done.7.refs_5_), channel_id=1, source_target_pairs={{0,2},{2,4},{4,6},{6,8},{8,10},{10,12},{12,14},{14,16},{16,18},{18... | collective-permute-start | bytes 393224 | tf_op jit(solution)/shard_map/ppermute | solution.py:373
  41.7 6.2 %collective-permute-start.4 = (bf16[16,16,256]{2,1,0:T(8,128)(2,1)S(1)}, bf16[16,16,256]{2,1,0:T(8,128)(2,1)S(1)}, u32[]{:S(2)}, u32[]{:S(2)}) collective-permute-start(bf16[16,16,256]{2,1,0:T(8,128)(2,1)S(1)} %collective-permute-done.3.refs_6_), channel_id=1, source_target_pairs={{0,2},{2,4},{4,6},{6,8},{8,10},{10,12},{12,14},{14,16},{16,18},{18... | collective-permute-start | bytes 393224 | tf_op jit(solution)/shard_map/ppermute | solution.py:373
  44.8 6.2 %collective-permute-start.9 = (bf16[16,16,256]{2,1,0:T(8,128)(2,1)S(1)}, bf16[16,16,256]{2,1,0:T(8,128)(2,1)S(1)}, u32[]{:S(2)}, u32[]{:S(2)}) collective-permute-start(bf16[16,16,256]{2,1,0:T(8,128)(2,1)S(1)} %collective-permute-done.8.refs_7_), channel_id=1, source_target_pairs={{0,2},{2,4},{4,6},{6,8},{8,10},{10,12},{12,14},{14,16},{16,18},{18... | collective-permute-start | bytes 393224 | tf_op jit(solution)/shard_map/ppermute | solution.py:373
  47.9 10.6 %collective-permute-start.10 = (bf16[16,16,256]{2,1,0:T(8,128)(2,1)S(1)}, bf16[16,16,256]{2,1,0:T(8,128)(2,1)S(1)}, u32[]{:S(2)}, u32[]{:S(2)}) collective-permute-start(bf16[16,16,256]{2,1,0:T(8,128)(2,1)S(1)} %collective-permute-done.4.refs_0_), channel_id=1, source_target_pairs={{0,2},{2,4},{4,6},{6,8},{8,10},{10,12},{12,14},{14,16},{16,18},{18... | collective-permute-start | bytes 393224 | tf_op jit(solution)/shard_map/ppermute | solution.py:373
  50.9 7.6 %collective-permute-start.11 = (bf16[16,16,256]{2,1,0:T(8,128)(2,1)S(1)}, bf16[16,16,256]{2,1,0:T(8,128)(2,1)S(1)}, u32[]{:S(2)}, u32[]{:S(2)}) collective-permute-start(bf16[16,16,256]{2,1,0:T(8,128)(2,1)S(1)} %collective-permute-done.9.refs_1_), channel_id=1, source_target_pairs={{0,2},{2,4},{4,6},{6,8},{8,10},{10,12},{12,14},{14,16},{16,18},{18... | collective-permute-start | bytes 393224 | tf_op jit(solution)/shard_map/ppermute | solution.py:373
  58.5 6.2 %collective-permute-start.12 = (bf16[16,16,256]{2,1,0:T(8,128)(2,1)S(1)}, bf16[16,16,256]{2,1,0:T(8,128)(2,1)S(1)}, u32[]{:S(2)}, u32[]{:S(2)}) collective-permute-start(bf16[16,16,256]{2,1,0:T(8,128)(2,1)S(1)} %collective-permute-done.10.refs_2_), channel_id=1, source_target_pairs={{0,2},{2,4},{4,6},{6,8},{8,10},{10,12},{12,14},{14,16},{16,18},{18... | collective-permute-start | bytes 393224 | tf_op jit(solution)/shard_map/ppermute | solution.py:373
  58.6 7.5 %collective-permute-start.13 = (bf16[16,16,256]{2,1,0:T(8,128)(2,1)S(1)}, bf16[16,16,256]{2,1,0:T(8,128)(2,1)S(1)}, u32[]{:S(2)}, u32[]{:S(2)}) collective-permute-start(bf16[16,16,256]{2,1,0:T(8,128)(2,1)S(1)} %collective-permute-done.11.refs_3_), channel_id=1, source_target_pairs={{0,2},{2,4},{4,6},{6,8},{8,10},{10,12},{12,14},{14,16},{16,18},{18... | collective-permute-start | bytes 393224 | tf_op jit(solution)/shard_map/ppermute | solution.py:373
  64.7 8.7 %collective-permute-start.14 = (bf16[16,16,256]{2,1,0:T(8,128)(2,1)S(1)}, bf16[16,16,256]{2,1,0:T(8,128)(2,1)S(1)}, u32[]{:S(2)}, u32[]{:S(2)}) collective-permute-start(bf16[16,16,256]{2,1,0:T(8,128)(2,1)S(1)} %collective-permute-done.12.refs_4_), channel_id=1, source_target_pairs={{0,2},{2,4},{4,6},{6,8},{8,10},{10,12},{12,14},{14,16},{16,18},{18... | collective-permute-start | bytes 393224 | tf_op jit(solution)/shard_map/ppermute | solution.py:373
  66.1 7.3 %collective-permute-start.15 = (bf16[16,16,256]{2,1,0:T(8,128)(2,1)S(1)}, bf16[16,16,256]{2,1,0:T(8,128)(2,1)S(1)}, u32[]{:S(2)}, u32[]{:S(2)}) collective-permute-start(bf16[16,16,256]{2,1,0:T(8,128)(2,1)S(1)} %collective-permute-done.13.refs_5_), channel_id=1, source_target_pairs={{0,2},{2,4},{4,6},{6,8},{8,10},{10,12},{12,14},{14,16},{16,18},{18... | collective-permute-start | bytes 393224 | tf_op jit(solution)/shard_map/ppermute | solution.py:373
  85.2 11.6 %collective-permute-start.24 = (bf16[272,256]{1,0:T(8,128)(2,1)}, bf16[272,256]{1,0:T(8,128)(2,1)S(1)}, u32[]{:S(2)}, u32[]{:S(2)}) collective-permute-start(bf16[272,256]{1,0:T(8,128)(2,1)} %get-tuple-element.37), channel_id=1, source_target_pairs={{2,0},{4,2},{6,4},{8,6},{10,8},{12,10},{14,12},{16,14},{18,16},{20... | collective-permute-start | bytes 417800 | tf_op jit(solution)/shard_map/ppermute | solution.py:373
  96.7 5.4 %collective-permute-start.17 = (bf16[272,256]{1,0:T(8,128)(2,1)}, bf16[272,256]{1,0:T(8,128)(2,1)S(1)}, u32[]{:S(2)}, u32[]{:S(2)}) collective-permute-start(bf16[272,256]{1,0:T(8,128)(2,1)} %get-tuple-element.30), channel_id=1, source_target_pairs={{2,0},{4,2},{6,4},{8,6},{10,8},{12,10},{14,12},{16,14},{18,16},{20... | collective-permute-start | bytes 417800 | tf_op jit(solution)/shard_map/ppermute | solution.py:373
  99.2 6.5 %collective-permute-start.25 = (bf16[272,256]{1,0:T(8,128)(2,1)}, bf16[272,256]{1,0:T(8,128)(2,1)S(1)}, u32[]{:S(2)}, u32[]{:S(2)}) collective-permute-start(bf16[272,256]{1,0:T(8,128)(2,1)} %merge.18), channel_id=1, source_target_pairs={{2,0},{4,2},{6,4},{8,6},{10,8},{12,10},{14,12},{16,14},{18,16},{20... | collective-permute-start | bytes 417800 | tf_op jit(solution)/shard_map/ppermute | solution.py:373
  104.4 5.3 %collective-permute-start.18 = (bf16[272,256]{1,0:T(8,128)(2,1)}, bf16[272,256]{1,0:T(8,128)(2,1)S(1)}, u32[]{:S(2)}, u32[]{:S(2)}) collective-permute-start(bf16[272,256]{1,0:T(8,128)(2,1)} %merge.12), channel_id=1, source_target_pairs={{2,0},{4,2},{6,4},{8,6},{10,8},{12,10},{14,12},{16,14},{18,16},{20... | collective-permute-start | bytes 417800 | tf_op jit(solution)/shard_map/ppermute | solution.py:373
  108.0 17.6 %collective-permute-start.26 = (bf16[272,256]{1,0:T(8,128)(2,1)}, bf16[272,256]{1,0:T(8,128)(2,1)S(1)}, u32[]{:S(2)}, u32[]{:S(2)}) collective-permute-start(bf16[272,256]{1,0:T(8,128)(2,1)} %merge.19), channel_id=1, source_target_pairs={{2,0},{4,2},{6,4},{8,6},{10,8},{12,10},{14,12},{16,14},{18,16},{20... | collective-permute-start | bytes 417800 | tf_op jit(solution)/shard_map/ppermute | solution.py:373
  112.0 16.0 %collective-permute-start.19 = (bf16[272,256]{1,0:T(8,128)(2,1)}, bf16[272,256]{1,0:T(8,128)(2,1)S(1)}, u32[]{:S(2)}, u32[]{:S(2)}) collective-permute-start(bf16[272,256]{1,0:T(8,128)(2,1)} %merge.13), channel_id=1, source_target_pairs={{2,0},{4,2},{6,4},{8,6},{10,8},{12,10},{14,12},{16,14},{18,16},{20... | collective-permute-start | bytes 417800 | tf_op jit(solution)/shard_map/ppermute | solution.py:373
  128.0 13.6 %collective-permute-start.27 = (bf16[272,256]{1,0:T(8,128)(2,1)}, bf16[272,256]{1,0:T(8,128)(2,1)S(1)}, u32[]{:S(2)}, u32[]{:S(2)}) collective-permute-start(bf16[272,256]{1,0:T(8,128)(2,1)} %merge.20), channel_id=1, source_target_pairs={{2,0},{4,2},{6,4},{8,6},{10,8},{12,10},{14,12},{16,14},{18,16},{20... | collective-permute-start | bytes 417800 | tf_op jit(solution)/shard_map/ppermute | solution.py:373
  130.3 13.6 %collective-permute-start.20 = (bf16[272,256]{1,0:T(8,128)(2,1)}, bf16[272,256]{1,0:T(8,128)(2,1)S(1)}, u32[]{:S(2)}, u32[]{:S(2)}) collective-permute-start(bf16[272,256]{1,0:T(8,128)(2,1)} %merge.14), channel_id=1, source_target_pairs={{2,0},{4,2},{6,4},{8,6},{10,8},{12,10},{14,12},{16,14},{18,16},{20... | collective-permute-start | bytes 417800 | tf_op jit(solution)/shard_map/ppermute | solution.py:373
  143.9 5.3 %collective-permute-start.28 = (bf16[272,256]{1,0:T(8,128)(2,1)}, bf16[272,256]{1,0:T(8,128)(2,1)S(1)}, u32[]{:S(2)}, u32[]{:S(2)}) collective-permute-start(bf16[272,256]{1,0:T(8,128)(2,1)} %merge.21), channel_id=1, source_target_pairs={{2,0},{4,2},{6,4},{8,6},{10,8},{12,10},{14,12},{16,14},{18,16},{20... | collective-permute-start | bytes 417800 | tf_op jit(solution)/shard_map/ppermute | solution.py:373
  146.3 6.5 %collective-permute-start.21 = (bf16[272,256]{1,0:T(8,128)(2,1)}, bf16[272,256]{1,0:T(8,128)(2,1)S(1)}, u32[]{:S(2)}, u32[]{:S(2)}) collective-permute-start(bf16[272,256]{1,0:T(8,128)(2,1)} %merge.15), channel_id=1, source_target_pairs={{2,0},{4,2},{6,4},{8,6},{10,8},{12,10},{14,12},{16,14},{18,16},{20... | collective-permute-start | bytes 417800 | tf_op jit(solution)/shard_map/ppermute | solution.py:373
  151.5 5.3 %collective-permute-start.29 = (bf16[272,256]{1,0:T(8,128)(2,1)}, bf16[272,256]{1,0:T(8,128)(2,1)S(1)}, u32[]{:S(2)}, u32[]{:S(2)}) collective-permute-start(bf16[272,256]{1,0:T(8,128)(2,1)} %merge.22), channel_id=1, source_target_pairs={{2,0},{4,2},{6,4},{8,6},{10,8},{12,10},{14,12},{16,14},{18,16},{20... | collective-permute-start | bytes 417800 | tf_op jit(solution)/shard_map/ppermute | solution.py:373
  155.1 6.5 %collective-permute-start.22 = (bf16[272,256]{1,0:T(8,128)(2,1)}, bf16[272,256]{1,0:T(8,128)(2,1)S(1)}, u32[]{:S(2)}, u32[]{:S(2)}) collective-permute-start(bf16[272,256]{1,0:T(8,128)(2,1)} %merge.16), channel_id=1, source_target_pairs={{2,0},{4,2},{6,4},{8,6},{10,8},{12,10},{14,12},{16,14},{18,16},{20... | collective-permute-start | bytes 417800 | tf_op jit(solution)/shard_map/ppermute | solution.py:373
  159.2 5.5 %collective-permute-start.30 = (bf16[272,256]{1,0:T(8,128)(2,1)}, bf16[272,256]{1,0:T(8,128)(2,1)S(1)}, u32[]{:S(2)}, u32[]{:S(2)}) collective-permute-start(bf16[272,256]{1,0:T(8,128)(2,1)} %merge.23), channel_id=1, source_target_pairs={{2,0},{4,2},{6,4},{8,6},{10,8},{12,10},{14,12},{16,14},{18,16},{20... | collective-permute-start | bytes 417800 | tf_op jit(solution)/shard_map/ppermute | solution.py:373
  163.9 5.3 %collective-permute-start.23 = (bf16[272,256]{1,0:T(8,128)(2,1)}, bf16[272,256]{1,0:T(8,128)(2,1)S(1)}, u32[]{:S(2)}, u32[]{:S(2)}) collective-permute-start(bf16[272,256]{1,0:T(8,128)(2,1)} %merge.17), channel_id=1, source_target_pairs={{2,0},{4,2},{6,4},{8,6},{10,8},{12,10},{14,12},{16,14},{18,16},{20... | collective-permute-start | bytes 417800 | tf_op jit(solution)/shard_map/ppermute | solution.py:373
  173.6 5.9 %collective-permute-start.32 = (bf16[272,256]{1,0:T(8,128)(2,1)}, bf16[272,256]{1,0:T(8,128)(2,1)S(1)}, u32[]{:S(2)}, u32[]{:S(2)}) collective-permute-start(bf16[272,256]{1,0:T(8,128)(2,1)} %get-tuple-element.47), channel_id=1, source_target_pairs={{0,1},{2,3},{4,5},{6,7},{8,9},{10,11},{12,13},{14,15},{16,17},{18,... | collective-permute-start | bytes 417800 | tf_op jit(solution)/shard_map/ppermute | solution.py:373
  (36 other events, 377.0 us)

commit v2 on v1

--- a/solution.py
+++ b/solution.py
@@ -6,6 +6,7 @@
 from jax.experimental import pallas as pl
 from jax.experimental.pallas import tpu as pltpu
 from jax.sharding import PartitionSpec as P
+
 
 HEADS = 4
 GRAIN = 128
@@ -15,7 +16,9 @@
 GROUP = 4
 STATS = 16
 ONES = 16
+PARTS = 2
 BATCH = 4
+FULL = 62.5
 
 NT = (((1,), (1,)), ((), ()))
 TN = (((0,), (0,)), ((), ()))
@@ -27,6 +30,10 @@
 
 def cost(flops, moved):
     return pl.CostEstimate(flops=int(flops), bytes_accessed=int(moved), transcendentals=0)
+
+
+def room(mib):
+    return pltpu.CompilerParams(vmem_limit_bytes=int(mib * 2**20))
 
 
 def history_body(words, index, table, out):
@@ -71,6 +78,7 @@
         out_specs=pl.BlockSpec((BATCH, places, width), lambda u: (u, 0, 0)),
         out_shape=jax.ShapeDtypeStruct((users, places, width), jnp.bfloat16),
         cost_estimate=cost(2e9, 6e6),
+        compiler_params=room(FULL),
         name="history",
     )(codes, scale_index, scale_table.reshape(1, levels))
 
@@ -109,6 +117,7 @@
             jax.ShapeDtypeStruct((users, tall, places), jnp.bfloat16),
         ],
         cost_estimate=cost(3e9, 12e6),
+        compiler_params=room(12),
         name="project",
     )(rows, key_w, value_wt)
 
@@ -124,6 +133,7 @@
         query_body,
         out_shape=jax.ShapeDtypeStruct((rows.shape[0], weight.shape[1]), jnp.bfloat16),
         cost_estimate=cost(3e7, 4e5),
+        compiler_params=room(2),
         name="query",
     )(rows, weight)
 
@@ -134,67 +144,83 @@
     return [hi, mid, peak - hi - mid]
 
 
-def attend_user(user, k, pieces, live, k_own, k_other, v_own, v_other, scores, weights, held, at):
-    width = k_own.shape[2]
-    head = width // HEADS
-    pair = 2 * head
-    counts = (live[0, user], live[1, user])
-    per = k_own.shape[1] // GRAIN
-    lanes = held.shape[1] // GROUP
-
-    @pl.when(counts[0] + counts[1] == 0)
-    def _():
-        held[0:width, at] = jnp.zeros((width, lanes), jnp.bfloat16)
-        row = lax.broadcasted_iota(jnp.int32, (STATS, lanes), 0)
-        held[width : width + STATS, at] = jnp.where(row < HEADS, NEG, 0.0).astype(jnp.bfloat16)
-
-    @pl.when(counts[0] + counts[1] > 0)
-    def _():
-        q = jnp.concatenate([r[user] for r in pieces], axis=0)
-        lane = lax.broadcasted_iota(jnp.int32, (lanes, pair), 1)
-        peaks, totals = [], []
-        for p in range(HEADS // 2):
-            both = q[:, p * pair : (p + 1) * pair].astype(jnp.float32)
-            right = jnp.concatenate(
-                [jnp.where(lane < head, both, 0.0), jnp.where(lane < head, 0.0, both)], axis=0
-            ).astype(jnp.bfloat16)
-            tops = []
-            for t in range(2 * per):
-                source, place = ((k_own, t), (k_other, t - per))[t >= per]
-                s = dot(source[k, place * GRAIN : (place + 1) * GRAIN, p * pair : (p + 1) * pair], right, NT)
-                scores[p, t * GRAIN : (t + 1) * GRAIN, :] = s
-                alive = place < counts[t >= per]
-                tops.append(jnp.where(alive, jnp.max(s, axis=0, keepdims=True), NEG))
-            peaks.append(functools.reduce(jnp.maximum, tops))
-        for p in range(HEADS // 2):
-            for t in range(2 * per):
-                alive = t % per < counts[t >= per]
-                lift = jnp.where(alive, peaks[p], -NEG)
-                w = jnp.exp(scores[p, t * GRAIN : (t + 1) * GRAIN, :] - lift)
-                weights[p, t * GRAIN : (t + 1) * GRAIN, :] = w.astype(jnp.bfloat16)
-            rows = slice(p * (pair + ONES), (p + 1) * (pair + ONES))
-            half = per * GRAIN
-            o = dot(v_own[k, rows, :], weights[p, 0:half, :]) + dot(v_other[k, rows, :], weights[p, half : 2 * half, :])
-            held[p * pair : p * pair + head, at] = o[0:head, 0:lanes].astype(jnp.bfloat16)
-            held[p * pair + head : (p + 1) * pair, at] = o[head:pair, lanes:].astype(jnp.bfloat16)
-            totals += [o[pair : pair + 1, 0:lanes], o[pair : pair + 1, lanes:]]
-        peak = jnp.concatenate([x for p in peaks for x in (p[:, 0:lanes], p[:, lanes:])], axis=0)
-        stats = jnp.concatenate(parts_of(peak) + totals, axis=0)
-        held[width : width + STATS, at] = stats.astype(jnp.bfloat16)
+def pair_query(q, p):
+    pair = 2 * q.shape[1] // HEADS
+    lane = lax.broadcasted_iota(jnp.int32, (q.shape[0], pair), 1)
+    both = q[:, p * pair : (p + 1) * pair].astype(jnp.float32)
+    two = [jnp.where(lane < pair // 2, both, 0.0), jnp.where(lane < pair // 2, 0.0, both)]
+    return jnp.concatenate(two, axis=0).astype(jnp.bfloat16)
+
+
+def score_pair(p, k, q, counts, sources, scores):
+    per = sources[0].shape[1] // GRAIN
+    pair = 2 * q.shape[1] // HEADS
+    right = pair_query(q, p)
+    tops = []
+    for half, source in enumerate(sources):
+        for t in range(per):
+            s = dot(source[k, t * GRAIN : (t + 1) * GRAIN, p * pair : (p + 1) * pair], right, NT)
+            at = (half * per + t) * GRAIN
+            scores[at : at + GRAIN, :] = s
+            tops.append(jnp.where(t < counts[half], jnp.max(s, axis=0, keepdims=True), NEG))
+    return functools.reduce(jnp.maximum, tops)
+
+
+def blend_pair(p, k, peak, counts, sources, scores, weights):
+    span = sources[0].shape[2]
+    per = span // GRAIN
+    tall = sources[0].shape[1] // (HEADS // 2)
+    o = 0.0
+    for half, source in enumerate(sources):
+        for t in range(per):
+            lift = jnp.where(t < counts[half], peak, -NEG)
+            rows = slice((half * per + t) * GRAIN, (half * per + t + 1) * GRAIN)
+            weights[rows, :] = jnp.exp(scores[rows, :] - lift).astype(jnp.bfloat16)
+        o = o + dot(source[k, p * tall : (p + 1) * tall, :], weights[half * span : (half + 1) * span, :])
+    return o
 
 
 def attend_body(base, live, *refs):
-    pieces, refs = refs[: 2 * SPAN], refs[2 * SPAN :]
+    hops, refs = refs[: 2 * SPAN + 2], refs[2 * SPAN + 2 :]
     (k_own, k_other, v_own, v_other, order), refs = refs[:5], refs[5:]
     outs, (scores, weights, held) = refs[:SPAN], refs[SPAN:]
     lanes = held.shape[1] // GROUP
-    batch = k_own.shape[0]
+    batch, _, width = k_own.shape
+    pair = 2 * width // HEADS
+    head = pair // 2
+    pairs = HEADS // 2
     i = pl.program_id(1)
+    north = live[2, 0] > 0
+
+    def begin(n):
+        k, p = divmod(n, pairs)
+        place = pl.program_id(0) * GROUP + i * batch + k
+        user = base + place
+        counts = (live[0, user], live[1, user])
+        rows = [jnp.where(north, hops[j + 2][user], hops[j][user]) for j in range(2 * SPAN)]
+        q = jnp.concatenate(rows, axis=0)
+        return counts, score_pair(p, k, q, counts, (k_own, k_other), scores.at[n])
+
+    def end(n, counts, peak):
+        k, p = divmod(n, pairs)
+        at = pl.ds(pl.multiple_of((i * batch + k) * lanes, lanes), lanes)
+        o = blend_pair(p, k, peak, counts, (v_own, v_other), scores.at[n], weights.at[n])
+        held[p * pair : p * pair + head, at] = o[0:head, 0:lanes].astype(jnp.bfloat16)
+        held[p * pair + head : (p + 1) * pair, at] = o[head:pair, lanes:].astype(jnp.bfloat16)
+        return [o[pair : pair + 1, 0:lanes], o[pair : pair + 1, lanes:]]
+
+    begun = [begin(0)]
+    totals = []
+    for n in range(batch * pairs):
+        if n + 1 < batch * pairs:
+            begun.append(begin(n + 1))
+        totals.append(end(n, *begun[n]))
     for k in range(batch):
-        place = i * batch + k
-        user = base + pl.program_id(0) * GROUP + place
-        at = pl.ds(pl.multiple_of(place * lanes, lanes), lanes)
-        attend_user(user, k, pieces, live, k_own, k_other, v_own, v_other, scores, weights, held, at)
+        at = pl.ds(pl.multiple_of((i * batch + k) * lanes, lanes), lanes)
+        peaks = [begun[k * pairs + p][1] for p in range(pairs)]
+        peak = jnp.concatenate([x for p in peaks for x in (p[:, 0:lanes], p[:, lanes:])], axis=0)
+        sums = [x for p in range(pairs) for x in totals[k * pairs + p]]
+        held[width : width + STATS, at] = jnp.concatenate(parts_of(peak) + sums, axis=0).astype(jnp.bfloat16)
 
     @pl.when(i == GROUP // batch - 1)
     def _():
@@ -203,22 +229,20 @@
             outs[s][...] = mixed[:, s * lanes : (s + 1) * lanes]
 
 
-def attend(base, users, live, pieces, k_own, k_other, v_own, v_other, order):
-    cand, width = pieces[0].shape[1:]
+def attend(base, groups, live, hops, k_own, k_other, v_own, v_other, order):
+    cand, width = hops[0].shape[1:]
     places = k_own.shape[1]
     tall = v_own.shape[1]
-    lanes = cand * len(pieces)
+    lanes = cand * 2 * SPAN
     deep = width + STATS
     batch = 2
-    steps = GROUP // batch
-    some = lambda g, i, live: (base // batch + g * steps + i, 0, 0)
-    flat = lambda g, i, live: (0, 0)
+    some = lambda g, i, live: (base // batch + g * (GROUP // batch) + i, 0, 0)
     return pl.pallas_call(
         functools.partial(attend_body, base),
         grid_spec=pltpu.PrefetchScalarGridSpec(
             num_scalar_prefetch=1,
-            grid=(users // GROUP, steps),
-            in_specs=[pl.BlockSpec(memory_space=pltpu.VMEM) for _ in pieces]
+            grid=(groups, GROUP // batch),
+            in_specs=[pl.BlockSpec(memory_space=pltpu.VMEM) for _ in hops]
             + [
                 pl.BlockSpec((batch, places, width), some),
                 pl.BlockSpec((batch, places, width), some),
@@ -228,15 +252,16 @@
             ],
             out_specs=[pl.BlockSpec((deep, lanes), lambda g, i, live: (0, g))] * SPAN,
             scratch_shapes=[
-                pltpu.VMEM((HEADS // 2, 2 * places, 2 * lanes), jnp.float32),
-                pltpu.VMEM((HEADS // 2, 2 * places, 2 * lanes), jnp.bfloat16),
+                pltpu.VMEM((batch * HEADS // 2, 2 * places, 2 * lanes), jnp.float32),
+                pltpu.VMEM((batch * HEADS // 2, 2 * places, 2 * lanes), jnp.bfloat16),
                 pltpu.VMEM((deep, GROUP * lanes), jnp.bfloat16),
             ],
         ),
-        out_shape=[jax.ShapeDtypeStruct((deep, users * lanes // SPAN), jnp.bfloat16)] * SPAN,
-        cost_estimate=cost(6e9, 9e6),
+        out_shape=[jax.ShapeDtypeStruct((deep, groups * lanes), jnp.bfloat16)] * SPAN,
+        cost_estimate=cost(3e9 * groups, 5e6),
+        compiler_params=room(20),
         name="attend",
-    )(live, *pieces, k_own, k_other, v_own, v_other, order)
+    )(live, *hops, k_own, k_other, v_own, v_other, order)
 
 
 def merged(a, b):
@@ -261,8 +286,12 @@
     return jnp.concatenate([r.astype(jnp.bfloat16) for r in rows] + [stats.astype(jnp.bfloat16)], axis=0)
 
 
-def merge_body(came, mine, out):
-    out[...] = packed(*merged(came[...], mine[...]))
+def merge_body(came, *refs):
+    mine, out = refs[:-1], refs[-1]
+    lanes = came.shape[1] // len(mine)
+    for n, m in enumerate(mine):
+        at = slice(n * lanes, (n + 1) * lanes)
+        out[:, at] = packed(*merged(came[:, at], m[...]))
 
 
 def merge(came, mine):
@@ -270,25 +299,34 @@
         merge_body,
         out_shape=jax.ShapeDtypeStruct(came.shape, jnp.bfloat16),
         cost_estimate=cost(1e8, 5e5),
+        compiler_params=room(3),
         name="merge",
-    )(came, mine)
-
-
-def split_body(came_a, came_b, mine_a, mine_b, order, near, far):
-    lanes = came_a.shape[1] // 2
-    for n, (came, mine) in enumerate(((came_a, mine_a), (came_b, mine_b))):
-        both = dot(packed(*merged(came[...], mine[...])), order[...]).astype(jnp.bfloat16)
-        near[:, n * lanes : (n + 1) * lanes] = both[:, 0:lanes]
-        far[:, n * lanes : (n + 1) * lanes] = both[:, lanes:]
-
-
-def split(came_a, came_b, mine_a, mine_b, order):
-    return pl.pallas_call(
-        split_body,
-        out_shape=[jax.ShapeDtypeStruct(came_a.shape, jnp.bfloat16)] * 2,
+    )(came, *mine)
+
+
+def split_body(parts, *refs):
+    came, mine, (order, near, far) = refs[:parts], refs[parts:-3], refs[-3:]
+    lanes = order.shape[0]
+    per = len(mine) // parts
+    for n, m in enumerate(mine):
+        at = (n % per) * lanes
+        both = packed(*merged(came[n // per][:, at : at + lanes], m[...]))
+        both = dot(both, order[...]).astype(jnp.bfloat16)
+        to = slice(n * lanes // 2, (n + 1) * lanes // 2)
+        near[:, to] = both[:, : lanes // 2]
+        far[:, to] = both[:, lanes // 2 :]
+
+
+def split(came, mine, order):
+    deep, lanes = came[0].shape
+    shape = jax.ShapeDtypeStruct((deep, lanes * len(came) // 2), jnp.bfloat16)
+    return pl.pallas_call(
+        functools.partial(split_body, len(came)),
+        out_shape=[shape] * 2,
         cost_estimate=cost(1e8, 1e6),
+        compiler_params=room(6),
         name="split",
-    )(came_a, came_b, mine_a, mine_b, order)
+    )(*came, *mine, order)
 
 
 def finish_body(a, b, out_w, gain, hidden_w, bias, score_w, interest, logits):
@@ -322,6 +360,7 @@
             jax.ShapeDtypeStruct((users, lanes // users), jnp.float32),
         ],
         cost_estimate=cost(2e8, 1e6),
+        compiler_params=room(8),
         name="finish",
     )(a, b, out_w, gain.reshape(1, width), hidden_w, bias.reshape(1, wide), score_w.reshape(1, wide))
 
@@ -375,11 +414,13 @@
         mate = me + 1 - 2 * (me % 2)
         starts = jnp.stack([me, mate])[:, None] * places
         live = jnp.clip((lengths[None, :] - starts) // GRAIN, 0, places // GRAIN).astype(jnp.int32)
+        live = jnp.concatenate([live, jnp.full((1, users), me % 2, jnp.int32)])
 
         mine = query_rows(candidates.reshape(users * cand, width), query_weight).reshape(users, cand, width)
-        chunks = [(send(mine, stay), send(mine, cross))]
-        for _ in range(slots - 1):
-            chunks.append(tuple(send(c, ring) for c in chunks[-1]))
+        hops = [mine, send(mine, swap)]
+        for _ in range(1, slots + 1):
+            for _ in range(2):
+                hops.append(send(hops[-2], ring))
 
         value_wt = value_weight.T
         own = history_rows(codes, scale_index, scale_table)
@@ -388,20 +429,27 @@
         k_other, v_other = project(other, key_weight, value_wt)
 
         order = reorder((GROUP, SPAN, 2 * cand), (1, 0, 2))
-        half = users // 2
-        partial = [[], []]
-        for block in range(slots // SPAN):
-            pieces = [c for pair in chunks[block * SPAN : (block + 1) * SPAN] for c in pair]
-            for part in range(2):
-                partial[part] += attend(part * half, half, live, pieces, k_own, k_other, v_own, v_other, order)
-
-        come = [p[-1] for p in partial]
+        partial = []
+        for block, groups in ((0, 1), (1, users // PARTS // GROUP)):
+            calls = []
+            for call in range(users // (groups * GROUP)):
+                base = call * groups * GROUP
+                near_hops = hops[2 * block * SPAN : 2 * (block + 1) * SPAN + 2]
+                calls.append(attend(base, groups, live, near_hops, k_own, k_other, v_own, v_other, order))
+            partial.append(calls)
+
+        def result(part, slot):
+            calls = partial[slot // SPAN]
+            per = len(calls) // PARTS
+            return [c[slot % SPAN] for c in calls[part * per : (part + 1) * per]]
+
+        come = [result(part, slots - 1)[0] for part in range(PARTS)]
         for slot in range(slots - 2, -1, -1):
             come = [send(c, back(ring)) for c in come]
             if slot:
-                come = [merge(c, p[slot]) for c, p in zip(come, partial)]
-        halves = reorder((half, 2, cand), (1, 0, 2))
-        first, second = split(*come, partial[0][0], partial[1][0], halves)
+                come = [merge(c, result(part, slot)) for part, c in enumerate(come)]
+        halves = reorder((GROUP, 2, cand), (1, 0, 2))
+        first, second = split(come, [x for part in range(PARTS) for x in result(part, 0)], halves)
         first, second = send(first, back(stay)), send(second, back(cross))
         interest, logits = finish(
             users, first, second, out_weight, norm_gain, hidden_weight, hidden_bias, score_weight
@@ -415,4 +463,5 @@
         P("groups"),
     ) + (P(),) * 9
     out_specs = (P("groups", "seq", None), P("groups", "seq"))
+
     return jax.shard_map(on_device, mesh=mesh, in_specs=in_specs, out_specs=out_specs, check_vma=False)

time: 184 us -> 146 us (0.79)
  Pallas kernels: 91.8 us -> 44 us
  waiting for transfers between devices: 49.5 us -> 64 us
  local copies, waits for them, and re-layouts: 11.1 us -> 6.62 us
  starting transfers between devices: 26.9 us -> 29.8 us
  other arithmetic: 2.41 us -> 0.38 us
    pallas_call x12, Pallas kernels: 20.4 us -> 0.95 us  [merge(): pl.pallas_call(merge_body, out_shape=jax.ShapeDtypeStruct(came.shape, jnp...]
    pallas_call x4 -> x6, Pallas kernels: 44.5 us -> 27.7 us  [attend(): pl.pallas_call(functools.partial(attend_body, base), grid_spec=pltpu.Pref...]
    ppermute x33 -> x34, waiting for transfers between devices: 49.5 us -> 64 us  [on_device(): send = lambda array, pairs: lax.ppermute(array, 'seq', pairs)]
    pallas_call x2, Pallas kernels: 14.6 us -> 7.61 us  [project(): pl.pallas_call(project_body, grid=(users // BATCH,), in_specs=[pl.BlockSp...]
    unnamed x71 -> x33, local copies, waits for them, and re-layouts: 10.5 us -> 6.61 us
    ppermute x33 -> x34, starting transfers between devices: 26.9 us -> 29.8 us  [on_device(): send = lambda array, pairs: lax.ppermute(array, 'seq', pairs)]
  transfers between devices with their start and end apart: 33 -> 34, of which waited for: 17 -> 20; matrix products, arithmetic and copies ran while one was open for 2% -> 0% of each run, Pallas kernels for 38% -> 20%
where the time goes in v2:
time: 146 us
  waiting for transfers between devices  64 us (44%)
  Pallas kernels  44 us (30%)
  starting transfers between devices  29.8 us (20%)
  local copies, waits for them, and re-layouts  6.62 us (5%)
    ppermute x34, waiting for transfers between devices, on_device(): send = lambda array, pairs: lax.ppermute(array, 'seq', pairs)  64 us
    ppermute x34, starting transfers between devices, on_device(): send = lambda array, pairs: lax.ppermute(array, 'seq', pairs)  29.8 us
    pallas_call x6, Pallas kernels, attend(): pl.pallas_call(functools.partial(attend_body, base), grid_spec=pltpu.Pref...  27.7 us
    pallas_call x2, Pallas kernels, project(): pl.pallas_call(project_body, grid=(users // BATCH,), in_specs=[pl.BlockSp...  7.61 us
    unnamed x33, local copies, waits for them, and re-layouts  6.61 us
    pallas_call x1, Pallas kernels, history_rows(): pl.pallas_call(history_body, grid=(users // BATCH,), in_specs=[pl.BlockSp...  5.64 us
  transfers between devices with their start and end apart: 34, of which 20 were waited for; matrix products, arithmetic and copies ran while one was open for 0% of the time, Pallas kernels for 20%

profile of v2, /device:TPU:70, one launch (start us, length us, event | category | flops | bytes accessed | tf_op | source)
XLA Modules:
  0.0 145.8 jit_solution(8177543005907910571)
XLA Ops:
  0.7 5.6 %history.1.rows = bf16[16,512,256]{2,1,0:T(8,128)(2,1)} custom-call(s32[16,128,256]{2,1,0:T(8,128)} %words.1, s32[16,512]{1,0:T(8,128)} %index.1, f32[1,256]{1,0:T(1,128)} %bitcast.22), custom_call_target="tpu_custom_call" | custom-call | flops 2000000000 | bytes 6000000 | tf_op jit(solution)/shard_map/history/pallas_call | solution.py:70
  7.1 2.1 %collective-permute-start = (bf16[16,16,256]{2,1,0:T(8,128)(2,1)S(1)}, bf16[16,16,256]{2,1,0:T(8,128)(2,1)S(1)}, u32[]{:S(2)}, u32[]{:S(2)}) collective-permute-start(bf16[16,16,256]{2,1,0:T(8,128)(2,1)S(1)} %bitcast.12), channel_id=1, source_target_pairs={{0,2},{2,4},{4,6},{6,8},{8,10},{10,12},{12,14},{14,16},{16,18},{18... | collective-permute-start | bytes 393224 | tf_op jit(solution)/shard_map/ppermute | solution.py:412
  9.3 4.6 %collective-permute-done.4.refs_1_ = bf16[16,16,256]{2,1,0:T(8,128)(2,1)S(1)} collective-permute-done((bf16[16,16,256]{2,1,0:T(8,128)(2,1)S(1)}, bf16[16,16,256]{2,1,0:T(8,128)(2,1)S(1)}, u32[]{:S(2)}, u32[]{:S(2)}) %collective-permute-start.4) | collective-permute-done | bytes 131104 | tf_op jit(solution)/shard_map/ppermute | solution.py:412
  13.9 2.1 %collective-permute-start.5 = (bf16[16,16,256]{2,1,0:T(8,128)(2,1)S(1)}, bf16[16,16,256]{2,1,0:T(8,128)(2,1)S(1)}, u32[]{:S(2)}, u32[]{:S(2)}) collective-permute-start(bf16[16,16,256]{2,1,0:T(8,128)(2,1)S(1)} %collective-permute-done.4.refs_1_), channel_id=1, source_target_pairs={{0,2},{2,4},{4,6},{6,8},{8,10},{10,12},{12,14},{14,16},{16,18},{18... | collective-permute-start | bytes 393224 | tf_op jit(solution)/shard_map/ppermute | solution.py:412
  16.0 6.6 %collective-permute-done.refs_2_ = bf16[16,16,256]{2,1,0:T(8,128)(2,1)S(1)} collective-permute-done((bf16[16,16,256]{2,1,0:T(8,128)(2,1)S(1)}, bf16[16,16,256]{2,1,0:T(8,128)(2,1)S(1)}, u32[]{:S(2)}, u32[]{:S(2)}) %collective-permute-start) | collective-permute-done | bytes 131104 | tf_op jit(solution)/shard_map/ppermute | solution.py:412
  22.6 6.7 %collective-permute-done.5.refs_3_ = bf16[16,16,256]{2,1,0:T(8,128)(2,1)S(1)} collective-permute-done((bf16[16,16,256]{2,1,0:T(8,128)(2,1)S(1)}, bf16[16,16,256]{2,1,0:T(8,128)(2,1)S(1)}, u32[]{:S(2)}, u32[]{:S(2)}) %collective-permute-start.5) | collective-permute-done | bytes 131104 | tf_op jit(solution)/shard_map/ppermute | solution.py:412
  30.7 4.8 %collective-permute-done.6.refs_5_ = bf16[16,16,256]{2,1,0:T(8,128)(2,1)S(1)} collective-permute-done((bf16[16,16,256]{2,1,0:T(8,128)(2,1)S(1)}, bf16[16,16,256]{2,1,0:T(8,128)(2,1)S(1)}, u32[]{:S(2)}, u32[]{:S(2)}) %collective-permute-start.6) | collective-permute-done | bytes 131104 | tf_op jit(solution)/shard_map/ppermute | solution.py:412
  36.9 4.8 %collective-permute-done.7.refs_7_ = bf16[16,16,256]{2,1,0:T(8,128)(2,1)S(1)} collective-permute-done((bf16[16,16,256]{2,1,0:T(8,128)(2,1)S(1)}, bf16[16,16,256]{2,1,0:T(8,128)(2,1)S(1)}, u32[]{:S(2)}, u32[]{:S(2)}) %collective-permute-start.7) | collective-permute-done | bytes 131104 | tf_op jit(solution)/shard_map/ppermute | solution.py:412
  43.1 4.8 %collective-permute-done.8.refs_1_.refs_9_ = bf16[16,16,256]{2,1,0:T(8,128)(2,1)S(1)} collective-permute-done((bf16[16,16,256]{2,1,0:T(8,128)(2,1)S(1)}, bf16[16,16,256]{2,1,0:T(8,128)(2,1)S(1)}, u32[]{:S(2)}, u32[]{:S(2)}) %collective-permute-start.8) | collective-permute-done | bytes 131104 | tf_op jit(solution)/shard_map/ppermute | solution.py:412
  49.3 4.8 %collective-permute-done.10.refs_3_ = bf16[16,16,256]{2,1,0:T(8,128)(2,1)S(1)} collective-permute-done((bf16[16,16,256]{2,1,0:T(8,128)(2,1)S(1)}, bf16[16,16,256]{2,1,0:T(8,128)(2,1)S(1)}, u32[]{:S(2)}, u32[]{:S(2)}) %collective-permute-start.10) | collective-permute-done | bytes 131104 | tf_op jit(solution)/shard_map/ppermute | solution.py:412
  54.1 2.2 %copy-done.5 = bf16[16,512,256]{2,1,0:T(8,128)(2,1)S(1)} copy-done((bf16[16,512,256]{2,1,0:T(8,128)(2,1)S(1)}, bf16[16,512,256]{2,1,0:T(8,128)(2,1)}, u32[]{:S(2)}) %copy-start.5) | copy-done | bytes 4194328
  56.3 2.9 %project.2 = (bf16[16,512,256]{2,1,0:T(8,128)(2,1)S(1)}, bf16[16,288,512]{2,1,0:T(8,128)(2,1)S(1)}) custom-call(bf16[16,512,256]{2,1,0:T(8,128)(2,1)S(1)} %copy-done.5, bf16[256,256]{1,0:T(8,128)(2,1)S(1)} %copy-done.7, bf16[256,256]{1,0:T(8,128)(2,1)S(1)} %bitcast.18), custom_call_target="tpu_custom_call" | custom-call | flops 3000000000 | bytes 12000000 | tf_op jit(solution)/shard_map/project/pallas_call | solution.py:103
  59.2 2.2 %copy-done = bf16[16,288,512]{2,1,0:T(8,128)(2,1)} copy-done((bf16[16,288,512]{2,1,0:T(8,128)(2,1)}, bf16[16,288,512]{2,1,0:T(8,128)(2,1)S(1)}, u32[]{:S(2)}) %copy-start) | copy-done | bytes 4718616
  61.4 2.1 %copy-done.1 = bf16[16,512,256]{2,1,0:T(8,128)(2,1)} copy-done((bf16[16,512,256]{2,1,0:T(8,128)(2,1)}, bf16[16,512,256]{2,1,0:T(8,128)(2,1)S(1)}, u32[]{:S(2)}) %copy-start.1) | copy-done | bytes 4194328
  63.9 5.9 %collective-permute-done.13.refs_6_ = bf16[16,16,256]{2,1,0:T(8,128)(2,1)S(1)} collective-permute-done((bf16[16,16,256]{2,1,0:T(8,128)(2,1)S(1)}, bf16[16,16,256]{2,1,0:T(8,128)(2,1)S(1)}, u32[]{:S(2)}, u32[]{:S(2)}) %collective-permute-start.13) | collective-permute-done | bytes 131104 | tf_op jit(solution)/shard_map/ppermute | solution.py:412
  71.2 4.7 %project.3 = (bf16[16,512,256]{2,1,0:T(8,128)(2,1)S(1)}, bf16[16,288,512]{2,1,0:T(8,128)(2,1)S(1)}) custom-call(bf16[16,512,256]{2,1,0:T(8,128)(2,1)} %collective-permute-done.17.rows, bf16[256,256]{1,0:T(8,128)(2,1)S(1)} %copy-done.7, bf16[256,256]{1,0:T(8,128)(2,1)S(1)} %bitcast.19), custom_call_target="tpu_custom_call" | custom-call | flops 3000000000 | bytes 12000000 | tf_op jit(solution)/shard_map/project/pallas_call | solution.py:103
  77.4 6.7 %attend.9 = (bf16[272,256]{1,0:T(8,128)(2,1)S(1)}, bf16[272,256]{1,0:T(8,128)(2,1)S(1)}, bf16[272,256]{1,0:T(8,128)(2,1)S(1)}, bf16[272,256]{1,0:T(8,128)(2,1)S(1)}) custom-call(s32[3,16]{1,0:T(4,128)S(1)} %concatenate.7.live, bf16[16,16,256]{2,1,0:T(8,128)(2,1)S(1)} %collective-permute-done.3.refs_0_.refs_8_, ...), custom_call_target="tpu_custom_call" | custom-call | flops 6000000000 | bytes 5000000 | tf_op jit(solution)/shard_map/attend/pallas_call | solution.py:240
  84.1 2.1 %collective-permute-start.25 = (bf16[272,256]{1,0:T(8,128)(2,1)S(1)}, bf16[272,256]{1,0:T(8,128)(2,1)S(1)}, u32[]{:S(2)}, u32[]{:S(2)}) collective-permute-start(bf16[272,256]{1,0:T(8,128)(2,1)S(1)} %get-tuple-element.48), channel_id=1, source_target_pairs={{2,0},{4,2},{6,4},{8,6},{10,8},{12,10},{14,12},{16,14},{18,16},{20... | collective-permute-start | bytes 417800 | tf_op jit(solution)/shard_map/ppermute | solution.py:412
  86.2 6.7 %attend.6 = (bf16[272,256]{1,0:T(8,128)(2,1)S(1)}, bf16[272,256]{1,0:T(8,128)(2,1)S(1)}, bf16[272,256]{1,0:T(8,128)(2,1)S(1)}, bf16[272,256]{1,0:T(8,128)(2,1)S(1)}) custom-call(s32[3,16]{1,0:T(4,128)S(1)} %concatenate.7.live, bf16[16,16,256]{2,1,0:T(8,128)(2,1)S(1)} %collective-permute-done.3.refs_0_.refs_8_, ...), custom_call_target="tpu_custom_call" | custom-call | flops 6000000000 | bytes 5000000 | tf_op jit(solution)/shard_map/attend/pallas_call | solution.py:240
  93.8 3.6 %attend.11 = (bf16[272,128]{1,0:T(8,128)(2,1)S(1)}, bf16[272,128]{1,0:T(8,128)(2,1)S(1)}, bf16[272,128]{1,0:T(8,128)(2,1)S(1)}, bf16[272,128]{1,0:T(8,128)(2,1)S(1)}) custom-call(s32[3,16]{1,0:T(4,128)S(1)} %concatenate.7.live, bf16[16,16,256]{2,1,0:T(8,128)(2,1)S(1)} %bitcast.13, bf16[16,16,256]{2,1,0:T(8,128)(2,1)S(1)} %collective-permute-done.4.refs_1_, ...), custom_call_target="tpu_custom_call" | custom-call | flops 3000000000 | bytes 5000000 | tf_op jit(solution)/shard_map/attend/pallas_call | solution.py:240
  98.3 2.5 %collective-permute-start.19 = (bf16[272,256]{1,0:T(8,128)(2,1)S(1)}, bf16[272,256]{1,0:T(8,128)(2,1)S(1)}, u32[]{:S(2)}, u32[]{:S(2)}) collective-permute-start(bf16[272,256]{1,0:T(8,128)(2,1)S(1)} %merge.12), channel_id=1, source_target_pairs={{2,0},{4,2},{6,4},{8,6},{10,8},{12,10},{14,12},{16,14},{18,16},{20... | collective-permute-start | bytes 417800 | tf_op jit(solution)/shard_map/ppermute | solution.py:412
  100.8 3.6 %attend.10 = (bf16[272,128]{1,0:T(8,128)(2,1)S(1)}, bf16[272,128]{1,0:T(8,128)(2,1)S(1)}, bf16[272,128]{1,0:T(8,128)(2,1)S(1)}, bf16[272,128]{1,0:T(8,128)(2,1)S(1)}) custom-call(s32[3,16]{1,0:T(4,128)S(1)} %concatenate.7.live, bf16[16,16,256]{2,1,0:T(8,128)(2,1)S(1)} %bitcast.14, bf16[16,16,256]{2,1,0:T(8,128)(2,1)S(1)} %collective-permute-done.4.refs_1_, ...), custom_call_target="tpu_custom_call" | custom-call | flops 3000000000 | bytes 5000000 | tf_op jit(solution)/shard_map/attend/pallas_call | solution.py:240
  104.5 1.9 %collective-permute-start.27 = (bf16[272,256]{1,0:T(8,128)(2,1)S(1)}, bf16[272,256]{1,0:T(8,128)(2,1)S(1)}, u32[]{:S(2)}, u32[]{:S(2)}) collective-permute-start(bf16[272,256]{1,0:T(8,128)(2,1)S(1)} %merge.19), channel_id=1, source_target_pairs={{2,0},{4,2},{6,4},{8,6},{10,8},{12,10},{14,12},{16,14},{18,16},{20... | collective-permute-start | bytes 417800 | tf_op jit(solution)/shard_map/ppermute | solution.py:412
  107.4 3.6 %attend.8 = (bf16[272,128]{1,0:T(8,128)(2,1)S(1)}, bf16[272,128]{1,0:T(8,128)(2,1)S(1)}, bf16[272,128]{1,0:T(8,128)(2,1)S(1)}, bf16[272,128]{1,0:T(8,128)(2,1)S(1)}) custom-call(s32[3,16]{1,0:T(4,128)S(1)} %concatenate.7.live, bf16[16,16,256]{2,1,0:T(8,128)(2,1)S(1)} %bitcast.15, bf16[16,16,256]{2,1,0:T(8,128)(2,1)S(1)} %collective-permute-done.4.refs_1_, ...), custom_call_target="tpu_custom_call" | custom-call | flops 3000000000 | bytes 5000000 | tf_op jit(solution)/shard_map/attend/pallas_call | solution.py:240
  111.0 1.8 %collective-permute-start.28 = (bf16[272,256]{1,0:T(8,128)(2,1)S(1)}, bf16[272,256]{1,0:T(8,128)(2,1)S(1)}, u32[]{:S(2)}, u32[]{:S(2)}) collective-permute-start(bf16[272,256]{1,0:T(8,128)(2,1)S(1)} %merge.20), channel_id=1, source_target_pairs={{2,0},{4,2},{6,4},{8,6},{10,8},{12,10},{14,12},{16,14},{18,16},{20... | collective-permute-start | bytes 417800 | tf_op jit(solution)/shard_map/ppermute | solution.py:412
  114.4 3.6 %attend.7 = (bf16[272,128]{1,0:T(8,128)(2,1)S(1)}, bf16[272,128]{1,0:T(8,128)(2,1)S(1)}, bf16[272,128]{1,0:T(8,128)(2,1)S(1)}, bf16[272,128]{1,0:T(8,128)(2,1)S(1)}) custom-call(s32[3,16]{1,0:T(4,128)S(1)} %concatenate.7.live, bf16[16,16,256]{2,1,0:T(8,128)(2,1)S(1)} %bitcast.16, bf16[16,16,256]{2,1,0:T(8,128)(2,1)S(1)} %collective-permute-done.4.refs_1_, ...), custom_call_target="tpu_custom_call" | custom-call | flops 3000000000 | bytes 5000000 | tf_op jit(solution)/shard_map/attend/pallas_call | solution.py:240
  120.9 2.4 %collective-permute-done.29.came = bf16[272,256]{1,0:T(8,128)(2,1)S(1)} collective-permute-done((bf16[272,256]{1,0:T(8,128)(2,1)S(1)}, bf16[272,256]{1,0:T(8,128)(2,1)S(1)}, u32[]{:S(2)}, u32[]{:S(2)}) %collective-permute-start.29) | collective-permute-done | bytes 139296 | tf_op jit(solution)/shard_map/ppermute | solution.py:412
  123.3 2.4 %collective-permute-start.30 = (bf16[272,256]{1,0:T(8,128)(2,1)S(1)}, bf16[272,256]{1,0:T(8,128)(2,1)S(1)}, u32[]{:S(2)}, u32[]{:S(2)}) collective-permute-start(bf16[272,256]{1,0:T(8,128)(2,1)S(1)} %merge.22), channel_id=1, source_target_pairs={{2,0},{4,2},{6,4},{8,6},{10,8},{12,10},{14,12},{16,14},{18,16},{20... | collective-permute-start | bytes 417800 | tf_op jit(solution)/shard_map/ppermute | solution.py:412
  128.6 3.6 %collective-permute-start.31 = (bf16[272,256]{1,0:T(8,128)(2,1)S(1)}, bf16[272,256]{1,0:T(8,128)(2,1)S(1)}, u32[]{:S(2)}, u32[]{:S(2)}) collective-permute-start(bf16[272,256]{1,0:T(8,128)(2,1)S(1)} %merge.23), channel_id=1, source_target_pairs={{2,0},{4,2},{6,4},{8,6},{10,8},{12,10},{14,12},{16,14},{18,16},{20... | collective-permute-start | bytes 417800 | tf_op jit(solution)/shard_map/ppermute | solution.py:412
  134.8 2.7 %collective-permute-done.24.refs_0_ = bf16[272,256]{1,0:T(8,128)(2,1)S(1)} collective-permute-done((bf16[272,256]{1,0:T(8,128)(2,1)S(1)}, bf16[272,256]{1,0:T(8,128)(2,1)S(1)}, u32[]{:S(2)}, u32[]{:S(2)}) %collective-permute-start.24) | collective-permute-done | bytes 139296 | tf_op jit(solution)/shard_map/ppermute | solution.py:412
  138.7 5.6 %collective-permute-done.33.b = bf16[272,256]{1,0:T(8,128)(2,1)S(1)} collective-permute-done((bf16[272,256]{1,0:T(8,128)(2,1)S(1)}, bf16[272,256]{1,0:T(8,128)(2,1)S(1)}, u32[]{:S(2)}, u32[]{:S(2)}) %collective-permute-start.33) | collective-permute-done | bytes 139296 | tf_op jit(solution)/shard_map/ppermute | solution.py:412
  144.3 1.5 %finish.1 = (bf16[256,256]{1,0:T(8,128)(2,1)}, f32[16,16]{1,0:T(8,128)}) custom-call(bf16[272,256]{1,0:T(8,128)(2,1)S(1)} %collective-permute-done.32.a, bf16[272,256]{1,0:T(8,128)(2,1)S(1)} %collective-permute-done.33.b, bf16[256,256]{1,0:T(8,128)(2,1)S(1)} %copy-done.8, f32[1,256]{1,0:T(1,128)S(1)} %bitcast.21, bf16[256,512]{1,0:T(8,128)(2,1)S(1)} %copy-done.6, ...), custom_call_target="tpu_custom_call" | custom-call | flops 200000000 | bytes 1000000 | tf_op jit(solution)/shard_map/finish/pallas_call | solution.py:356
  (106 shorter events, 23.5 us)
Async XLA Ops:
  6.3 64.9 %collective-permute-start.17 = (bf16[16,512,256]{2,1,0:T(8,128)(2,1)}, bf16[16,512,256]{2,1,0:T(8,128)(2,1)}, u32[]{:S(2)}, u32[]{:S(2)}) collective-permute-start(bf16[16,512,256]{2,1,0:T(8,128)(2,1)} %history.1.rows), channel_id=1, source_target_pairs={{0,1},{1,0},{2,3},{3,2},{4,5},{5,4},{6,7},{7,6},{8,9},{9,8},{10,11... | collective-permute-start | bytes 12582920 | tf_op jit(solution)/shard_map/ppermute | solution.py:412
  6.5 7.3 %collective-permute-start.4 = (bf16[16,16,256]{2,1,0:T(8,128)(2,1)S(1)}, bf16[16,16,256]{2,1,0:T(8,128)(2,1)S(1)}, u32[]{:S(2)}, u32[]{:S(2)}) collective-permute-start(bf16[16,16,256]{2,1,0:T(8,128)(2,1)S(1)} %bitcast.11), channel_id=1, source_target_pairs={{0,1},{1,0},{2,3},{3,2},{4,5},{5,4},{6,7},{7,6},{8,9},{9,8},{10,11... | collective-permute-start | bytes 393224 | tf_op jit(solution)/shard_map/ppermute | solution.py:412
  7.1 15.5 %collective-permute-start = (bf16[16,16,256]{2,1,0:T(8,128)(2,1)S(1)}, bf16[16,16,256]{2,1,0:T(8,128)(2,1)S(1)}, u32[]{:S(2)}, u32[]{:S(2)}) collective-permute-start(bf16[16,16,256]{2,1,0:T(8,128)(2,1)S(1)} %bitcast.12), channel_id=1, source_target_pairs={{0,2},{2,4},{4,6},{6,8},{8,10},{10,12},{12,14},{14,16},{16,18},{18... | collective-permute-start | bytes 393224 | tf_op jit(solution)/shard_map/ppermute | solution.py:412
  13.9 15.5 %collective-permute-start.5 = (bf16[16,16,256]{2,1,0:T(8,128)(2,1)S(1)}, bf16[16,16,256]{2,1,0:T(8,128)(2,1)S(1)}, u32[]{:S(2)}, u32[]{:S(2)}) collective-permute-start(bf16[16,16,256]{2,1,0:T(8,128)(2,1)S(1)} %collective-permute-done.4.refs_1_), channel_id=1, source_target_pairs={{0,2},{2,4},{4,6},{6,8},{8,10},{10,12},{12,14},{14,16},{16,18},{18... | collective-permute-start | bytes 393224 | tf_op jit(solution)/shard_map/ppermute | solution.py:412
  22.6 8.1 %collective-permute-start.1 = (bf16[16,16,256]{2,1,0:T(8,128)(2,1)S(1)}, bf16[16,16,256]{2,1,0:T(8,128)(2,1)S(1)}, u32[]{:S(2)}, u32[]{:S(2)}) collective-permute-start(bf16[16,16,256]{2,1,0:T(8,128)(2,1)S(1)} %collective-permute-done.refs_2_), channel_id=1, source_target_pairs={{0,2},{2,4},{4,6},{6,8},{8,10},{10,12},{12,14},{14,16},{16,18},{18... | collective-permute-start | bytes 393224 | tf_op jit(solution)/shard_map/ppermute | solution.py:412
  29.3 6.2 %collective-permute-start.6 = (bf16[16,16,256]{2,1,0:T(8,128)(2,1)S(1)}, bf16[16,16,256]{2,1,0:T(8,128)(2,1)S(1)}, u32[]{:S(2)}, u32[]{:S(2)}) collective-permute-start(bf16[16,16,256]{2,1,0:T(8,128)(2,1)S(1)} %collective-permute-done.5.refs_3_), channel_id=1, source_target_pairs={{0,2},{2,4},{4,6},{6,8},{8,10},{10,12},{12,14},{14,16},{16,18},{18... | collective-permute-start | bytes 393224 | tf_op jit(solution)/shard_map/ppermute | solution.py:412
  30.7 6.2 %collective-permute-start.2 = (bf16[16,16,256]{2,1,0:T(8,128)(2,1)S(1)}, bf16[16,16,256]{2,1,0:T(8,128)(2,1)S(1)}, u32[]{:S(2)}, u32[]{:S(2)}) collective-permute-start(bf16[16,16,256]{2,1,0:T(8,128)(2,1)S(1)} %collective-permute-done.1.refs_4_), channel_id=1, source_target_pairs={{0,2},{2,4},{4,6},{6,8},{8,10},{10,12},{12,14},{14,16},{16,18},{18... | collective-permute-start | bytes 393224 | tf_op jit(solution)/shard_map/ppermute | solution.py:412
  35.5 6.2 %collective-permute-start.7 = (bf16[16,16,256]{2,1,0:T(8,128)(2,1)S(1)}, bf16[16,16,256]{2,1,0:T(8,128)(2,1)S(1)}, u32[]{:S(2)}, u32[]{:S(2)}) collective-permute-start(bf16[16,16,256]{2,1,0:T(8,128)(2,1)S(1)} %collective-permute-done.6.refs_5_), channel_id=1, source_target_pairs={{0,2},{2,4},{4,6},{6,8},{8,10},{10,12},{12,14},{14,16},{16,18},{18... | collective-permute-start | bytes 393224 | tf_op jit(solution)/shard_map/ppermute | solution.py:412
  36.9 6.2 %collective-permute-start.3 = (bf16[16,16,256]{2,1,0:T(8,128)(2,1)S(1)}, bf16[16,16,256]{2,1,0:T(8,128)(2,1)S(1)}, u32[]{:S(2)}, u32[]{:S(2)}) collective-permute-start(bf16[16,16,256]{2,1,0:T(8,128)(2,1)S(1)} %collective-permute-done.2.refs_6_), channel_id=1, source_target_pairs={{0,2},{2,4},{4,6},{6,8},{8,10},{10,12},{12,14},{14,16},{16,18},{18... | collective-permute-start | bytes 393224 | tf_op jit(solution)/shard_map/ppermute | solution.py:412
  41.7 6.2 %collective-permute-start.8 = (bf16[16,16,256]{2,1,0:T(8,128)(2,1)S(1)}, bf16[16,16,256]{2,1,0:T(8,128)(2,1)S(1)}, u32[]{:S(2)}, u32[]{:S(2)}) collective-permute-start(bf16[16,16,256]{2,1,0:T(8,128)(2,1)S(1)} %collective-permute-done.7.refs_7_), channel_id=1, source_target_pairs={{0,2},{2,4},{4,6},{6,8},{8,10},{10,12},{12,14},{14,16},{16,18},{18... | collective-permute-start | bytes 393224 | tf_op jit(solution)/shard_map/ppermute | solution.py:412
  43.1 6.2 %collective-permute-start.9 = (bf16[16,16,256]{2,1,0:T(8,128)(2,1)S(1)}, bf16[16,16,256]{2,1,0:T(8,128)(2,1)S(1)}, u32[]{:S(2)}, u32[]{:S(2)}) collective-permute-start(bf16[16,16,256]{2,1,0:T(8,128)(2,1)S(1)} %collective-permute-done.3.refs_0_.refs_8_), channel_id=1, source_target_pairs={{0,2},{2,4},{4,6},{6,8},{8,10},{10,12},{12,14},{14,16},{16,18},{18... | collective-permute-start | bytes 393224 | tf_op jit(solution)/shard_map/ppermute | solution.py:412
  47.9 6.2 %collective-permute-start.10 = (bf16[16,16,256]{2,1,0:T(8,128)(2,1)S(1)}, bf16[16,16,256]{2,1,0:T(8,128)(2,1)S(1)}, u32[]{:S(2)}, u32[]{:S(2)}) collective-permute-start(bf16[16,16,256]{2,1,0:T(8,128)(2,1)S(1)} %collective-permute-done.8.refs_1_.refs_9_), channel_id=1, source_target_pairs={{0,2},{2,4},{4,6},{6,8},{8,10},{10,12},{12,14},{14,16},{16,18},{18... | collective-permute-start | bytes 393224 | tf_op jit(solution)/shard_map/ppermute | solution.py:412
  49.3 14.2 %collective-permute-start.11 = (bf16[16,16,256]{2,1,0:T(8,128)(2,1)S(1)}, bf16[16,16,256]{2,1,0:T(8,128)(2,1)S(1)}, u32[]{:S(2)}, u32[]{:S(2)}) collective-permute-start(bf16[16,16,256]{2,1,0:T(8,128)(2,1)S(1)} %collective-permute-done.9.refs_2_), channel_id=1, source_target_pairs={{0,2},{2,4},{4,6},{6,8},{8,10},{10,12},{12,14},{14,16},{16,18},{18... | collective-permute-start | bytes 393224 | tf_op jit(solution)/shard_map/ppermute | solution.py:412
  54.1 9.5 %collective-permute-start.12 = (bf16[16,16,256]{2,1,0:T(8,128)(2,1)S(1)}, bf16[16,16,256]{2,1,0:T(8,128)(2,1)S(1)}, u32[]{:S(2)}, u32[]{:S(2)}) collective-permute-start(bf16[16,16,256]{2,1,0:T(8,128)(2,1)S(1)} %collective-permute-done.10.refs_3_), channel_id=1, source_target_pairs={{0,2},{2,4},{4,6},{6,8},{8,10},{10,12},{12,14},{14,16},{16,18},{18... | collective-permute-start | bytes 393224 | tf_op jit(solution)/shard_map/ppermute | solution.py:412
  63.5 6.2 %collective-permute-start.13 = (bf16[16,16,256]{2,1,0:T(8,128)(2,1)S(1)}, bf16[16,16,256]{2,1,0:T(8,128)(2,1)S(1)}, u32[]{:S(2)}, u32[]{:S(2)}) collective-permute-start(bf16[16,16,256]{2,1,0:T(8,128)(2,1)S(1)} %collective-permute-done.11.refs_4_), channel_id=1, source_target_pairs={{0,2},{2,4},{4,6},{6,8},{8,10},{10,12},{12,14},{14,16},{16,18},{18... | collective-permute-start | bytes 393224 | tf_op jit(solution)/shard_map/ppermute | solution.py:412
  63.6 7.6 %collective-permute-start.14 = (bf16[16,16,256]{2,1,0:T(8,128)(2,1)S(1)}, bf16[16,16,256]{2,1,0:T(8,128)(2,1)S(1)}, u32[]{:S(2)}, u32[]{:S(2)}) collective-permute-start(bf16[16,16,256]{2,1,0:T(8,128)(2,1)S(1)} %collective-permute-done.12.refs_5_), channel_id=1, source_target_pairs={{0,2},{2,4},{4,6},{6,8},{8,10},{10,12},{12,14},{14,16},{16,18},{18... | collective-permute-start | bytes 393224 | tf_op jit(solution)/shard_map/ppermute | solution.py:412
  69.8 6.2 %collective-permute-start.15 = (bf16[16,16,256]{2,1,0:T(8,128)(2,1)S(1)}, bf16[16,16,256]{2,1,0:T(8,128)(2,1)S(1)}, u32[]{:S(2)}, u32[]{:S(2)}) collective-permute-start(bf16[16,16,256]{2,1,0:T(8,128)(2,1)S(1)} %collective-permute-done.13.refs_6_), channel_id=1, source_target_pairs={{0,2},{2,4},{4,6},{6,8},{8,10},{10,12},{12,14},{14,16},{16,18},{18... | collective-permute-start | bytes 393224 | tf_op jit(solution)/shard_map/ppermute | solution.py:412
  71.2 6.2 %collective-permute-start.16 = (bf16[16,16,256]{2,1,0:T(8,128)(2,1)S(1)}, bf16[16,16,256]{2,1,0:T(8,128)(2,1)S(1)}, u32[]{:S(2)}, u32[]{:S(2)}) collective-permute-start(bf16[16,16,256]{2,1,0:T(8,128)(2,1)S(1)} %collective-permute-done.14.refs_7_), channel_id=1, source_target_pairs={{0,2},{2,4},{4,6},{6,8},{8,10},{10,12},{12,14},{14,16},{16,18},{18... | collective-permute-start | bytes 393224 | tf_op jit(solution)/shard_map/ppermute | solution.py:412
  84.1 13.3 %collective-permute-start.25 = (bf16[272,256]{1,0:T(8,128)(2,1)S(1)}, bf16[272,256]{1,0:T(8,128)(2,1)S(1)}, u32[]{:S(2)}, u32[]{:S(2)}) collective-permute-start(bf16[272,256]{1,0:T(8,128)(2,1)S(1)} %get-tuple-element.48), channel_id=1, source_target_pairs={{2,0},{4,2},{6,4},{8,6},{10,8},{12,10},{14,12},{16,14},{18,16},{20... | collective-permute-start | bytes 417800 | tf_op jit(solution)/shard_map/ppermute | solution.py:412
  92.9 5.3 %collective-permute-start.18 = (bf16[272,256]{1,0:T(8,128)(2,1)S(1)}, bf16[272,256]{1,0:T(8,128)(2,1)S(1)}, u32[]{:S(2)}, u32[]{:S(2)}) collective-permute-start(bf16[272,256]{1,0:T(8,128)(2,1)S(1)} %get-tuple-element.38), channel_id=1, source_target_pairs={{2,0},{4,2},{6,4},{8,6},{10,8},{12,10},{14,12},{16,14},{18,16},{20... | collective-permute-start | bytes 417800 | tf_op jit(solution)/shard_map/ppermute | solution.py:412
  97.5 6.9 %collective-permute-start.26 = (bf16[272,256]{1,0:T(8,128)(2,1)S(1)}, bf16[272,256]{1,0:T(8,128)(2,1)S(1)}, u32[]{:S(2)}, u32[]{:S(2)}) collective-permute-start(bf16[272,256]{1,0:T(8,128)(2,1)S(1)} %merge.18), channel_id=1, source_target_pairs={{2,0},{4,2},{6,4},{8,6},{10,8},{12,10},{14,12},{16,14},{18,16},{20... | collective-permute-start | bytes 417800 | tf_op jit(solution)/shard_map/ppermute | solution.py:412
  98.3 8.1 %collective-permute-start.19 = (bf16[272,256]{1,0:T(8,128)(2,1)S(1)}, bf16[272,256]{1,0:T(8,128)(2,1)S(1)}, u32[]{:S(2)}, u32[]{:S(2)}) collective-permute-start(bf16[272,256]{1,0:T(8,128)(2,1)S(1)} %merge.12), channel_id=1, source_target_pairs={{2,0},{4,2},{6,4},{8,6},{10,8},{12,10},{14,12},{16,14},{18,16},{20... | collective-permute-start | bytes 417800 | tf_op jit(solution)/shard_map/ppermute | solution.py:412
  104.5 6.5 %collective-permute-start.27 = (bf16[272,256]{1,0:T(8,128)(2,1)S(1)}, bf16[272,256]{1,0:T(8,128)(2,1)S(1)}, u32[]{:S(2)}, u32[]{:S(2)}) collective-permute-start(bf16[272,256]{1,0:T(8,128)(2,1)S(1)} %merge.19), channel_id=1, source_target_pairs={{2,0},{4,2},{6,4},{8,6},{10,8},{12,10},{14,12},{16,14},{18,16},{20... | collective-permute-start | bytes 417800 | tf_op jit(solution)/shard_map/ppermute | solution.py:412
  106.5 6.4 %collective-permute-start.20 = (bf16[272,256]{1,0:T(8,128)(2,1)S(1)}, bf16[272,256]{1,0:T(8,128)(2,1)S(1)}, u32[]{:S(2)}, u32[]{:S(2)}) collective-permute-start(bf16[272,256]{1,0:T(8,128)(2,1)S(1)} %merge.13), channel_id=1, source_target_pairs={{2,0},{4,2},{6,4},{8,6},{10,8},{12,10},{14,12},{16,14},{18,16},{20... | collective-permute-start | bytes 417800 | tf_op jit(solution)/shard_map/ppermute | solution.py:412
  111.0 6.9 %collective-permute-start.28 = (bf16[272,256]{1,0:T(8,128)(2,1)S(1)}, bf16[272,256]{1,0:T(8,128)(2,1)S(1)}, u32[]{:S(2)}, u32[]{:S(2)}) collective-permute-start(bf16[272,256]{1,0:T(8,128)(2,1)S(1)} %merge.20), channel_id=1, source_target_pairs={{2,0},{4,2},{6,4},{8,6},{10,8},{12,10},{14,12},{16,14},{18,16},{20... | collective-permute-start | bytes 417800 | tf_op jit(solution)/shard_map/ppermute | solution.py:412
  113.0 6.3 %collective-permute-start.21 = (bf16[272,256]{1,0:T(8,128)(2,1)S(1)}, bf16[272,256]{1,0:T(8,128)(2,1)S(1)}, u32[]{:S(2)}, u32[]{:S(2)}) collective-permute-start(bf16[272,256]{1,0:T(8,128)(2,1)S(1)} %merge.14), channel_id=1, source_target_pairs={{2,0},{4,2},{6,4},{8,6},{10,8},{12,10},{14,12},{16,14},{18,16},{20... | collective-permute-start | bytes 417800 | tf_op jit(solution)/shard_map/ppermute | solution.py:412
  118.1 5.2 %collective-permute-start.29 = (bf16[272,256]{1,0:T(8,128)(2,1)S(1)}, bf16[272,256]{1,0:T(8,128)(2,1)S(1)}, u32[]{:S(2)}, u32[]{:S(2)}) collective-permute-start(bf16[272,256]{1,0:T(8,128)(2,1)S(1)} %merge.21), channel_id=1, source_target_pairs={{2,0},{4,2},{6,4},{8,6},{10,8},{12,10},{14,12},{16,14},{18,16},{20... | collective-permute-start | bytes 417800 | tf_op jit(solution)/shard_map/ppermute | solution.py:412
  119.4 6.4 %collective-permute-start.22 = (bf16[272,256]{1,0:T(8,128)(2,1)S(1)}, bf16[272,256]{1,0:T(8,128)(2,1)S(1)}, u32[]{:S(2)}, u32[]{:S(2)}) collective-permute-start(bf16[272,256]{1,0:T(8,128)(2,1)S(1)} %merge.15), channel_id=1, source_target_pairs={{2,0},{4,2},{6,4},{8,6},{10,8},{12,10},{14,12},{16,14},{18,16},{20... | collective-permute-start | bytes 417800 | tf_op jit(solution)/shard_map/ppermute | solution.py:412
  123.3 5.2 %collective-permute-start.30 = (bf16[272,256]{1,0:T(8,128)(2,1)S(1)}, bf16[272,256]{1,0:T(8,128)(2,1)S(1)}, u32[]{:S(2)}, u32[]{:S(2)}) collective-permute-start(bf16[272,256]{1,0:T(8,128)(2,1)S(1)} %merge.22), channel_id=1, source_target_pairs={{2,0},{4,2},{6,4},{8,6},{10,8},{12,10},{14,12},{16,14},{18,16},{20... | collective-permute-start | bytes 417800 | tf_op jit(solution)/shard_map/ppermute | solution.py:412
  125.9 6.4 %collective-permute-start.23 = (bf16[272,256]{1,0:T(8,128)(2,1)S(1)}, bf16[272,256]{1,0:T(8,128)(2,1)S(1)}, u32[]{:S(2)}, u32[]{:S(2)}) collective-permute-start(bf16[272,256]{1,0:T(8,128)(2,1)S(1)} %merge.16), channel_id=1, source_target_pairs={{2,0},{4,2},{6,4},{8,6},{10,8},{12,10},{14,12},{16,14},{18,16},{20... | collective-permute-start | bytes 417800 | tf_op jit(solution)/shard_map/ppermute | solution.py:412
  128.6 6.2 %collective-permute-start.31 = (bf16[272,256]{1,0:T(8,128)(2,1)S(1)}, bf16[272,256]{1,0:T(8,128)(2,1)S(1)}, u32[]{:S(2)}, u32[]{:S(2)}) collective-permute-start(bf16[272,256]{1,0:T(8,128)(2,1)S(1)} %merge.23), channel_id=1, source_target_pairs={{2,0},{4,2},{6,4},{8,6},{10,8},{12,10},{14,12},{16,14},{18,16},{20... | collective-permute-start | bytes 417800 | tf_op jit(solution)/shard_map/ppermute | solution.py:412
  138.6 5.7 %collective-permute-start.33 = (bf16[272,256]{1,0:T(8,128)(2,1)S(1)}, bf16[272,256]{1,0:T(8,128)(2,1)S(1)}, u32[]{:S(2)}, u32[]{:S(2)}) collective-permute-start(bf16[272,256]{1,0:T(8,128)(2,1)S(1)} %get-tuple-element.63), channel_id=1, source_target_pairs={{0,1},{2,3},{4,5},{6,7},{8,9},{10,11},{12,13},{14,15},{16,17},{18,... | collective-permute-start | bytes 417800 | tf_op jit(solution)/shard_map/ppermute | solution.py:412
  (18 other events, 323.7 us)

commit v3 on v2

--- a/solution.py
+++ b/solution.py
@@ -389,6 +389,7 @@
     ring = [(near(d, 0), near(d + 1, 0)) for d in range(chips)] + [(near(d, 1), near(d - 1, 1)) for d in range(chips)]
     stay = [(near(d, 0), near(d, 0)) for d in range(chips)] + [(near(d, 1), near(d - 1, 1)) for d in range(chips)]
     cross = [(near(d, 1), near(d, 0)) for d in range(chips)] + [(near(d, 0), near(d - 1, 1)) for d in range(chips)]
+    tail = [(near(d, 1), near(d - 1, 1)) for d in range(chips)]
     swap = [(near(d, c), near(d, 1 - c)) for d in range(chips) for c in range(2)]
     back = lambda pairs: [(b, a) for a, b in pairs]
 
@@ -418,9 +419,9 @@
 
         mine = query_rows(candidates.reshape(users * cand, width), query_weight).reshape(users, cand, width)
         hops = [mine, send(mine, swap)]
-        for _ in range(1, slots + 1):
+        for hop in range(1, slots + 1):
             for _ in range(2):
-                hops.append(send(hops[-2], ring))
+                hops.append(send(hops[-2], ring if hop < slots else tail))
 
         value_wt = value_weight.T
         own = history_rows(codes, scale_index, scale_table)

time: 146 us -> 146 us (level)
  waiting for transfers between devices: 64 us -> 62.5 us
    ppermute x34, waiting for transfers between devices: 64 us -> 62.5 us  [on_device(): send = lambda array, pairs: lax.ppermute(array, 'seq', pairs)]
  transfers between devices with their start and end apart: 34 -> 34, of which waited for: 20 -> 19; matrix products, arithmetic and copies ran while one was open for 0% -> 0% of each run, Pallas kernels for 20% -> 20%
where the time goes in v3:
time: 146 us; the launch traced here: 145 us
  waiting for transfers between devices  62.5 us (43%)
  Pallas kernels  44 us (30%)
  starting transfers between devices  30.7 us (21%)
  local copies, waits for them, and re-layouts  6.62 us (5%)
    ppermute x34, waiting for transfers between devices, on_device(): send = lambda array, pairs: lax.ppermute(array, 'seq', pairs)  62.5 us
    ppermute x34, starting transfers between devices, on_device(): send = lambda array, pairs: lax.ppermute(array, 'seq', pairs)  30.7 us
    pallas_call x6, Pallas kernels, attend(): pl.pallas_call(functools.partial(attend_body, base), grid_spec=pltpu.Pref...  27.7 us
    pallas_call x2, Pallas kernels, project(): pl.pallas_call(project_body, grid=(users // BATCH,), in_specs=[pl.BlockSp...  7.62 us
    unnamed x33, local copies, waits for them, and re-layouts  6.61 us
    pallas_call x1, Pallas kernels, history_rows(): pl.pallas_call(history_body, grid=(users // BATCH,), in_specs=[pl.BlockSp...  5.64 us
  transfers between devices with their start and end apart: 34, of which 19 were waited for; matrix products, arithmetic and copies ran while one was open for 0% of the time, Pallas kernels for 20%

profile of v3, /device:TPU:70, one launch (start us, length us, event | category | flops | bytes accessed | tf_op | source)
XLA Modules:
  0.0 145.3 jit_solution(7444995606629472747)
XLA Ops:
  0.7 5.6 %history.1.rows = bf16[16,512,256]{2,1,0:T(8,128)(2,1)} custom-call(s32[16,128,256]{2,1,0:T(8,128)} %words.1, s32[16,512]{1,0:T(8,128)} %index.1, f32[1,256]{1,0:T(1,128)} %bitcast.22), custom_call_target="tpu_custom_call" | custom-call | flops 2000000000 | bytes 6000000 | tf_op jit(solution)/shard_map/history/pallas_call | solution.py:70
  7.1 2.1 %collective-permute-start = (bf16[16,16,256]{2,1,0:T(8,128)(2,1)S(1)}, bf16[16,16,256]{2,1,0:T(8,128)(2,1)S(1)}, u32[]{:S(2)}, u32[]{:S(2)}) collective-permute-start(bf16[16,16,256]{2,1,0:T(8,128)(2,1)S(1)} %bitcast.12), channel_id=1, source_target_pairs={{0,2},{2,4},{4,6},{6,8},{8,10},{10,12},{12,14},{14,16},{16,18},{18... | collective-permute-start | bytes 393224 | tf_op jit(solution)/shard_map/ppermute | solution.py:413
  9.3 4.6 %collective-permute-done.4.refs_1_ = bf16[16,16,256]{2,1,0:T(8,128)(2,1)S(1)} collective-permute-done((bf16[16,16,256]{2,1,0:T(8,128)(2,1)S(1)}, bf16[16,16,256]{2,1,0:T(8,128)(2,1)S(1)}, u32[]{:S(2)}, u32[]{:S(2)}) %collective-permute-start.4) | collective-permute-done | bytes 131104 | tf_op jit(solution)/shard_map/ppermute | solution.py:413
  13.9 2.1 %collective-permute-start.5 = (bf16[16,16,256]{2,1,0:T(8,128)(2,1)S(1)}, bf16[16,16,256]{2,1,0:T(8,128)(2,1)S(1)}, u32[]{:S(2)}, u32[]{:S(2)}) collective-permute-start(bf16[16,16,256]{2,1,0:T(8,128)(2,1)S(1)} %collective-permute-done.4.refs_1_), channel_id=1, source_target_pairs={{0,2},{2,4},{4,6},{6,8},{8,10},{10,12},{12,14},{14,16},{16,18},{18... | collective-permute-start | bytes 393224 | tf_op jit(solution)/shard_map/ppermute | solution.py:413
  16.0 6.6 %collective-permute-done.refs_2_ = bf16[16,16,256]{2,1,0:T(8,128)(2,1)S(1)} collective-permute-done((bf16[16,16,256]{2,1,0:T(8,128)(2,1)S(1)}, bf16[16,16,256]{2,1,0:T(8,128)(2,1)S(1)}, u32[]{:S(2)}, u32[]{:S(2)}) %collective-permute-start) | collective-permute-done | bytes 131104 | tf_op jit(solution)/shard_map/ppermute | solution.py:413
  22.6 6.7 %collective-permute-done.5.refs_3_ = bf16[16,16,256]{2,1,0:T(8,128)(2,1)S(1)} collective-permute-done((bf16[16,16,256]{2,1,0:T(8,128)(2,1)S(1)}, bf16[16,16,256]{2,1,0:T(8,128)(2,1)S(1)}, u32[]{:S(2)}, u32[]{:S(2)}) %collective-permute-start.5) | collective-permute-done | bytes 131104 | tf_op jit(solution)/shard_map/ppermute | solution.py:413
  30.7 4.8 %collective-permute-done.6.refs_5_ = bf16[16,16,256]{2,1,0:T(8,128)(2,1)S(1)} collective-permute-done((bf16[16,16,256]{2,1,0:T(8,128)(2,1)S(1)}, bf16[16,16,256]{2,1,0:T(8,128)(2,1)S(1)}, u32[]{:S(2)}, u32[]{:S(2)}) %collective-permute-start.6) | collective-permute-done | bytes 131104 | tf_op jit(solution)/shard_map/ppermute | solution.py:413
  36.9 4.8 %collective-permute-done.7.refs_7_ = bf16[16,16,256]{2,1,0:T(8,128)(2,1)S(1)} collective-permute-done((bf16[16,16,256]{2,1,0:T(8,128)(2,1)S(1)}, bf16[16,16,256]{2,1,0:T(8,128)(2,1)S(1)}, u32[]{:S(2)}, u32[]{:S(2)}) %collective-permute-start.7) | collective-permute-done | bytes 131104 | tf_op jit(solution)/shard_map/ppermute | solution.py:413
  43.1 4.8 %collective-permute-done.8.refs_1_.refs_9_ = bf16[16,16,256]{2,1,0:T(8,128)(2,1)S(1)} collective-permute-done((bf16[16,16,256]{2,1,0:T(8,128)(2,1)S(1)}, bf16[16,16,256]{2,1,0:T(8,128)(2,1)S(1)}, u32[]{:S(2)}, u32[]{:S(2)}) %collective-permute-start.8) | collective-permute-done | bytes 131104 | tf_op jit(solution)/shard_map/ppermute | solution.py:413
  49.3 4.8 %collective-permute-done.10.refs_3_ = bf16[16,16,256]{2,1,0:T(8,128)(2,1)S(1)} collective-permute-done((bf16[16,16,256]{2,1,0:T(8,128)(2,1)S(1)}, bf16[16,16,256]{2,1,0:T(8,128)(2,1)S(1)}, u32[]{:S(2)}, u32[]{:S(2)}) %collective-permute-start.10) | collective-permute-done | bytes 131104 | tf_op jit(solution)/shard_map/ppermute | solution.py:413
  54.1 2.2 %copy-done.5 = bf16[16,512,256]{2,1,0:T(8,128)(2,1)S(1)} copy-done((bf16[16,512,256]{2,1,0:T(8,128)(2,1)S(1)}, bf16[16,512,256]{2,1,0:T(8,128)(2,1)}, u32[]{:S(2)}) %copy-start.5) | copy-done | bytes 4194328
  56.3 2.9 %project.2 = (bf16[16,512,256]{2,1,0:T(8,128)(2,1)S(1)}, bf16[16,288,512]{2,1,0:T(8,128)(2,1)S(1)}) custom-call(bf16[16,512,256]{2,1,0:T(8,128)(2,1)S(1)} %copy-done.5, bf16[256,256]{1,0:T(8,128)(2,1)S(1)} %copy-done.7, bf16[256,256]{1,0:T(8,128)(2,1)S(1)} %bitcast.18), custom_call_target="tpu_custom_call" | custom-call | flops 3000000000 | bytes 12000000 | tf_op jit(solution)/shard_map/project/pallas_call | solution.py:103
  59.2 2.2 %copy-done = bf16[16,288,512]{2,1,0:T(8,128)(2,1)} copy-done((bf16[16,288,512]{2,1,0:T(8,128)(2,1)}, bf16[16,288,512]{2,1,0:T(8,128)(2,1)S(1)}, u32[]{:S(2)}) %copy-start) | copy-done | bytes 4718616
  61.4 2.1 %copy-done.1 = bf16[16,512,256]{2,1,0:T(8,128)(2,1)} copy-done((bf16[16,512,256]{2,1,0:T(8,128)(2,1)}, bf16[16,512,256]{2,1,0:T(8,128)(2,1)S(1)}, u32[]{:S(2)}) %copy-start.1) | copy-done | bytes 4194328
  63.9 5.9 %collective-permute-done.13.refs_6_ = bf16[16,16,256]{2,1,0:T(8,128)(2,1)S(1)} collective-permute-done((bf16[16,16,256]{2,1,0:T(8,128)(2,1)S(1)}, bf16[16,16,256]{2,1,0:T(8,128)(2,1)S(1)}, u32[]{:S(2)}, u32[]{:S(2)}) %collective-permute-start.13) | collective-permute-done | bytes 131104 | tf_op jit(solution)/shard_map/ppermute | solution.py:413
  71.8 4.7 %project.3 = (bf16[16,512,256]{2,1,0:T(8,128)(2,1)S(1)}, bf16[16,288,512]{2,1,0:T(8,128)(2,1)S(1)}) custom-call(bf16[16,512,256]{2,1,0:T(8,128)(2,1)} %collective-permute-done.17.rows, bf16[256,256]{1,0:T(8,128)(2,1)S(1)} %copy-done.7, bf16[256,256]{1,0:T(8,128)(2,1)S(1)} %bitcast.19), custom_call_target="tpu_custom_call" | custom-call | flops 3000000000 | bytes 12000000 | tf_op jit(solution)/shard_map/project/pallas_call | solution.py:103
  76.6 6.7 %attend.9 = (bf16[272,256]{1,0:T(8,128)(2,1)S(1)}, bf16[272,256]{1,0:T(8,128)(2,1)S(1)}, bf16[272,256]{1,0:T(8,128)(2,1)S(1)}, bf16[272,256]{1,0:T(8,128)(2,1)S(1)}) custom-call(s32[3,16]{1,0:T(4,128)S(1)} %concatenate.7.live, bf16[16,16,256]{2,1,0:T(8,128)(2,1)S(1)} %collective-permute-done.3.refs_0_.refs_8_, ...), custom_call_target="tpu_custom_call" | custom-call | flops 6000000000 | bytes 5000000 | tf_op jit(solution)/shard_map/attend/pallas_call | solution.py:240
  83.3 2.3 %collective-permute-start.25 = (bf16[272,256]{1,0:T(8,128)(2,1)S(1)}, bf16[272,256]{1,0:T(8,128)(2,1)S(1)}, u32[]{:S(2)}, u32[]{:S(2)}) collective-permute-start(bf16[272,256]{1,0:T(8,128)(2,1)S(1)} %get-tuple-element.48), channel_id=1, source_target_pairs={{2,0},{4,2},{6,4},{8,6},{10,8},{12,10},{14,12},{16,14},{18,16},{20... | collective-permute-start | bytes 417800 | tf_op jit(solution)/shard_map/ppermute | solution.py:413
  85.6 6.7 %attend.6 = (bf16[272,256]{1,0:T(8,128)(2,1)S(1)}, bf16[272,256]{1,0:T(8,128)(2,1)S(1)}, bf16[272,256]{1,0:T(8,128)(2,1)S(1)}, bf16[272,256]{1,0:T(8,128)(2,1)S(1)}) custom-call(s32[3,16]{1,0:T(4,128)S(1)} %concatenate.7.live, bf16[16,16,256]{2,1,0:T(8,128)(2,1)S(1)} %collective-permute-done.3.refs_0_.refs_8_, ...), custom_call_target="tpu_custom_call" | custom-call | flops 6000000000 | bytes 5000000 | tf_op jit(solution)/shard_map/attend/pallas_call | solution.py:240
  93.1 3.6 %attend.11 = (bf16[272,128]{1,0:T(8,128)(2,1)S(1)}, bf16[272,128]{1,0:T(8,128)(2,1)S(1)}, bf16[272,128]{1,0:T(8,128)(2,1)S(1)}, bf16[272,128]{1,0:T(8,128)(2,1)S(1)}) custom-call(s32[3,16]{1,0:T(4,128)S(1)} %concatenate.7.live, bf16[16,16,256]{2,1,0:T(8,128)(2,1)S(1)} %bitcast.13, bf16[16,16,256]{2,1,0:T(8,128)(2,1)S(1)} %collective-permute-done.4.refs_1_, ...), custom_call_target="tpu_custom_call" | custom-call | flops 3000000000 | bytes 5000000 | tf_op jit(solution)/shard_map/attend/pallas_call | solution.py:240
  97.6 2.5 %collective-permute-start.19 = (bf16[272,256]{1,0:T(8,128)(2,1)S(1)}, bf16[272,256]{1,0:T(8,128)(2,1)S(1)}, u32[]{:S(2)}, u32[]{:S(2)}) collective-permute-start(bf16[272,256]{1,0:T(8,128)(2,1)S(1)} %merge.12), channel_id=1, source_target_pairs={{2,0},{4,2},{6,4},{8,6},{10,8},{12,10},{14,12},{16,14},{18,16},{20... | collective-permute-start | bytes 417800 | tf_op jit(solution)/shard_map/ppermute | solution.py:413
  100.1 3.6 %attend.10 = (bf16[272,128]{1,0:T(8,128)(2,1)S(1)}, bf16[272,128]{1,0:T(8,128)(2,1)S(1)}, bf16[272,128]{1,0:T(8,128)(2,1)S(1)}, bf16[272,128]{1,0:T(8,128)(2,1)S(1)}) custom-call(s32[3,16]{1,0:T(4,128)S(1)} %concatenate.7.live, bf16[16,16,256]{2,1,0:T(8,128)(2,1)S(1)} %bitcast.14, bf16[16,16,256]{2,1,0:T(8,128)(2,1)S(1)} %collective-permute-done.4.refs_1_, ...), custom_call_target="tpu_custom_call" | custom-call | flops 3000000000 | bytes 5000000 | tf_op jit(solution)/shard_map/attend/pallas_call | solution.py:240
  103.7 2.1 %collective-permute-start.27 = (bf16[272,256]{1,0:T(8,128)(2,1)S(1)}, bf16[272,256]{1,0:T(8,128)(2,1)S(1)}, u32[]{:S(2)}, u32[]{:S(2)}) collective-permute-start(bf16[272,256]{1,0:T(8,128)(2,1)S(1)} %merge.19), channel_id=1, source_target_pairs={{2,0},{4,2},{6,4},{8,6},{10,8},{12,10},{14,12},{16,14},{18,16},{20... | collective-permute-start | bytes 417800 | tf_op jit(solution)/shard_map/ppermute | solution.py:413
  106.6 3.6 %attend.8 = (bf16[272,128]{1,0:T(8,128)(2,1)S(1)}, bf16[272,128]{1,0:T(8,128)(2,1)S(1)}, bf16[272,128]{1,0:T(8,128)(2,1)S(1)}, bf16[272,128]{1,0:T(8,128)(2,1)S(1)}) custom-call(s32[3,16]{1,0:T(4,128)S(1)} %concatenate.7.live, bf16[16,16,256]{2,1,0:T(8,128)(2,1)S(1)} %bitcast.15, bf16[16,16,256]{2,1,0:T(8,128)(2,1)S(1)} %collective-permute-done.4.refs_1_, ...), custom_call_target="tpu_custom_call" | custom-call | flops 3000000000 | bytes 5000000 | tf_op jit(solution)/shard_map/attend/pallas_call | solution.py:240
  110.3 2.0 %collective-permute-start.28 = (bf16[272,256]{1,0:T(8,128)(2,1)S(1)}, bf16[272,256]{1,0:T(8,128)(2,1)S(1)}, u32[]{:S(2)}, u32[]{:S(2)}) collective-permute-start(bf16[272,256]{1,0:T(8,128)(2,1)S(1)} %merge.20), channel_id=1, source_target_pairs={{2,0},{4,2},{6,4},{8,6},{10,8},{12,10},{14,12},{16,14},{18,16},{20... | collective-permute-start | bytes 417800 | tf_op jit(solution)/shard_map/ppermute | solution.py:413
  113.8 3.6 %attend.7 = (bf16[272,128]{1,0:T(8,128)(2,1)S(1)}, bf16[272,128]{1,0:T(8,128)(2,1)S(1)}, bf16[272,128]{1,0:T(8,128)(2,1)S(1)}, bf16[272,128]{1,0:T(8,128)(2,1)S(1)}) custom-call(s32[3,16]{1,0:T(4,128)S(1)} %concatenate.7.live, bf16[16,16,256]{2,1,0:T(8,128)(2,1)S(1)} %bitcast.16, bf16[16,16,256]{2,1,0:T(8,128)(2,1)S(1)} %collective-permute-done.4.refs_1_, ...), custom_call_target="tpu_custom_call" | custom-call | flops 3000000000 | bytes 5000000 | tf_op jit(solution)/shard_map/attend/pallas_call | solution.py:240
  120.3 2.4 %collective-permute-done.29.came = bf16[272,256]{1,0:T(8,128)(2,1)S(1)} collective-permute-done((bf16[272,256]{1,0:T(8,128)(2,1)S(1)}, bf16[272,256]{1,0:T(8,128)(2,1)S(1)}, u32[]{:S(2)}, u32[]{:S(2)}) %collective-permute-start.29) | collective-permute-done | bytes 139296 | tf_op jit(solution)/shard_map/ppermute | solution.py:413
  122.8 2.4 %collective-permute-start.30 = (bf16[272,256]{1,0:T(8,128)(2,1)S(1)}, bf16[272,256]{1,0:T(8,128)(2,1)S(1)}, u32[]{:S(2)}, u32[]{:S(2)}) collective-permute-start(bf16[272,256]{1,0:T(8,128)(2,1)S(1)} %merge.22), channel_id=1, source_target_pairs={{2,0},{4,2},{6,4},{8,6},{10,8},{12,10},{14,12},{16,14},{18,16},{20... | collective-permute-start | bytes 417800 | tf_op jit(solution)/shard_map/ppermute | solution.py:413
  128.0 3.6 %collective-permute-start.31 = (bf16[272,256]{1,0:T(8,128)(2,1)S(1)}, bf16[272,256]{1,0:T(8,128)(2,1)S(1)}, u32[]{:S(2)}, u32[]{:S(2)}) collective-permute-start(bf16[272,256]{1,0:T(8,128)(2,1)S(1)} %merge.23), channel_id=1, source_target_pairs={{2,0},{4,2},{6,4},{8,6},{10,8},{12,10},{14,12},{16,14},{18,16},{20... | collective-permute-start | bytes 417800 | tf_op jit(solution)/shard_map/ppermute | solution.py:413
  134.3 2.7 %collective-permute-done.24.refs_0_ = bf16[272,256]{1,0:T(8,128)(2,1)S(1)} collective-permute-done((bf16[272,256]{1,0:T(8,128)(2,1)S(1)}, bf16[272,256]{1,0:T(8,128)(2,1)S(1)}, u32[]{:S(2)}, u32[]{:S(2)}) %collective-permute-start.24) | collective-permute-done | bytes 139296 | tf_op jit(solution)/shard_map/ppermute | solution.py:413
  138.1 5.6 %collective-permute-done.33.b = bf16[272,256]{1,0:T(8,128)(2,1)S(1)} collective-permute-done((bf16[272,256]{1,0:T(8,128)(2,1)S(1)}, bf16[272,256]{1,0:T(8,128)(2,1)S(1)}, u32[]{:S(2)}, u32[]{:S(2)}) %collective-permute-start.33) | collective-permute-done | bytes 139296 | tf_op jit(solution)/shard_map/ppermute | solution.py:413
  143.8 1.5 %finish.1 = (bf16[256,256]{1,0:T(8,128)(2,1)}, f32[16,16]{1,0:T(8,128)}) custom-call(bf16[272,256]{1,0:T(8,128)(2,1)S(1)} %collective-permute-done.32.a, bf16[272,256]{1,0:T(8,128)(2,1)S(1)} %collective-permute-done.33.b, bf16[256,256]{1,0:T(8,128)(2,1)S(1)} %copy-done.8, f32[1,256]{1,0:T(1,128)S(1)} %bitcast.21, bf16[256,512]{1,0:T(8,128)(2,1)S(1)} %copy-done.6, ...), custom_call_target="tpu_custom_call" | custom-call | flops 200000000 | bytes 1000000 | tf_op jit(solution)/shard_map/finish/pallas_call | solution.py:356
  (106 shorter events, 22.4 us)
Async XLA Ops:
  6.3 65.5 %collective-permute-start.17 = (bf16[16,512,256]{2,1,0:T(8,128)(2,1)}, bf16[16,512,256]{2,1,0:T(8,128)(2,1)}, u32[]{:S(2)}, u32[]{:S(2)}) collective-permute-start(bf16[16,512,256]{2,1,0:T(8,128)(2,1)} %history.1.rows), channel_id=1, source_target_pairs={{0,1},{1,0},{2,3},{3,2},{4,5},{5,4},{6,7},{7,6},{8,9},{9,8},{10,11... | collective-permute-start | bytes 12582920 | tf_op jit(solution)/shard_map/ppermute | solution.py:413
  6.5 7.3 %collective-permute-start.4 = (bf16[16,16,256]{2,1,0:T(8,128)(2,1)S(1)}, bf16[16,16,256]{2,1,0:T(8,128)(2,1)S(1)}, u32[]{:S(2)}, u32[]{:S(2)}) collective-permute-start(bf16[16,16,256]{2,1,0:T(8,128)(2,1)S(1)} %bitcast.11), channel_id=1, source_target_pairs={{0,1},{1,0},{2,3},{3,2},{4,5},{5,4},{6,7},{7,6},{8,9},{9,8},{10,11... | collective-permute-start | bytes 393224 | tf_op jit(solution)/shard_map/ppermute | solution.py:413
  7.1 15.5 %collective-permute-start = (bf16[16,16,256]{2,1,0:T(8,128)(2,1)S(1)}, bf16[16,16,256]{2,1,0:T(8,128)(2,1)S(1)}, u32[]{:S(2)}, u32[]{:S(2)}) collective-permute-start(bf16[16,16,256]{2,1,0:T(8,128)(2,1)S(1)} %bitcast.12), channel_id=1, source_target_pairs={{0,2},{2,4},{4,6},{6,8},{8,10},{10,12},{12,14},{14,16},{16,18},{18... | collective-permute-start | bytes 393224 | tf_op jit(solution)/shard_map/ppermute | solution.py:413
  13.9 15.5 %collective-permute-start.5 = (bf16[16,16,256]{2,1,0:T(8,128)(2,1)S(1)}, bf16[16,16,256]{2,1,0:T(8,128)(2,1)S(1)}, u32[]{:S(2)}, u32[]{:S(2)}) collective-permute-start(bf16[16,16,256]{2,1,0:T(8,128)(2,1)S(1)} %collective-permute-done.4.refs_1_), channel_id=1, source_target_pairs={{0,2},{2,4},{4,6},{6,8},{8,10},{10,12},{12,14},{14,16},{16,18},{18... | collective-permute-start | bytes 393224 | tf_op jit(solution)/shard_map/ppermute | solution.py:413
  22.6 8.1 %collective-permute-start.1 = (bf16[16,16,256]{2,1,0:T(8,128)(2,1)S(1)}, bf16[16,16,256]{2,1,0:T(8,128)(2,1)S(1)}, u32[]{:S(2)}, u32[]{:S(2)}) collective-permute-start(bf16[16,16,256]{2,1,0:T(8,128)(2,1)S(1)} %collective-permute-done.refs_2_), channel_id=1, source_target_pairs={{0,2},{2,4},{4,6},{6,8},{8,10},{10,12},{12,14},{14,16},{16,18},{18... | collective-permute-start | bytes 393224 | tf_op jit(solution)/shard_map/ppermute | solution.py:413
  29.3 6.2 %collective-permute-start.6 = (bf16[16,16,256]{2,1,0:T(8,128)(2,1)S(1)}, bf16[16,16,256]{2,1,0:T(8,128)(2,1)S(1)}, u32[]{:S(2)}, u32[]{:S(2)}) collective-permute-start(bf16[16,16,256]{2,1,0:T(8,128)(2,1)S(1)} %collective-permute-done.5.refs_3_), channel_id=1, source_target_pairs={{0,2},{2,4},{4,6},{6,8},{8,10},{10,12},{12,14},{14,16},{16,18},{18... | collective-permute-start | bytes 393224 | tf_op jit(solution)/shard_map/ppermute | solution.py:413
  30.7 6.2 %collective-permute-start.2 = (bf16[16,16,256]{2,1,0:T(8,128)(2,1)S(1)}, bf16[16,16,256]{2,1,0:T(8,128)(2,1)S(1)}, u32[]{:S(2)}, u32[]{:S(2)}) collective-permute-start(bf16[16,16,256]{2,1,0:T(8,128)(2,1)S(1)} %collective-permute-done.1.refs_4_), channel_id=1, source_target_pairs={{0,2},{2,4},{4,6},{6,8},{8,10},{10,12},{12,14},{14,16},{16,18},{18... | collective-permute-start | bytes 393224 | tf_op jit(solution)/shard_map/ppermute | solution.py:413
  35.5 6.2 %collective-permute-start.7 = (bf16[16,16,256]{2,1,0:T(8,128)(2,1)S(1)}, bf16[16,16,256]{2,1,0:T(8,128)(2,1)S(1)}, u32[]{:S(2)}, u32[]{:S(2)}) collective-permute-start(bf16[16,16,256]{2,1,0:T(8,128)(2,1)S(1)} %collective-permute-done.6.refs_5_), channel_id=1, source_target_pairs={{0,2},{2,4},{4,6},{6,8},{8,10},{10,12},{12,14},{14,16},{16,18},{18... | collective-permute-start | bytes 393224 | tf_op jit(solution)/shard_map/ppermute | solution.py:413
  36.9 6.2 %collective-permute-start.3 = (bf16[16,16,256]{2,1,0:T(8,128)(2,1)S(1)}, bf16[16,16,256]{2,1,0:T(8,128)(2,1)S(1)}, u32[]{:S(2)}, u32[]{:S(2)}) collective-permute-start(bf16[16,16,256]{2,1,0:T(8,128)(2,1)S(1)} %collective-permute-done.2.refs_6_), channel_id=1, source_target_pairs={{0,2},{2,4},{4,6},{6,8},{8,10},{10,12},{12,14},{14,16},{16,18},{18... | collective-permute-start | bytes 393224 | tf_op jit(solution)/shard_map/ppermute | solution.py:413
  41.7 6.2 %collective-permute-start.8 = (bf16[16,16,256]{2,1,0:T(8,128)(2,1)S(1)}, bf16[16,16,256]{2,1,0:T(8,128)(2,1)S(1)}, u32[]{:S(2)}, u32[]{:S(2)}) collective-permute-start(bf16[16,16,256]{2,1,0:T(8,128)(2,1)S(1)} %collective-permute-done.7.refs_7_), channel_id=1, source_target_pairs={{0,2},{2,4},{4,6},{6,8},{8,10},{10,12},{12,14},{14,16},{16,18},{18... | collective-permute-start | bytes 393224 | tf_op jit(solution)/shard_map/ppermute | solution.py:413
  43.1 6.2 %collective-permute-start.9 = (bf16[16,16,256]{2,1,0:T(8,128)(2,1)S(1)}, bf16[16,16,256]{2,1,0:T(8,128)(2,1)S(1)}, u32[]{:S(2)}, u32[]{:S(2)}) collective-permute-start(bf16[16,16,256]{2,1,0:T(8,128)(2,1)S(1)} %collective-permute-done.3.refs_0_.refs_8_), channel_id=1, source_target_pairs={{0,2},{2,4},{4,6},{6,8},{8,10},{10,12},{12,14},{14,16},{16,18},{18... | collective-permute-start | bytes 393224 | tf_op jit(solution)/shard_map/ppermute | solution.py:413
  47.9 6.2 %collective-permute-start.10 = (bf16[16,16,256]{2,1,0:T(8,128)(2,1)S(1)}, bf16[16,16,256]{2,1,0:T(8,128)(2,1)S(1)}, u32[]{:S(2)}, u32[]{:S(2)}) collective-permute-start(bf16[16,16,256]{2,1,0:T(8,128)(2,1)S(1)} %collective-permute-done.8.refs_1_.refs_9_), channel_id=1, source_target_pairs={{0,2},{2,4},{4,6},{6,8},{8,10},{10,12},{12,14},{14,16},{16,18},{18... | collective-permute-start | bytes 393224 | tf_op jit(solution)/shard_map/ppermute | solution.py:413
  49.3 14.2 %collective-permute-start.11 = (bf16[16,16,256]{2,1,0:T(8,128)(2,1)S(1)}, bf16[16,16,256]{2,1,0:T(8,128)(2,1)S(1)}, u32[]{:S(2)}, u32[]{:S(2)}) collective-permute-start(bf16[16,16,256]{2,1,0:T(8,128)(2,1)S(1)} %collective-permute-done.9.refs_2_), channel_id=1, source_target_pairs={{0,2},{2,4},{4,6},{6,8},{8,10},{10,12},{12,14},{14,16},{16,18},{18... | collective-permute-start | bytes 393224 | tf_op jit(solution)/shard_map/ppermute | solution.py:413
  54.1 9.5 %collective-permute-start.12 = (bf16[16,16,256]{2,1,0:T(8,128)(2,1)S(1)}, bf16[16,16,256]{2,1,0:T(8,128)(2,1)S(1)}, u32[]{:S(2)}, u32[]{:S(2)}) collective-permute-start(bf16[16,16,256]{2,1,0:T(8,128)(2,1)S(1)} %collective-permute-done.10.refs_3_), channel_id=1, source_target_pairs={{0,2},{2,4},{4,6},{6,8},{8,10},{10,12},{12,14},{14,16},{16,18},{18... | collective-permute-start | bytes 393224 | tf_op jit(solution)/shard_map/ppermute | solution.py:413
  63.5 6.2 %collective-permute-start.13 = (bf16[16,16,256]{2,1,0:T(8,128)(2,1)S(1)}, bf16[16,16,256]{2,1,0:T(8,128)(2,1)S(1)}, u32[]{:S(2)}, u32[]{:S(2)}) collective-permute-start(bf16[16,16,256]{2,1,0:T(8,128)(2,1)S(1)} %collective-permute-done.11.refs_4_), channel_id=1, source_target_pairs={{0,2},{2,4},{4,6},{6,8},{8,10},{10,12},{12,14},{14,16},{16,18},{18... | collective-permute-start | bytes 393224 | tf_op jit(solution)/shard_map/ppermute | solution.py:413
  63.6 7.6 %collective-permute-start.14 = (bf16[16,16,256]{2,1,0:T(8,128)(2,1)S(1)}, bf16[16,16,256]{2,1,0:T(8,128)(2,1)S(1)}, u32[]{:S(2)}, u32[]{:S(2)}) collective-permute-start(bf16[16,16,256]{2,1,0:T(8,128)(2,1)S(1)} %collective-permute-done.12.refs_5_), channel_id=1, source_target_pairs={{0,2},{2,4},{4,6},{6,8},{8,10},{10,12},{12,14},{14,16},{16,18},{18... | collective-permute-start | bytes 393224 | tf_op jit(solution)/shard_map/ppermute | solution.py:413
  69.8 6.8 %collective-permute-start.15 = (bf16[16,16,256]{2,1,0:T(8,128)(2,1)S(1)}, bf16[16,16,256]{2,1,0:T(8,128)(2,1)S(1)}, u32[]{:S(2)}, u32[]{:S(2)}) collective-permute-start(bf16[16,16,256]{2,1,0:T(8,128)(2,1)S(1)} %collective-permute-done.13.refs_6_), channel_id=1, source_target_pairs={{1,31},{3,1},{5,3},{7,5},{9,7},{11,9},{13,11},{15,13},{17,15},{19,... | collective-permute-start | bytes 393224 | tf_op jit(solution)/shard_map/ppermute | solution.py:413
  71.2 5.4 %collective-permute-start.16 = (bf16[16,16,256]{2,1,0:T(8,128)(2,1)S(1)}, bf16[16,16,256]{2,1,0:T(8,128)(2,1)S(1)}, u32[]{:S(2)}, u32[]{:S(2)}) collective-permute-start(bf16[16,16,256]{2,1,0:T(8,128)(2,1)S(1)} %collective-permute-done.14.refs_7_), channel_id=1, source_target_pairs={{1,31},{3,1},{5,3},{7,5},{9,7},{11,9},{13,11},{15,13},{17,15},{19,... | collective-permute-start | bytes 393224 | tf_op jit(solution)/shard_map/ppermute | solution.py:413
  83.3 13.3 %collective-permute-start.25 = (bf16[272,256]{1,0:T(8,128)(2,1)S(1)}, bf16[272,256]{1,0:T(8,128)(2,1)S(1)}, u32[]{:S(2)}, u32[]{:S(2)}) collective-permute-start(bf16[272,256]{1,0:T(8,128)(2,1)S(1)} %get-tuple-element.48), channel_id=1, source_target_pairs={{2,0},{4,2},{6,4},{8,6},{10,8},{12,10},{14,12},{16,14},{18,16},{20... | collective-permute-start | bytes 417800 | tf_op jit(solution)/shard_map/ppermute | solution.py:413
  92.3 5.2 %collective-permute-start.18 = (bf16[272,256]{1,0:T(8,128)(2,1)S(1)}, bf16[272,256]{1,0:T(8,128)(2,1)S(1)}, u32[]{:S(2)}, u32[]{:S(2)}) collective-permute-start(bf16[272,256]{1,0:T(8,128)(2,1)S(1)} %get-tuple-element.38), channel_id=1, source_target_pairs={{2,0},{4,2},{6,4},{8,6},{10,8},{12,10},{14,12},{16,14},{18,16},{20... | collective-permute-start | bytes 417800 | tf_op jit(solution)/shard_map/ppermute | solution.py:413
  96.8 6.9 %collective-permute-start.26 = (bf16[272,256]{1,0:T(8,128)(2,1)S(1)}, bf16[272,256]{1,0:T(8,128)(2,1)S(1)}, u32[]{:S(2)}, u32[]{:S(2)}) collective-permute-start(bf16[272,256]{1,0:T(8,128)(2,1)S(1)} %merge.18), channel_id=1, source_target_pairs={{2,0},{4,2},{6,4},{8,6},{10,8},{12,10},{14,12},{16,14},{18,16},{20... | collective-permute-start | bytes 417800 | tf_op jit(solution)/shard_map/ppermute | solution.py:413
  97.6 8.3 %collective-permute-start.19 = (bf16[272,256]{1,0:T(8,128)(2,1)S(1)}, bf16[272,256]{1,0:T(8,128)(2,1)S(1)}, u32[]{:S(2)}, u32[]{:S(2)}) collective-permute-start(bf16[272,256]{1,0:T(8,128)(2,1)S(1)} %merge.12), channel_id=1, source_target_pairs={{2,0},{4,2},{6,4},{8,6},{10,8},{12,10},{14,12},{16,14},{18,16},{20... | collective-permute-start | bytes 417800 | tf_op jit(solution)/shard_map/ppermute | solution.py:413
  103.7 6.5 %collective-permute-start.27 = (bf16[272,256]{1,0:T(8,128)(2,1)S(1)}, bf16[272,256]{1,0:T(8,128)(2,1)S(1)}, u32[]{:S(2)}, u32[]{:S(2)}) collective-permute-start(bf16[272,256]{1,0:T(8,128)(2,1)S(1)} %merge.19), channel_id=1, source_target_pairs={{2,0},{4,2},{6,4},{8,6},{10,8},{12,10},{14,12},{16,14},{18,16},{20... | collective-permute-start | bytes 417800 | tf_op jit(solution)/shard_map/ppermute | solution.py:413
  105.9 6.4 %collective-permute-start.20 = (bf16[272,256]{1,0:T(8,128)(2,1)S(1)}, bf16[272,256]{1,0:T(8,128)(2,1)S(1)}, u32[]{:S(2)}, u32[]{:S(2)}) collective-permute-start(bf16[272,256]{1,0:T(8,128)(2,1)S(1)} %merge.13), channel_id=1, source_target_pairs={{2,0},{4,2},{6,4},{8,6},{10,8},{12,10},{14,12},{16,14},{18,16},{20... | collective-permute-start | bytes 417800 | tf_op jit(solution)/shard_map/ppermute | solution.py:413
  110.3 7.1 %collective-permute-start.28 = (bf16[272,256]{1,0:T(8,128)(2,1)S(1)}, bf16[272,256]{1,0:T(8,128)(2,1)S(1)}, u32[]{:S(2)}, u32[]{:S(2)}) collective-permute-start(bf16[272,256]{1,0:T(8,128)(2,1)S(1)} %merge.20), channel_id=1, source_target_pairs={{2,0},{4,2},{6,4},{8,6},{10,8},{12,10},{14,12},{16,14},{18,16},{20... | collective-permute-start | bytes 417800 | tf_op jit(solution)/shard_map/ppermute | solution.py:413
  112.4 6.3 %collective-permute-start.21 = (bf16[272,256]{1,0:T(8,128)(2,1)S(1)}, bf16[272,256]{1,0:T(8,128)(2,1)S(1)}, u32[]{:S(2)}, u32[]{:S(2)}) collective-permute-start(bf16[272,256]{1,0:T(8,128)(2,1)S(1)} %merge.14), channel_id=1, source_target_pairs={{2,0},{4,2},{6,4},{8,6},{10,8},{12,10},{14,12},{16,14},{18,16},{20... | collective-permute-start | bytes 417800 | tf_op jit(solution)/shard_map/ppermute | solution.py:413
  117.5 5.2 %collective-permute-start.29 = (bf16[272,256]{1,0:T(8,128)(2,1)S(1)}, bf16[272,256]{1,0:T(8,128)(2,1)S(1)}, u32[]{:S(2)}, u32[]{:S(2)}) collective-permute-start(bf16[272,256]{1,0:T(8,128)(2,1)S(1)} %merge.21), channel_id=1, source_target_pairs={{2,0},{4,2},{6,4},{8,6},{10,8},{12,10},{14,12},{16,14},{18,16},{20... | collective-permute-start | bytes 417800 | tf_op jit(solution)/shard_map/ppermute | solution.py:413
  118.8 6.4 %collective-permute-start.22 = (bf16[272,256]{1,0:T(8,128)(2,1)S(1)}, bf16[272,256]{1,0:T(8,128)(2,1)S(1)}, u32[]{:S(2)}, u32[]{:S(2)}) collective-permute-start(bf16[272,256]{1,0:T(8,128)(2,1)S(1)} %merge.15), channel_id=1, source_target_pairs={{2,0},{4,2},{6,4},{8,6},{10,8},{12,10},{14,12},{16,14},{18,16},{20... | collective-permute-start | bytes 417800 | tf_op jit(solution)/shard_map/ppermute | solution.py:413
  122.8 5.2 %collective-permute-start.30 = (bf16[272,256]{1,0:T(8,128)(2,1)S(1)}, bf16[272,256]{1,0:T(8,128)(2,1)S(1)}, u32[]{:S(2)}, u32[]{:S(2)}) collective-permute-start(bf16[272,256]{1,0:T(8,128)(2,1)S(1)} %merge.22), channel_id=1, source_target_pairs={{2,0},{4,2},{6,4},{8,6},{10,8},{12,10},{14,12},{16,14},{18,16},{20... | collective-permute-start | bytes 417800 | tf_op jit(solution)/shard_map/ppermute | solution.py:413
  125.3 6.4 %collective-permute-start.23 = (bf16[272,256]{1,0:T(8,128)(2,1)S(1)}, bf16[272,256]{1,0:T(8,128)(2,1)S(1)}, u32[]{:S(2)}, u32[]{:S(2)}) collective-permute-start(bf16[272,256]{1,0:T(8,128)(2,1)S(1)} %merge.16), channel_id=1, source_target_pairs={{2,0},{4,2},{6,4},{8,6},{10,8},{12,10},{14,12},{16,14},{18,16},{20... | collective-permute-start | bytes 417800 | tf_op jit(solution)/shard_map/ppermute | solution.py:413
  128.0 6.2 %collective-permute-start.31 = (bf16[272,256]{1,0:T(8,128)(2,1)S(1)}, bf16[272,256]{1,0:T(8,128)(2,1)S(1)}, u32[]{:S(2)}, u32[]{:S(2)}) collective-permute-start(bf16[272,256]{1,0:T(8,128)(2,1)S(1)} %merge.23), channel_id=1, source_target_pairs={{2,0},{4,2},{6,4},{8,6},{10,8},{12,10},{14,12},{16,14},{18,16},{20... | collective-permute-start | bytes 417800 | tf_op jit(solution)/shard_map/ppermute | solution.py:413
  138.0 5.7 %collective-permute-start.33 = (bf16[272,256]{1,0:T(8,128)(2,1)S(1)}, bf16[272,256]{1,0:T(8,128)(2,1)S(1)}, u32[]{:S(2)}, u32[]{:S(2)}) collective-permute-start(bf16[272,256]{1,0:T(8,128)(2,1)S(1)} %get-tuple-element.63), channel_id=1, source_target_pairs={{0,1},{2,3},{4,5},{6,7},{8,9},{10,11},{12,13},{14,15},{16,17},{18,... | collective-permute-start | bytes 417800 | tf_op jit(solution)/shard_map/ppermute | solution.py:413
  (18 other events, 321.4 us)

commit v4 on v3

--- a/solution.py
+++ b/solution.py
@@ -387,8 +387,6 @@
     slots = chips // 2
     near = lambda d, c: (d % chips) * 2 + c
     ring = [(near(d, 0), near(d + 1, 0)) for d in range(chips)] + [(near(d, 1), near(d - 1, 1)) for d in range(chips)]
-    stay = [(near(d, 0), near(d, 0)) for d in range(chips)] + [(near(d, 1), near(d - 1, 1)) for d in range(chips)]
-    cross = [(near(d, 1), near(d, 0)) for d in range(chips)] + [(near(d, 0), near(d - 1, 1)) for d in range(chips)]
     tail = [(near(d, 1), near(d - 1, 1)) for d in range(chips)]
     swap = [(near(d, c), near(d, 1 - c)) for d in range(chips) for c in range(2)]
     back = lambda pairs: [(b, a) for a, b in pairs]
@@ -451,7 +449,9 @@
                 come = [merge(c, result(part, slot)) for part, c in enumerate(come)]
         halves = reorder((GROUP, 2, cand), (1, 0, 2))
         first, second = split(come, [x for part in range(PARTS) for x in result(part, 0)], halves)
-        first, second = send(first, back(stay)), send(second, back(cross))
+        moved = [send(x, back(tail)) for x in (first, second)]
+        kept, given = (jnp.where(me % 2 == 0, x, y) for x, y in zip((first, second), moved))
+        first, second = kept, send(given, swap)
         interest, logits = finish(
             users, first, second, out_weight, norm_gain, hidden_weight, hidden_bias, score_weight
         )

time: 146 us -> 143 us (0.979)
  waiting for transfers between devices: 62.5 us -> 57.7 us
    ppermute x34 -> x35, waiting for transfers between devices: 62.5 us -> 57.7 us  [on_device(): send = lambda array, pairs: lax.ppermute(array, 'seq', pairs)]
    ppermute x34 -> x35, starting transfers between devices: 30.7 us -> 31.8 us  [on_device(): send = lambda array, pairs: lax.ppermute(array, 'seq', pairs)]
  transfers between devices with their start and end apart: 34 -> 35, of which waited for: 19 -> 19; matrix products, arithmetic and copies ran while one was open for 0% -> 0% of each run, Pallas kernels for 20% -> 21%
where the time goes in v4:
time: 143 us; the launch traced here: 142 us
  waiting for transfers between devices  57.7 us (40%)
  Pallas kernels  44 us (31%)
  starting transfers between devices  31.8 us (22%)
  local copies, waits for them, and re-layouts  6.61 us (5%)
    ppermute x35, waiting for transfers between devices, on_device(): send = lambda array, pairs: lax.ppermute(array, 'seq', pairs)  57.7 us
    ppermute x35, starting transfers between devices, on_device(): send = lambda array, pairs: lax.ppermute(array, 'seq', pairs)  31.8 us
    pallas_call x6, Pallas kernels, attend(): pl.pallas_call(functools.partial(attend_body, base), grid_spec=pltpu.Pref...  27.7 us
    pallas_call x2, Pallas kernels, project(): pl.pallas_call(project_body, grid=(users // BATCH,), in_specs=[pl.BlockSp...  7.62 us
    unnamed x33, local copies, waits for them, and re-layouts  6.6 us
    pallas_call x1, Pallas kernels, history_rows(): pl.pallas_call(history_body, grid=(users // BATCH,), in_specs=[pl.BlockSp...  5.62 us
  transfers between devices with their start and end apart: 35, of which 19 were waited for; matrix products, arithmetic and copies ran while one was open for 0% of the time, Pallas kernels for 21%

profile of v4, /device:TPU:70, one launch (start us, length us, event | category | flops | bytes accessed | tf_op | source)
XLA Modules:
  0.0 141.7 jit_solution(6387762990386182672)
XLA Ops:
  0.7 5.6 %history.1.rows = bf16[16,512,256]{2,1,0:T(8,128)(2,1)} custom-call(s32[16,128,256]{2,1,0:T(8,128)} %words.1, s32[16,512]{1,0:T(8,128)} %index.1, f32[1,256]{1,0:T(1,128)} %bitcast.22), custom_call_target="tpu_custom_call" | custom-call | flops 2000000000 | bytes 6000000 | tf_op jit(solution)/shard_map/history/pallas_call | solution.py:70
  7.1 2.1 %collective-permute-start = (bf16[16,16,256]{2,1,0:T(8,128)(2,1)S(1)}, bf16[16,16,256]{2,1,0:T(8,128)(2,1)S(1)}, u32[]{:S(2)}, u32[]{:S(2)}) collective-permute-start(bf16[16,16,256]{2,1,0:T(8,128)(2,1)S(1)} %bitcast.12), channel_id=1, source_target_pairs={{0,2},{2,4},{4,6},{6,8},{8,10},{10,12},{12,14},{14,16},{16,18},{18... | collective-permute-start | bytes 393224 | tf_op jit(solution)/shard_map/ppermute | solution.py:411
  9.2 4.6 %collective-permute-done.4.refs_1_ = bf16[16,16,256]{2,1,0:T(8,128)(2,1)S(1)} collective-permute-done((bf16[16,16,256]{2,1,0:T(8,128)(2,1)S(1)}, bf16[16,16,256]{2,1,0:T(8,128)(2,1)S(1)}, u32[]{:S(2)}, u32[]{:S(2)}) %collective-permute-start.4) | collective-permute-done | bytes 131104 | tf_op jit(solution)/shard_map/ppermute | solution.py:411
  13.9 2.1 %collective-permute-start.5 = (bf16[16,16,256]{2,1,0:T(8,128)(2,1)S(1)}, bf16[16,16,256]{2,1,0:T(8,128)(2,1)S(1)}, u32[]{:S(2)}, u32[]{:S(2)}) collective-permute-start(bf16[16,16,256]{2,1,0:T(8,128)(2,1)S(1)} %collective-permute-done.4.refs_1_), channel_id=1, source_target_pairs={{0,2},{2,4},{4,6},{6,8},{8,10},{10,12},{12,14},{14,16},{16,18},{18... | collective-permute-start | bytes 393224 | tf_op jit(solution)/shard_map/ppermute | solution.py:411
  16.0 6.6 %collective-permute-done.refs_2_ = bf16[16,16,256]{2,1,0:T(8,128)(2,1)S(1)} collective-permute-done((bf16[16,16,256]{2,1,0:T(8,128)(2,1)S(1)}, bf16[16,16,256]{2,1,0:T(8,128)(2,1)S(1)}, u32[]{:S(2)}, u32[]{:S(2)}) %collective-permute-start) | collective-permute-done | bytes 131104 | tf_op jit(solution)/shard_map/ppermute | solution.py:411
  22.6 6.7 %collective-permute-done.5.refs_3_ = bf16[16,16,256]{2,1,0:T(8,128)(2,1)S(1)} collective-permute-done((bf16[16,16,256]{2,1,0:T(8,128)(2,1)S(1)}, bf16[16,16,256]{2,1,0:T(8,128)(2,1)S(1)}, u32[]{:S(2)}, u32[]{:S(2)}) %collective-permute-start.5) | collective-permute-done | bytes 131104 | tf_op jit(solution)/shard_map/ppermute | solution.py:411
  30.7 4.8 %collective-permute-done.6.refs_5_ = bf16[16,16,256]{2,1,0:T(8,128)(2,1)S(1)} collective-permute-done((bf16[16,16,256]{2,1,0:T(8,128)(2,1)S(1)}, bf16[16,16,256]{2,1,0:T(8,128)(2,1)S(1)}, u32[]{:S(2)}, u32[]{:S(2)}) %collective-permute-start.6) | collective-permute-done | bytes 131104 | tf_op jit(solution)/shard_map/ppermute | solution.py:411
  36.9 4.8 %collective-permute-done.7.refs_7_ = bf16[16,16,256]{2,1,0:T(8,128)(2,1)S(1)} collective-permute-done((bf16[16,16,256]{2,1,0:T(8,128)(2,1)S(1)}, bf16[16,16,256]{2,1,0:T(8,128)(2,1)S(1)}, u32[]{:S(2)}, u32[]{:S(2)}) %collective-permute-start.7) | collective-permute-done | bytes 131104 | tf_op jit(solution)/shard_map/ppermute | solution.py:411
  43.1 4.8 %collective-permute-done.8.refs_1_.refs_9_ = bf16[16,16,256]{2,1,0:T(8,128)(2,1)S(1)} collective-permute-done((bf16[16,16,256]{2,1,0:T(8,128)(2,1)S(1)}, bf16[16,16,256]{2,1,0:T(8,128)(2,1)S(1)}, u32[]{:S(2)}, u32[]{:S(2)}) %collective-permute-start.8) | collective-permute-done | bytes 131104 | tf_op jit(solution)/shard_map/ppermute | solution.py:411
  49.3 4.8 %collective-permute-done.10.refs_3_ = bf16[16,16,256]{2,1,0:T(8,128)(2,1)S(1)} collective-permute-done((bf16[16,16,256]{2,1,0:T(8,128)(2,1)S(1)}, bf16[16,16,256]{2,1,0:T(8,128)(2,1)S(1)}, u32[]{:S(2)}, u32[]{:S(2)}) %collective-permute-start.10) | collective-permute-done | bytes 131104 | tf_op jit(solution)/shard_map/ppermute | solution.py:411
  54.1 2.2 %copy-done.5 = bf16[16,512,256]{2,1,0:T(8,128)(2,1)S(1)} copy-done((bf16[16,512,256]{2,1,0:T(8,128)(2,1)S(1)}, bf16[16,512,256]{2,1,0:T(8,128)(2,1)}, u32[]{:S(2)}) %copy-start.5) | copy-done | bytes 4194328
  56.2 2.9 %project.2 = (bf16[16,512,256]{2,1,0:T(8,128)(2,1)S(1)}, bf16[16,288,512]{2,1,0:T(8,128)(2,1)S(1)}) custom-call(bf16[16,512,256]{2,1,0:T(8,128)(2,1)S(1)} %copy-done.5, bf16[256,256]{1,0:T(8,128)(2,1)S(1)} %copy-done.7, bf16[256,256]{1,0:T(8,128)(2,1)S(1)} %bitcast.18), custom_call_target="tpu_custom_call" | custom-call | flops 3000000000 | bytes 12000000 | tf_op jit(solution)/shard_map/project/pallas_call | solution.py:103
  59.2 2.2 %copy-done = bf16[16,288,512]{2,1,0:T(8,128)(2,1)} copy-done((bf16[16,288,512]{2,1,0:T(8,128)(2,1)}, bf16[16,288,512]{2,1,0:T(8,128)(2,1)S(1)}, u32[]{:S(2)}) %copy-start) | copy-done | bytes 4718616
  61.3 2.1 %copy-done.1 = bf16[16,512,256]{2,1,0:T(8,128)(2,1)} copy-done((bf16[16,512,256]{2,1,0:T(8,128)(2,1)}, bf16[16,512,256]{2,1,0:T(8,128)(2,1)S(1)}, u32[]{:S(2)}) %copy-start.1) | copy-done | bytes 4194328
  63.8 5.9 %collective-permute-done.13.refs_6_ = bf16[16,16,256]{2,1,0:T(8,128)(2,1)S(1)} collective-permute-done((bf16[16,16,256]{2,1,0:T(8,128)(2,1)S(1)}, bf16[16,16,256]{2,1,0:T(8,128)(2,1)S(1)}, u32[]{:S(2)}, u32[]{:S(2)}) %collective-permute-start.13) | collective-permute-done | bytes 131104 | tf_op jit(solution)/shard_map/ppermute | solution.py:411
  71.8 4.7 %project.3 = (bf16[16,512,256]{2,1,0:T(8,128)(2,1)S(1)}, bf16[16,288,512]{2,1,0:T(8,128)(2,1)S(1)}) custom-call(bf16[16,512,256]{2,1,0:T(8,128)(2,1)} %collective-permute-done.17.rows, bf16[256,256]{1,0:T(8,128)(2,1)S(1)} %copy-done.7, bf16[256,256]{1,0:T(8,128)(2,1)S(1)} %bitcast.19), custom_call_target="tpu_custom_call" | custom-call | flops 3000000000 | bytes 12000000 | tf_op jit(solution)/shard_map/project/pallas_call | solution.py:103
  76.6 6.7 %attend.9 = (bf16[272,256]{1,0:T(8,128)(2,1)S(1)}, bf16[272,256]{1,0:T(8,128)(2,1)S(1)}, bf16[272,256]{1,0:T(8,128)(2,1)S(1)}, bf16[272,256]{1,0:T(8,128)(2,1)S(1)}) custom-call(s32[3,16]{1,0:T(4,128)S(1)} %concatenate.7.live, bf16[16,16,256]{2,1,0:T(8,128)(2,1)S(1)} %collective-permute-done.3.refs_0_.refs_8_, ...), custom_call_target="tpu_custom_call" | custom-call | flops 6000000000 | bytes 5000000 | tf_op jit(solution)/shard_map/attend/pallas_call | solution.py:240
  83.3 2.3 %collective-permute-start.25 = (bf16[272,256]{1,0:T(8,128)(2,1)S(1)}, bf16[272,256]{1,0:T(8,128)(2,1)S(1)}, u32[]{:S(2)}, u32[]{:S(2)}) collective-permute-start(bf16[272,256]{1,0:T(8,128)(2,1)S(1)} %get-tuple-element.48), channel_id=1, source_target_pairs={{2,0},{4,2},{6,4},{8,6},{10,8},{12,10},{14,12},{16,14},{18,16},{20... | collective-permute-start | bytes 417800 | tf_op jit(solution)/shard_map/ppermute | solution.py:411
  85.6 6.7 %attend.6 = (bf16[272,256]{1,0:T(8,128)(2,1)S(1)}, bf16[272,256]{1,0:T(8,128)(2,1)S(1)}, bf16[272,256]{1,0:T(8,128)(2,1)S(1)}, bf16[272,256]{1,0:T(8,128)(2,1)S(1)}) custom-call(s32[3,16]{1,0:T(4,128)S(1)} %concatenate.7.live, bf16[16,16,256]{2,1,0:T(8,128)(2,1)S(1)} %collective-permute-done.3.refs_0_.refs_8_, ...), custom_call_target="tpu_custom_call" | custom-call | flops 6000000000 | bytes 5000000 | tf_op jit(solution)/shard_map/attend/pallas_call | solution.py:240
  93.1 3.6 %attend.11 = (bf16[272,128]{1,0:T(8,128)(2,1)S(1)}, bf16[272,128]{1,0:T(8,128)(2,1)S(1)}, bf16[272,128]{1,0:T(8,128)(2,1)S(1)}, bf16[272,128]{1,0:T(8,128)(2,1)S(1)}) custom-call(s32[3,16]{1,0:T(4,128)S(1)} %concatenate.7.live, bf16[16,16,256]{2,1,0:T(8,128)(2,1)S(1)} %bitcast.13, bf16[16,16,256]{2,1,0:T(8,128)(2,1)S(1)} %collective-permute-done.4.refs_1_, ...), custom_call_target="tpu_custom_call" | custom-call | flops 3000000000 | bytes 5000000 | tf_op jit(solution)/shard_map/attend/pallas_call | solution.py:240
  97.6 2.5 %collective-permute-start.19 = (bf16[272,256]{1,0:T(8,128)(2,1)S(1)}, bf16[272,256]{1,0:T(8,128)(2,1)S(1)}, u32[]{:S(2)}, u32[]{:S(2)}) collective-permute-start(bf16[272,256]{1,0:T(8,128)(2,1)S(1)} %merge.12), channel_id=1, source_target_pairs={{2,0},{4,2},{6,4},{8,6},{10,8},{12,10},{14,12},{16,14},{18,16},{20... | collective-permute-start | bytes 417800 | tf_op jit(solution)/shard_map/ppermute | solution.py:411
  100.0 3.6 %attend.10 = (bf16[272,128]{1,0:T(8,128)(2,1)S(1)}, bf16[272,128]{1,0:T(8,128)(2,1)S(1)}, bf16[272,128]{1,0:T(8,128)(2,1)S(1)}, bf16[272,128]{1,0:T(8,128)(2,1)S(1)}) custom-call(s32[3,16]{1,0:T(4,128)S(1)} %concatenate.7.live, bf16[16,16,256]{2,1,0:T(8,128)(2,1)S(1)} %bitcast.14, bf16[16,16,256]{2,1,0:T(8,128)(2,1)S(1)} %collective-permute-done.4.refs_1_, ...), custom_call_target="tpu_custom_call" | custom-call | flops 3000000000 | bytes 5000000 | tf_op jit(solution)/shard_map/attend/pallas_call | solution.py:240
  103.7 2.1 %collective-permute-start.27 = (bf16[272,256]{1,0:T(8,128)(2,1)S(1)}, bf16[272,256]{1,0:T(8,128)(2,1)S(1)}, u32[]{:S(2)}, u32[]{:S(2)}) collective-permute-start(bf16[272,256]{1,0:T(8,128)(2,1)S(1)} %merge.19), channel_id=1, source_target_pairs={{2,0},{4,2},{6,4},{8,6},{10,8},{12,10},{14,12},{16,14},{18,16},{20... | collective-permute-start | bytes 417800 | tf_op jit(solution)/shard_map/ppermute | solution.py:411
  106.6 3.6 %attend.8 = (bf16[272,128]{1,0:T(8,128)(2,1)S(1)}, bf16[272,128]{1,0:T(8,128)(2,1)S(1)}, bf16[272,128]{1,0:T(8,128)(2,1)S(1)}, bf16[272,128]{1,0:T(8,128)(2,1)S(1)}) custom-call(s32[3,16]{1,0:T(4,128)S(1)} %concatenate.7.live, bf16[16,16,256]{2,1,0:T(8,128)(2,1)S(1)} %bitcast.15, bf16[16,16,256]{2,1,0:T(8,128)(2,1)S(1)} %collective-permute-done.4.refs_1_, ...), custom_call_target="tpu_custom_call" | custom-call | flops 3000000000 | bytes 5000000 | tf_op jit(solution)/shard_map/attend/pallas_call | solution.py:240
  110.3 2.0 %collective-permute-start.28 = (bf16[272,256]{1,0:T(8,128)(2,1)S(1)}, bf16[272,256]{1,0:T(8,128)(2,1)S(1)}, u32[]{:S(2)}, u32[]{:S(2)}) collective-permute-start(bf16[272,256]{1,0:T(8,128)(2,1)S(1)} %merge.20), channel_id=1, source_target_pairs={{2,0},{4,2},{6,4},{8,6},{10,8},{12,10},{14,12},{16,14},{18,16},{20... | collective-permute-start | bytes 417800 | tf_op jit(solution)/shard_map/ppermute | solution.py:411
  113.8 3.6 %attend.7 = (bf16[272,128]{1,0:T(8,128)(2,1)S(1)}, bf16[272,128]{1,0:T(8,128)(2,1)S(1)}, bf16[272,128]{1,0:T(8,128)(2,1)S(1)}, bf16[272,128]{1,0:T(8,128)(2,1)S(1)}) custom-call(s32[3,16]{1,0:T(4,128)S(1)} %concatenate.7.live, bf16[16,16,256]{2,1,0:T(8,128)(2,1)S(1)} %bitcast.16, bf16[16,16,256]{2,1,0:T(8,128)(2,1)S(1)} %collective-permute-done.4.refs_1_, ...), custom_call_target="tpu_custom_call" | custom-call | flops 3000000000 | bytes 5000000 | tf_op jit(solution)/shard_map/attend/pallas_call | solution.py:240
  120.3 2.4 %collective-permute-done.29.came = bf16[272,256]{1,0:T(8,128)(2,1)S(1)} collective-permute-done((bf16[272,256]{1,0:T(8,128)(2,1)S(1)}, bf16[272,256]{1,0:T(8,128)(2,1)S(1)}, u32[]{:S(2)}, u32[]{:S(2)}) %collective-permute-start.29) | collective-permute-done | bytes 139296 | tf_op jit(solution)/shard_map/ppermute | solution.py:411
  122.7 2.4 %collective-permute-start.30 = (bf16[272,256]{1,0:T(8,128)(2,1)S(1)}, bf16[272,256]{1,0:T(8,128)(2,1)S(1)}, u32[]{:S(2)}, u32[]{:S(2)}) collective-permute-start(bf16[272,256]{1,0:T(8,128)(2,1)S(1)} %merge.22), channel_id=1, source_target_pairs={{2,0},{4,2},{6,4},{8,6},{10,8},{12,10},{14,12},{16,14},{18,16},{20... | collective-permute-start | bytes 417800 | tf_op jit(solution)/shard_map/ppermute | solution.py:411
  125.3 1.7 %collective-permute-start.23 = (bf16[272,256]{1,0:T(8,128)(2,1)S(1)}, bf16[272,256]{1,0:T(8,128)(2,1)S(1)}, u32[]{:S(2)}, u32[]{:S(2)}) collective-permute-start(bf16[272,256]{1,0:T(8,128)(2,1)S(1)} %merge.16), channel_id=1, source_target_pairs={{2,0},{4,2},{6,4},{8,6},{10,8},{12,10},{14,12},{16,14},{18,16},{20... | collective-permute-start | bytes 417800 | tf_op jit(solution)/shard_map/ppermute | solution.py:411
  128.0 3.6 %collective-permute-start.31 = (bf16[272,256]{1,0:T(8,128)(2,1)S(1)}, bf16[272,256]{1,0:T(8,128)(2,1)S(1)}, u32[]{:S(2)}, u32[]{:S(2)}) collective-permute-start(bf16[272,256]{1,0:T(8,128)(2,1)S(1)} %merge.23), channel_id=1, source_target_pairs={{2,0},{4,2},{6,4},{8,6},{10,8},{12,10},{14,12},{16,14},{18,16},{20... | collective-permute-start | bytes 417800 | tf_op jit(solution)/shard_map/ppermute | solution.py:411
  131.7 1.7 %collective-permute-start.24 = (bf16[272,256]{1,0:T(8,128)(2,1)S(1)}, bf16[272,256]{1,0:T(8,128)(2,1)S(1)}, u32[]{:S(2)}, u32[]{:S(2)}) collective-permute-start(bf16[272,256]{1,0:T(8,128)(2,1)S(1)} %merge.17), channel_id=1, source_target_pairs={{2,0},{4,2},{6,4},{8,6},{10,8},{12,10},{14,12},{16,14},{18,16},{20... | collective-permute-start | bytes 417800 | tf_op jit(solution)/shard_map/ppermute | solution.py:411
  134.2 2.7 %collective-permute-done.24.refs_0_ = bf16[272,256]{1,0:T(8,128)(2,1)S(1)} collective-permute-done((bf16[272,256]{1,0:T(8,128)(2,1)S(1)}, bf16[272,256]{1,0:T(8,128)(2,1)S(1)}, u32[]{:S(2)}, u32[]{:S(2)}) %collective-permute-start.24) | collective-permute-done | bytes 139296 | tf_op jit(solution)/shard_map/ppermute | solution.py:411
  (110 shorter events, 22.7 us)
Async XLA Ops:
  6.3 65.5 %collective-permute-start.17 = (bf16[16,512,256]{2,1,0:T(8,128)(2,1)}, bf16[16,512,256]{2,1,0:T(8,128)(2,1)}, u32[]{:S(2)}, u32[]{:S(2)}) collective-permute-start(bf16[16,512,256]{2,1,0:T(8,128)(2,1)} %history.1.rows), channel_id=1, source_target_pairs={{0,1},{1,0},{2,3},{3,2},{4,5},{5,4},{6,7},{7,6},{8,9},{9,8},{10,11... | collective-permute-start | bytes 12582920 | tf_op jit(solution)/shard_map/ppermute | solution.py:411
  6.5 7.3 %collective-permute-start.4 = (bf16[16,16,256]{2,1,0:T(8,128)(2,1)S(1)}, bf16[16,16,256]{2,1,0:T(8,128)(2,1)S(1)}, u32[]{:S(2)}, u32[]{:S(2)}) collective-permute-start(bf16[16,16,256]{2,1,0:T(8,128)(2,1)S(1)} %bitcast.11), channel_id=1, source_target_pairs={{0,1},{1,0},{2,3},{3,2},{4,5},{5,4},{6,7},{7,6},{8,9},{9,8},{10,11... | collective-permute-start | bytes 393224 | tf_op jit(solution)/shard_map/ppermute | solution.py:411
  7.1 15.5 %collective-permute-start = (bf16[16,16,256]{2,1,0:T(8,128)(2,1)S(1)}, bf16[16,16,256]{2,1,0:T(8,128)(2,1)S(1)}, u32[]{:S(2)}, u32[]{:S(2)}) collective-permute-start(bf16[16,16,256]{2,1,0:T(8,128)(2,1)S(1)} %bitcast.12), channel_id=1, source_target_pairs={{0,2},{2,4},{4,6},{6,8},{8,10},{10,12},{12,14},{14,16},{16,18},{18... | collective-permute-start | bytes 393224 | tf_op jit(solution)/shard_map/ppermute | solution.py:411
  13.9 15.5 %collective-permute-start.5 = (bf16[16,16,256]{2,1,0:T(8,128)(2,1)S(1)}, bf16[16,16,256]{2,1,0:T(8,128)(2,1)S(1)}, u32[]{:S(2)}, u32[]{:S(2)}) collective-permute-start(bf16[16,16,256]{2,1,0:T(8,128)(2,1)S(1)} %collective-permute-done.4.refs_1_), channel_id=1, source_target_pairs={{0,2},{2,4},{4,6},{6,8},{8,10},{10,12},{12,14},{14,16},{16,18},{18... | collective-permute-start | bytes 393224 | tf_op jit(solution)/shard_map/ppermute | solution.py:411
  22.6 8.1 %collective-permute-start.1 = (bf16[16,16,256]{2,1,0:T(8,128)(2,1)S(1)}, bf16[16,16,256]{2,1,0:T(8,128)(2,1)S(1)}, u32[]{:S(2)}, u32[]{:S(2)}) collective-permute-start(bf16[16,16,256]{2,1,0:T(8,128)(2,1)S(1)} %collective-permute-done.refs_2_), channel_id=1, source_target_pairs={{0,2},{2,4},{4,6},{6,8},{8,10},{10,12},{12,14},{14,16},{16,18},{18... | collective-permute-start | bytes 393224 | tf_op jit(solution)/shard_map/ppermute | solution.py:411
  29.3 6.2 %collective-permute-start.6 = (bf16[16,16,256]{2,1,0:T(8,128)(2,1)S(1)}, bf16[16,16,256]{2,1,0:T(8,128)(2,1)S(1)}, u32[]{:S(2)}, u32[]{:S(2)}) collective-permute-start(bf16[16,16,256]{2,1,0:T(8,128)(2,1)S(1)} %collective-permute-done.5.refs_3_), channel_id=1, source_target_pairs={{0,2},{2,4},{4,6},{6,8},{8,10},{10,12},{12,14},{14,16},{16,18},{18... | collective-permute-start | bytes 393224 | tf_op jit(solution)/shard_map/ppermute | solution.py:411
  30.7 6.2 %collective-permute-start.2 = (bf16[16,16,256]{2,1,0:T(8,128)(2,1)S(1)}, bf16[16,16,256]{2,1,0:T(8,128)(2,1)S(1)}, u32[]{:S(2)}, u32[]{:S(2)}) collective-permute-start(bf16[16,16,256]{2,1,0:T(8,128)(2,1)S(1)} %collective-permute-done.1.refs_4_), channel_id=1, source_target_pairs={{0,2},{2,4},{4,6},{6,8},{8,10},{10,12},{12,14},{14,16},{16,18},{18... | collective-permute-start | bytes 393224 | tf_op jit(solution)/shard_map/ppermute | solution.py:411
  35.5 6.2 %collective-permute-start.7 = (bf16[16,16,256]{2,1,0:T(8,128)(2,1)S(1)}, bf16[16,16,256]{2,1,0:T(8,128)(2,1)S(1)}, u32[]{:S(2)}, u32[]{:S(2)}) collective-permute-start(bf16[16,16,256]{2,1,0:T(8,128)(2,1)S(1)} %collective-permute-done.6.refs_5_), channel_id=1, source_target_pairs={{0,2},{2,4},{4,6},{6,8},{8,10},{10,12},{12,14},{14,16},{16,18},{18... | collective-permute-start | bytes 393224 | tf_op jit(solution)/shard_map/ppermute | solution.py:411
  36.9 6.2 %collective-permute-start.3 = (bf16[16,16,256]{2,1,0:T(8,128)(2,1)S(1)}, bf16[16,16,256]{2,1,0:T(8,128)(2,1)S(1)}, u32[]{:S(2)}, u32[]{:S(2)}) collective-permute-start(bf16[16,16,256]{2,1,0:T(8,128)(2,1)S(1)} %collective-permute-done.2.refs_6_), channel_id=1, source_target_pairs={{0,2},{2,4},{4,6},{6,8},{8,10},{10,12},{12,14},{14,16},{16,18},{18... | collective-permute-start | bytes 393224 | tf_op jit(solution)/shard_map/ppermute | solution.py:411
  41.7 6.2 %collective-permute-start.8 = (bf16[16,16,256]{2,1,0:T(8,128)(2,1)S(1)}, bf16[16,16,256]{2,1,0:T(8,128)(2,1)S(1)}, u32[]{:S(2)}, u32[]{:S(2)}) collective-permute-start(bf16[16,16,256]{2,1,0:T(8,128)(2,1)S(1)} %collective-permute-done.7.refs_7_), channel_id=1, source_target_pairs={{0,2},{2,4},{4,6},{6,8},{8,10},{10,12},{12,14},{14,16},{16,18},{18... | collective-permute-start | bytes 393224 | tf_op jit(solution)/shard_map/ppermute | solution.py:411
  43.1 6.2 %collective-permute-start.9 = (bf16[16,16,256]{2,1,0:T(8,128)(2,1)S(1)}, bf16[16,16,256]{2,1,0:T(8,128)(2,1)S(1)}, u32[]{:S(2)}, u32[]{:S(2)}) collective-permute-start(bf16[16,16,256]{2,1,0:T(8,128)(2,1)S(1)} %collective-permute-done.3.refs_0_.refs_8_), channel_id=1, source_target_pairs={{0,2},{2,4},{4,6},{6,8},{8,10},{10,12},{12,14},{14,16},{16,18},{18... | collective-permute-start | bytes 393224 | tf_op jit(solution)/shard_map/ppermute | solution.py:411
  47.9 6.2 %collective-permute-start.10 = (bf16[16,16,256]{2,1,0:T(8,128)(2,1)S(1)}, bf16[16,16,256]{2,1,0:T(8,128)(2,1)S(1)}, u32[]{:S(2)}, u32[]{:S(2)}) collective-permute-start(bf16[16,16,256]{2,1,0:T(8,128)(2,1)S(1)} %collective-permute-done.8.refs_1_.refs_9_), channel_id=1, source_target_pairs={{0,2},{2,4},{4,6},{6,8},{8,10},{10,12},{12,14},{14,16},{16,18},{18... | collective-permute-start | bytes 393224 | tf_op jit(solution)/shard_map/ppermute | solution.py:411
  49.3 14.2 %collective-permute-start.11 = (bf16[16,16,256]{2,1,0:T(8,128)(2,1)S(1)}, bf16[16,16,256]{2,1,0:T(8,128)(2,1)S(1)}, u32[]{:S(2)}, u32[]{:S(2)}) collective-permute-start(bf16[16,16,256]{2,1,0:T(8,128)(2,1)S(1)} %collective-permute-done.9.refs_2_), channel_id=1, source_target_pairs={{0,2},{2,4},{4,6},{6,8},{8,10},{10,12},{12,14},{14,16},{16,18},{18... | collective-permute-start | bytes 393224 | tf_op jit(solution)/shard_map/ppermute | solution.py:411
  54.0 9.5 %collective-permute-start.12 = (bf16[16,16,256]{2,1,0:T(8,128)(2,1)S(1)}, bf16[16,16,256]{2,1,0:T(8,128)(2,1)S(1)}, u32[]{:S(2)}, u32[]{:S(2)}) collective-permute-start(bf16[16,16,256]{2,1,0:T(8,128)(2,1)S(1)} %collective-permute-done.10.refs_3_), channel_id=1, source_target_pairs={{0,2},{2,4},{4,6},{6,8},{8,10},{10,12},{12,14},{14,16},{16,18},{18... | collective-permute-start | bytes 393224 | tf_op jit(solution)/shard_map/ppermute | solution.py:411
  63.5 6.2 %collective-permute-start.13 = (bf16[16,16,256]{2,1,0:T(8,128)(2,1)S(1)}, bf16[16,16,256]{2,1,0:T(8,128)(2,1)S(1)}, u32[]{:S(2)}, u32[]{:S(2)}) collective-permute-start(bf16[16,16,256]{2,1,0:T(8,128)(2,1)S(1)} %collective-permute-done.11.refs_4_), channel_id=1, source_target_pairs={{0,2},{2,4},{4,6},{6,8},{8,10},{10,12},{12,14},{14,16},{16,18},{18... | collective-permute-start | bytes 393224 | tf_op jit(solution)/shard_map/ppermute | solution.py:411
  63.6 7.6 %collective-permute-start.14 = (bf16[16,16,256]{2,1,0:T(8,128)(2,1)S(1)}, bf16[16,16,256]{2,1,0:T(8,128)(2,1)S(1)}, u32[]{:S(2)}, u32[]{:S(2)}) collective-permute-start(bf16[16,16,256]{2,1,0:T(8,128)(2,1)S(1)} %collective-permute-done.12.refs_5_), channel_id=1, source_target_pairs={{0,2},{2,4},{4,6},{6,8},{8,10},{10,12},{12,14},{14,16},{16,18},{18... | collective-permute-start | bytes 393224 | tf_op jit(solution)/shard_map/ppermute | solution.py:411
  69.7 6.8 %collective-permute-start.15 = (bf16[16,16,256]{2,1,0:T(8,128)(2,1)S(1)}, bf16[16,16,256]{2,1,0:T(8,128)(2,1)S(1)}, u32[]{:S(2)}, u32[]{:S(2)}) collective-permute-start(bf16[16,16,256]{2,1,0:T(8,128)(2,1)S(1)} %collective-permute-done.13.refs_6_), channel_id=1, source_target_pairs={{1,31},{3,1},{5,3},{7,5},{9,7},{11,9},{13,11},{15,13},{17,15},{19,... | collective-permute-start | bytes 393224 | tf_op jit(solution)/shard_map/ppermute | solution.py:411
  71.1 5.4 %collective-permute-start.16 = (bf16[16,16,256]{2,1,0:T(8,128)(2,1)S(1)}, bf16[16,16,256]{2,1,0:T(8,128)(2,1)S(1)}, u32[]{:S(2)}, u32[]{:S(2)}) collective-permute-start(bf16[16,16,256]{2,1,0:T(8,128)(2,1)S(1)} %collective-permute-done.14.refs_7_), channel_id=1, source_target_pairs={{1,31},{3,1},{5,3},{7,5},{9,7},{11,9},{13,11},{15,13},{17,15},{19,... | collective-permute-start | bytes 393224 | tf_op jit(solution)/shard_map/ppermute | solution.py:411
  83.3 13.3 %collective-permute-start.25 = (bf16[272,256]{1,0:T(8,128)(2,1)S(1)}, bf16[272,256]{1,0:T(8,128)(2,1)S(1)}, u32[]{:S(2)}, u32[]{:S(2)}) collective-permute-start(bf16[272,256]{1,0:T(8,128)(2,1)S(1)} %get-tuple-element.48), channel_id=1, source_target_pairs={{2,0},{4,2},{6,4},{8,6},{10,8},{12,10},{14,12},{16,14},{18,16},{20... | collective-permute-start | bytes 417800 | tf_op jit(solution)/shard_map/ppermute | solution.py:411
  92.3 5.2 %collective-permute-start.18 = (bf16[272,256]{1,0:T(8,128)(2,1)S(1)}, bf16[272,256]{1,0:T(8,128)(2,1)S(1)}, u32[]{:S(2)}, u32[]{:S(2)}) collective-permute-start(bf16[272,256]{1,0:T(8,128)(2,1)S(1)} %get-tuple-element.38), channel_id=1, source_target_pairs={{2,0},{4,2},{6,4},{8,6},{10,8},{12,10},{14,12},{16,14},{18,16},{20... | collective-permute-start | bytes 417800 | tf_op jit(solution)/shard_map/ppermute | solution.py:411
  96.7 6.9 %collective-permute-start.26 = (bf16[272,256]{1,0:T(8,128)(2,1)S(1)}, bf16[272,256]{1,0:T(8,128)(2,1)S(1)}, u32[]{:S(2)}, u32[]{:S(2)}) collective-permute-start(bf16[272,256]{1,0:T(8,128)(2,1)S(1)} %merge.18), channel_id=1, source_target_pairs={{2,0},{4,2},{6,4},{8,6},{10,8},{12,10},{14,12},{16,14},{18,16},{20... | collective-permute-start | bytes 417800 | tf_op jit(solution)/shard_map/ppermute | solution.py:411
  97.6 8.3 %collective-permute-start.19 = (bf16[272,256]{1,0:T(8,128)(2,1)S(1)}, bf16[272,256]{1,0:T(8,128)(2,1)S(1)}, u32[]{:S(2)}, u32[]{:S(2)}) collective-permute-start(bf16[272,256]{1,0:T(8,128)(2,1)S(1)} %merge.12), channel_id=1, source_target_pairs={{2,0},{4,2},{6,4},{8,6},{10,8},{12,10},{14,12},{16,14},{18,16},{20... | collective-permute-start | bytes 417800 | tf_op jit(solution)/shard_map/ppermute | solution.py:411
  103.7 6.5 %collective-permute-start.27 = (bf16[272,256]{1,0:T(8,128)(2,1)S(1)}, bf16[272,256]{1,0:T(8,128)(2,1)S(1)}, u32[]{:S(2)}, u32[]{:S(2)}) collective-permute-start(bf16[272,256]{1,0:T(8,128)(2,1)S(1)} %merge.19), channel_id=1, source_target_pairs={{2,0},{4,2},{6,4},{8,6},{10,8},{12,10},{14,12},{16,14},{18,16},{20... | collective-permute-start | bytes 417800 | tf_op jit(solution)/shard_map/ppermute | solution.py:411
  105.9 6.4 %collective-permute-start.20 = (bf16[272,256]{1,0:T(8,128)(2,1)S(1)}, bf16[272,256]{1,0:T(8,128)(2,1)S(1)}, u32[]{:S(2)}, u32[]{:S(2)}) collective-permute-start(bf16[272,256]{1,0:T(8,128)(2,1)S(1)} %merge.13), channel_id=1, source_target_pairs={{2,0},{4,2},{6,4},{8,6},{10,8},{12,10},{14,12},{16,14},{18,16},{20... | collective-permute-start | bytes 417800 | tf_op jit(solution)/shard_map/ppermute | solution.py:411
  110.3 7.1 %collective-permute-start.28 = (bf16[272,256]{1,0:T(8,128)(2,1)S(1)}, bf16[272,256]{1,0:T(8,128)(2,1)S(1)}, u32[]{:S(2)}, u32[]{:S(2)}) collective-permute-start(bf16[272,256]{1,0:T(8,128)(2,1)S(1)} %merge.20), channel_id=1, source_target_pairs={{2,0},{4,2},{6,4},{8,6},{10,8},{12,10},{14,12},{16,14},{18,16},{20... | collective-permute-start | bytes 417800 | tf_op jit(solution)/shard_map/ppermute | solution.py:411
  112.4 6.3 %collective-permute-start.21 = (bf16[272,256]{1,0:T(8,128)(2,1)S(1)}, bf16[272,256]{1,0:T(8,128)(2,1)S(1)}, u32[]{:S(2)}, u32[]{:S(2)}) collective-permute-start(bf16[272,256]{1,0:T(8,128)(2,1)S(1)} %merge.14), channel_id=1, source_target_pairs={{2,0},{4,2},{6,4},{8,6},{10,8},{12,10},{14,12},{16,14},{18,16},{20... | collective-permute-start | bytes 417800 | tf_op jit(solution)/shard_map/ppermute | solution.py:411
  117.5 5.2 %collective-permute-start.29 = (bf16[272,256]{1,0:T(8,128)(2,1)S(1)}, bf16[272,256]{1,0:T(8,128)(2,1)S(1)}, u32[]{:S(2)}, u32[]{:S(2)}) collective-permute-start(bf16[272,256]{1,0:T(8,128)(2,1)S(1)} %merge.21), channel_id=1, source_target_pairs={{2,0},{4,2},{6,4},{8,6},{10,8},{12,10},{14,12},{16,14},{18,16},{20... | collective-permute-start | bytes 417800 | tf_op jit(solution)/shard_map/ppermute | solution.py:411
  118.8 6.4 %collective-permute-start.22 = (bf16[272,256]{1,0:T(8,128)(2,1)S(1)}, bf16[272,256]{1,0:T(8,128)(2,1)S(1)}, u32[]{:S(2)}, u32[]{:S(2)}) collective-permute-start(bf16[272,256]{1,0:T(8,128)(2,1)S(1)} %merge.15), channel_id=1, source_target_pairs={{2,0},{4,2},{6,4},{8,6},{10,8},{12,10},{14,12},{16,14},{18,16},{20... | collective-permute-start | bytes 417800 | tf_op jit(solution)/shard_map/ppermute | solution.py:411
  122.7 5.2 %collective-permute-start.30 = (bf16[272,256]{1,0:T(8,128)(2,1)S(1)}, bf16[272,256]{1,0:T(8,128)(2,1)S(1)}, u32[]{:S(2)}, u32[]{:S(2)}) collective-permute-start(bf16[272,256]{1,0:T(8,128)(2,1)S(1)} %merge.22), channel_id=1, source_target_pairs={{2,0},{4,2},{6,4},{8,6},{10,8},{12,10},{14,12},{16,14},{18,16},{20... | collective-permute-start | bytes 417800 | tf_op jit(solution)/shard_map/ppermute | solution.py:411
  125.3 6.4 %collective-permute-start.23 = (bf16[272,256]{1,0:T(8,128)(2,1)S(1)}, bf16[272,256]{1,0:T(8,128)(2,1)S(1)}, u32[]{:S(2)}, u32[]{:S(2)}) collective-permute-start(bf16[272,256]{1,0:T(8,128)(2,1)S(1)} %merge.16), channel_id=1, source_target_pairs={{2,0},{4,2},{6,4},{8,6},{10,8},{12,10},{14,12},{16,14},{18,16},{20... | collective-permute-start | bytes 417800 | tf_op jit(solution)/shard_map/ppermute | solution.py:411
  128.0 6.2 %collective-permute-start.31 = (bf16[272,256]{1,0:T(8,128)(2,1)S(1)}, bf16[272,256]{1,0:T(8,128)(2,1)S(1)}, u32[]{:S(2)}, u32[]{:S(2)}) collective-permute-start(bf16[272,256]{1,0:T(8,128)(2,1)S(1)} %merge.23), channel_id=1, source_target_pairs={{2,0},{4,2},{6,4},{8,6},{10,8},{12,10},{14,12},{16,14},{18,16},{20... | collective-permute-start | bytes 417800 | tf_op jit(solution)/shard_map/ppermute | solution.py:411
  131.7 5.2 %collective-permute-start.24 = (bf16[272,256]{1,0:T(8,128)(2,1)S(1)}, bf16[272,256]{1,0:T(8,128)(2,1)S(1)}, u32[]{:S(2)}, u32[]{:S(2)}) collective-permute-start(bf16[272,256]{1,0:T(8,128)(2,1)S(1)} %merge.17), channel_id=1, source_target_pairs={{2,0},{4,2},{6,4},{8,6},{10,8},{12,10},{14,12},{16,14},{18,16},{20... | collective-permute-start | bytes 417800 | tf_op jit(solution)/shard_map/ppermute | solution.py:411
  (19 other events, 304.9 us)
